TPU v7x, 32 devices: a whole 2x2x4 slice. The times are simulated.
32 devices in a mesh: dp: 8 (over z, y), tensor: 4 (over x, core).
Axes of the slice: x: 2, y: 2, z: 4, core: 2. Of those that a mesh axis runs over, the one named last changes fastest.
Arguments:
- layer_input: bfloat16 [8192, 1536], P(('dp', 'tensor')), may hold values from -45 to 45
- text_states: bfloat16 [8, 64, 1536], P('dp'), may hold values from -6 to 6
- ln1_gain: float32 [1536], replicated, may hold values from 0.5 to 1.5
- ln1_bias: float32 [1536], replicated, may hold values from -1.5 to 1.5
- w_q: bfloat16 [1536, 1536], P(None, 'tensor'), may hold values from -0.15625 to 0.15625
- w_k: bfloat16 [1536, 1536], P(None, 'tensor'), may hold values from -0.15625 to 0.15625
- w_v: bfloat16 [1536, 1536], P(None, 'tensor'), may hold values from -0.15625 to 0.15625
- w_o: bfloat16 [1536, 1536], P('tensor'), may hold values from -0.625 to 0.625
- ln2_gain: float32 [1536], replicated, may hold values from 0.5 to 1.5
- ln2_bias: float32 [1536], replicated, may hold values from -1.5 to 1.5
- c_q: bfloat16 [1536, 1536], P(None, 'tensor'), may hold values from -0.15625 to 0.15625
- c_k: bfloat16 [1536, 1536], P(None, 'tensor'), may hold values from -0.15625 to 0.15625
- c_v: bfloat16 [1536, 1536], P(None, 'tensor'), may hold values from -0.15625 to 0.15625
- c_o: bfloat16 [1536, 1536], P('tensor'), may hold values from -0.625 to 0.625
- ln3_gain: float32 [1536], replicated, may hold values from 0.5 to 1.5
- ln3_bias: float32 [1536], replicated, may hold values from -1.5 to 1.5
- w_in: bfloat16 [1536, 6144], P(None, 'tensor'), may hold values from -0.15625 to 0.15625
- w_out: bfloat16 [6144, 1536], P('tensor'), may hold values from -0.078125 to 0.078125
- out_cotangent: bfloat16 [8192, 1536], P(('dp', 'tensor')), may hold values from -6 to 6
Outputs:
- block_out: bfloat16 [8192, 1536], P(('dp', 'tensor'))
- input_grad: bfloat16 [8192, 1536], P(('dp', 'tensor'))
- text_states_grad: bfloat16 [8, 64, 1536], P('dp', None, 'tensor')
- ln1_gain_grad: float32 [1536], replicated
- ln1_bias_grad: float32 [1536], replicated
- w_q_grad: float32 [1536, 1536], P('dp', 'tensor')
- w_k_grad: float32 [1536, 1536], P('dp', 'tensor')
- w_v_grad: float32 [1536, 1536], P('dp', 'tensor')
- w_o_grad: float32 [1536, 1536], P('tensor', 'dp')
- ln2_gain_grad: float32 [1536], replicated
- ln2_bias_grad: float32 [1536], replicated
- c_q_grad: float32 [1536, 1536], P('dp', 'tensor')
- c_k_grad: float32 [1536, 1536], P('dp', 'tensor')
- c_v_grad: float32 [1536, 1536], P('dp', 'tensor')
- c_o_grad: float32 [1536, 1536], P('tensor', 'dp')
- ln3_gain_grad: float32 [1536], replicated
- ln3_bias_grad: float32 [1536], replicated
- w_in_grad: float32 [1536, 6144], P('dp', 'tensor')
- w_out_grad: float32 [6144, 1536], P('tensor', 'dp')
- root_squares: float32 [4], replicated
All inputs are finite; a program needn't handle non-finite values.
Results may differ from a plain program's by a relative error of at most 0.022.
Values may be sent and summed in bfloat16 or wider, within the bound.
A program may use at most 192 MiB of HBM per device.

v0:
```python
from functools import partial

import jax
import jax.numpy as jnp
from jax import lax
from jax.sharding import PartitionSpec as P

HD = 64
FRAMES = 1024


norm_eps = 1e-05


def layer_norm(stream, gain_vec, shift_vec):
    centre = jnp.mean(stream, axis=-1, keepdims=True)
    centred = stream - centre
    spread = jnp.mean(centred * centred, axis=-1, keepdims=True)
    return centred * lax.rsqrt(spread + norm_eps) * gain_vec + shift_vec


def product(left_mat, right_mat):
    return jnp.dot(left_mat, right_mat, preferred_element_type=jnp.float32)


def contract_rows(left_mat, right_mat):
    return lax.dot_general(
        left_mat, right_mat, (((0,), (0,)), ((), ())), preferred_element_type=jnp.float32
    )


def contract_cols(left_mat, right_mat):
    return lax.dot_general(
        left_mat, right_mat, (((1,), (1,)), ((), ())), preferred_element_type=jnp.float32
    )


def gather_normed(values):
    return lax.all_gather(values, "tensor", axis=0, tiled=True)


def gather_grads(values):
    return lax.all_gather(values, "tensor", axis=0, tiled=True)


def sum_branch(values, weight_mat):
    return lax.psum_scatter(
        product(values, weight_mat).astype(jnp.bfloat16), "tensor", scatter_dimension=0, tiled=True
    ).astype(jnp.float32)


def sum_inputs(grad_list, weight_list):
    own_rows = grad_list[0].shape[0] // lax.axis_size("tensor")
    total_sum = jnp.zeros(
        (lax.axis_size("tensor") * own_rows, weight_list[0].shape[0]), jnp.float32
    )
    for grad_mat, weight_mat in zip(grad_list, weight_list):
        total_sum = total_sum + contract_cols(grad_mat, weight_mat)
    return lax.psum_scatter(
        total_sum.astype(jnp.bfloat16), "tensor", scatter_dimension=0, tiled=True
    ).astype(jnp.float32)


def block_scores(queries, all_keys, begin_row, end_row):
    scores = jnp.einsum(
        "cqhd,ckhd->chqk",
        queries[:, begin_row:end_row],
        all_keys[:, :end_row],
        preferred_element_type=jnp.float32,
    ) * HD ** (-0.5)
    row_ids = begin_row + lax.broadcasted_iota(jnp.int32, (end_row - begin_row, end_row), 0)
    col_ids = lax.broadcasted_iota(jnp.int32, (end_row - begin_row, end_row), 1)
    return jnp.where(col_ids <= row_ids, scores, -1e30)


def self_forward(queries, all_keys, all_values):
    block_rows = min(512, FRAMES)
    outputs, peak_list, sum_list = ([], [], [])
    for begin_row in range(0, FRAMES, block_rows):
        end_row = begin_row + block_rows
        scores = block_scores(queries, all_keys, begin_row, end_row)
        row_peak = jnp.max(scores, axis=-1, keepdims=True)
        exp_scores = jnp.exp(scores - row_peak)
        row_sum = jnp.sum(exp_scores, axis=-1, keepdims=True)
        weights = (exp_scores / row_sum).astype(jnp.bfloat16)
        outputs.append(
            jnp.einsum(
                "chqk,ckhd->cqhd",
                weights,
                all_values[:, :end_row],
                preferred_element_type=jnp.float32,
            )
        )
        peak_list.append(row_peak)
        sum_list.append(row_sum)
    return (jnp.concatenate(outputs, axis=1), peak_list, sum_list)


def self_backward(queries, all_keys, all_values, peak_list, sum_list, grad_mixed):
    block_rows = min(512, FRAMES)
    score_scale = HD ** (-0.5)
    query_parts = []
    grad_keys = jnp.zeros(all_keys.shape, jnp.float32)
    grad_values = jnp.zeros(all_values.shape, jnp.float32)
    for block_id, begin_row in enumerate(range(0, FRAMES, block_rows)):
        end_row = begin_row + block_rows
        scores = block_scores(queries, all_keys, begin_row, end_row)
        weights = jnp.exp(scores - peak_list[block_id]) / sum_list[block_id]
        grad_weights = jnp.einsum(
            "cqhd,ckhd->chqk",
            grad_mixed[:, begin_row:end_row],
            all_values[:, :end_row],
            preferred_element_type=jnp.float32,
        )
        row_dot = jnp.sum(weights * grad_weights, axis=-1, keepdims=True)
        grad_scores = (weights * (grad_weights - row_dot)).astype(jnp.bfloat16)
        query_parts.append(
            jnp.einsum(
                "chqk,ckhd->cqhd",
                grad_scores,
                all_keys[:, :end_row],
                preferred_element_type=jnp.float32,
            )
            * score_scale
        )
        grad_keys = grad_keys.at[:, :end_row].add(
            jnp.einsum(
                "chqk,cqhd->ckhd",
                grad_scores,
                queries[:, begin_row:end_row],
                preferred_element_type=jnp.float32,
            )
            * score_scale
        )
        grad_values = grad_values.at[:, :end_row].add(
            jnp.einsum(
                "chqk,cqhd->ckhd",
                weights.astype(jnp.bfloat16),
                grad_mixed[:, begin_row:end_row],
                preferred_element_type=jnp.float32,
            )
        )
    return (jnp.concatenate(query_parts, axis=1), grad_keys, grad_values)


def cross_forward(queries, all_keys, all_values):
    scores = jnp.einsum(
        "cqhd,ckhd->chqk", queries, all_keys, preferred_element_type=jnp.float32
    ) * HD ** (-0.5)
    row_peak = jnp.max(scores, axis=-1, keepdims=True)
    exp_scores = jnp.exp(scores - row_peak)
    weights = exp_scores / jnp.sum(exp_scores, axis=-1, keepdims=True)
    mixed_out = jnp.einsum(
        "chqk,ckhd->cqhd",
        weights.astype(jnp.bfloat16),
        all_values,
        preferred_element_type=jnp.float32,
    )
    return (mixed_out, weights)


def cross_backward(queries, all_keys, all_values, weights, grad_mixed):
    score_scale = HD ** (-0.5)
    grad_weights = jnp.einsum(
        "cqhd,ckhd->chqk", grad_mixed, all_values, preferred_element_type=jnp.float32
    )
    row_dot = jnp.sum(weights * grad_weights, axis=-1, keepdims=True)
    grad_scores = (weights * (grad_weights - row_dot)).astype(jnp.bfloat16)
    grad_queries = (
        jnp.einsum("chqk,ckhd->cqhd", grad_scores, all_keys, preferred_element_type=jnp.float32)
        * score_scale
    )
    grad_keys = (
        jnp.einsum("chqk,cqhd->ckhd", grad_scores, queries, preferred_element_type=jnp.float32)
        * score_scale
    )
    grad_values = jnp.einsum(
        "chqk,cqhd->ckhd",
        weights.astype(jnp.bfloat16),
        grad_mixed,
        preferred_element_type=jnp.float32,
    )
    return (grad_queries, grad_keys, grad_values)


def body(
    layer_input,
    text_states,
    ln1_gain,
    ln1_bias,
    w_q,
    w_k,
    w_v,
    w_o,
    ln2_gain,
    ln2_bias,
    c_q,
    c_k,
    c_v,
    c_o,
    ln3_gain,
    ln3_bias,
    w_in,
    w_out,
    out_cotangent,
):
    clip_count = text_states.shape[0]
    text_len = text_states.shape[1]
    model_width = layer_input.shape[1]
    local_heads = w_q.shape[1] // HD

    def split_heads(matrix, length):
        return matrix.astype(jnp.bfloat16).reshape(clip_count, length, local_heads, HD)

    def merge_heads(tensor_four):
        return tensor_four.reshape(clip_count * tensor_four.shape[1], local_heads * HD).astype(
            jnp.bfloat16
        )

    stream = layer_input.astype(jnp.float32)
    normed_one = layer_norm(stream, ln1_gain, ln1_bias).astype(jnp.bfloat16)
    rows_one = gather_normed(normed_one)
    queries = split_heads(product(rows_one, w_q), FRAMES)
    all_keys = split_heads(product(rows_one, w_k), FRAMES)
    all_values = split_heads(product(rows_one, w_v), FRAMES)
    mixed_one, peak_list, sum_list = self_forward(queries, all_keys, all_values)
    attended = merge_heads(mixed_one)
    branch_one = sum_branch(attended, w_o)
    hidden_one = stream + branch_one
    normed_two = layer_norm(hidden_one, ln2_gain, ln2_bias).astype(jnp.bfloat16)
    rows_two = gather_normed(normed_two)
    cross_queries = split_heads(product(rows_two, c_q), FRAMES)
    text_rows = text_states.reshape(clip_count * text_len, model_width)
    text_keys = split_heads(product(text_rows, c_k), text_len)
    text_values = split_heads(product(text_rows, c_v), text_len)
    mixed_two, cross_weights = cross_forward(cross_queries, text_keys, text_values)
    crossed = merge_heads(mixed_two)
    branch_two = sum_branch(crossed, c_o)
    hidden_two = hidden_one + branch_two
    normed_three = layer_norm(hidden_two, ln3_gain, ln3_bias).astype(jnp.bfloat16)
    rows_three = gather_normed(normed_three)
    pre_act = product(rows_three, w_in)
    activated = jax.nn.gelu(pre_act, approximate=False).astype(jnp.bfloat16)
    branch_three = sum_branch(activated, w_out)
    block_out = (hidden_two + branch_three).astype(jnp.bfloat16)
    squares = jnp.stack(
        [
            jnp.sum(stream * stream),
            jnp.sum(branch_one * branch_one),
            jnp.sum(branch_two * branch_two),
            jnp.sum(branch_three * branch_three),
        ]
    )
    square_totals = lax.psum(squares, ("dp", "tensor"))
    grad_out = out_cotangent.astype(jnp.float32)
    grad_three_rows = gather_grads(out_cotangent)
    w_out_part = contract_rows(activated, grad_three_rows)
    grad_act = contract_cols(grad_three_rows, w_out)
    gelu_value, gelu_back = jax.vjp(partial(jax.nn.gelu, approximate=False), pre_act)
    grad_pre = gelu_back(grad_act)[0].astype(jnp.bfloat16)
    w_in_part = contract_rows(rows_three, grad_pre)
    grad_normed_three = sum_inputs((grad_pre,), (w_in,))
    norm_value, norm_back = jax.vjp(layer_norm, hidden_two, ln3_gain, ln3_bias)
    back_rows, ln3_gain_part, ln3_bias_part = norm_back(grad_normed_three)
    grad_two = grad_out + back_rows
    grad_two_rows = gather_grads(grad_two.astype(jnp.bfloat16))
    c_o_part = contract_rows(crossed, grad_two_rows)
    grad_mixed_two = split_heads(contract_cols(grad_two_rows, c_o), FRAMES)
    grad_cq, grad_tk, grad_tv = cross_backward(
        cross_queries, text_keys, text_values, cross_weights, grad_mixed_two
    )
    grad_cq = merge_heads(grad_cq)
    grad_tk = merge_heads(grad_tk)
    grad_tv = merge_heads(grad_tv)
    c_q_part = contract_rows(rows_two, grad_cq)
    c_k_part = contract_rows(text_rows, grad_tk)
    c_v_part = contract_rows(text_rows, grad_tv)
    text_term = (contract_cols(grad_tk, c_k) + contract_cols(grad_tv, c_v)).reshape(
        clip_count, text_len, model_width
    )
    text_states_grad = lax.psum_scatter(
        text_term.astype(jnp.bfloat16), "tensor", scatter_dimension=2, tiled=True
    )
    grad_normed_two = sum_inputs((grad_cq,), (c_q,))
    norm_value, norm_back = jax.vjp(layer_norm, hidden_one, ln2_gain, ln2_bias)
    back_rows, ln2_gain_part, ln2_bias_part = norm_back(grad_normed_two)
    grad_one = grad_two + back_rows
    grad_one_rows = gather_grads(grad_one.astype(jnp.bfloat16))
    w_o_part = contract_rows(attended, grad_one_rows)
    grad_mixed_one = split_heads(contract_cols(grad_one_rows, w_o), FRAMES)
    grad_sq, grad_sk, grad_sv = self_backward(
        queries, all_keys, all_values, peak_list, sum_list, grad_mixed_one
    )
    grad_sq = merge_heads(grad_sq)
    grad_sk = merge_heads(grad_sk)
    grad_sv = merge_heads(grad_sv)
    w_q_part = contract_rows(rows_one, grad_sq)
    w_k_part = contract_rows(rows_one, grad_sk)
    w_v_part = contract_rows(rows_one, grad_sv)
    grad_normed_one = sum_inputs((grad_sq, grad_sk, grad_sv), (w_q, w_k, w_v))
    norm_value, norm_back = jax.vjp(layer_norm, stream, ln1_gain, ln1_bias)
    back_rows, ln1_gain_part, ln1_bias_part = norm_back(grad_normed_one)
    input_grad = (grad_one + back_rows).astype(jnp.bfloat16)
    (
        w_q_grad,
        w_k_grad,
        w_v_grad,
        w_o_grad,
        c_q_grad,
        c_k_grad,
        c_v_grad,
        c_o_grad,
        w_in_grad,
        w_out_grad,
    ) = (
        lax.psum_scatter(w_q_part, "dp", scatter_dimension=0, tiled=True),
        lax.psum_scatter(w_k_part, "dp", scatter_dimension=0, tiled=True),
        lax.psum_scatter(w_v_part, "dp", scatter_dimension=0, tiled=True),
        lax.psum_scatter(w_o_part, "dp", scatter_dimension=1, tiled=True),
        lax.psum_scatter(c_q_part, "dp", scatter_dimension=0, tiled=True),
        lax.psum_scatter(c_k_part, "dp", scatter_dimension=0, tiled=True),
        lax.psum_scatter(c_v_part, "dp", scatter_dimension=0, tiled=True),
        lax.psum_scatter(c_o_part, "dp", scatter_dimension=1, tiled=True),
        lax.psum_scatter(w_in_part, "dp", scatter_dimension=0, tiled=True),
        lax.psum_scatter(w_out_part, "dp", scatter_dimension=1, tiled=True),
    )
    ln1_gain_grad, ln1_bias_grad, ln2_gain_grad, ln2_bias_grad, ln3_gain_grad, ln3_bias_grad = (
        lax.psum(
            (
                ln1_gain_part,
                ln1_bias_part,
                ln2_gain_part,
                ln2_bias_part,
                ln3_gain_part,
                ln3_bias_part,
            ),
            ("dp", "tensor"),
        )
    )
    entry_count = layer_input.shape[0] * lax.axis_size("dp") * lax.axis_size("tensor") * model_width
    root_squares = jnp.sqrt(square_totals / entry_count)
    return (
        block_out,
        input_grad,
        text_states_grad,
        ln1_gain_grad,
        ln1_bias_grad,
        w_q_grad,
        w_k_grad,
        w_v_grad,
        w_o_grad,
        ln2_gain_grad,
        ln2_bias_grad,
        c_q_grad,
        c_k_grad,
        c_v_grad,
        c_o_grad,
        ln3_gain_grad,
        ln3_bias_grad,
        w_in_grad,
        w_out_grad,
        root_squares,
    )


def solution(mesh):
    return jax.shard_map(
        body,
        mesh=mesh,
        in_specs=(
            P(("dp", "tensor"), None),
            P("dp", None, None),
            P(),
            P(),
            P(None, "tensor"),
            P(None, "tensor"),
            P(None, "tensor"),
            P("tensor", None),
            P(),
            P(),
            P(None, "tensor"),
            P(None, "tensor"),
            P(None, "tensor"),
            P("tensor", None),
            P(),
            P(),
            P(None, "tensor"),
            P("tensor", None),
            P(("dp", "tensor"), None),
        ),
        out_specs=(
            P(("dp", "tensor"), None),
            P(("dp", "tensor"), None),
            P("dp", None, "tensor"),
            P(),
            P(),
            P("dp", "tensor"),
            P("dp", "tensor"),
            P("dp", "tensor"),
            P("tensor", "dp"),
            P(),
            P(),
            P("dp", "tensor"),
            P("dp", "tensor"),
            P("dp", "tensor"),
            P("tensor", "dp"),
            P(),
            P(),
            P("dp", "tensor"),
            P("tensor", "dp"),
            P(),
        ),
        check_vma=False,
    )
```

profile of v0, /device:TPU:8, one launch (start us, length us, event | category | flops | bytes accessed | tf_op | source)
XLA Modules:
  0.0 1511.7 jit_solution(7373976846131511236)
XLA Ops:
  10.3 2.4 fusion.35
  14.0 28.5 %all-gather.7.cloned.1.call-done = bf16[1024,1536]{1,0:T(8,128)(2,1)} async-done(((bf16[256,1536]{1,0:T(8,128)(2,1)}), bf16[1024,1536]{1,0:T(8,128)(2,1)}) %all-gather.7.cloned.1.call-update) | async-done | bytes 3145744 | tf_op jit(solution)/shard_map/all_gather | solution.py:39
  42.5 3.5 convolution_convert_fusion.8
  47.5 6.3 fusion.87
  53.8 5.1 fusion.112
  59.0 16.8 %fusion.111 = (f32[6,512]{1,0:T(8,128)S(1)}, f32[6,512,1024]{2,1,0:T(8,128)}) fusion(f32[6,512,1024]{2,1,0:T(8,128)} %fusion.87, pred[512,1024]{1,0:T(8,128)(4,1)S(1)} %copy-done.36), kind=kOutput, calls=%fused_computation.203 | output fusion | flops 18875392 | bytes 25702400 | tf_op jit(solution)/shard_map/sub | solution.py:83
  75.8 3.5 convolution_convert_fusion.10
  82.0 2.3 fusion.71
  85.3 3.5 convolution_convert_fusion.4
  88.9 38.0 %reduce-scatter.24.cloned.1.call-done = bf16[256,1536]{1,0:T(8,128)(2,1)} async-done(((bf16[1024,1536]{1,0:T(8,128)(2,1)}), bf16[256,1536]{1,0:T(8,128)(2,1)}) %reduce-scatter.24.cloned.1.call-update) | async-done | bytes 786448 | tf_op jit(solution)/shard_map/reduce_scatter | solution.py:47
  135.2 24.9 %all-gather.9.cloned.1.call-done = bf16[1024,1536]{1,0:T(8,128)(2,1)} async-done(((bf16[256,1536]{1,0:T(8,128)(2,1)}), bf16[1024,1536]{1,0:T(8,128)(2,1)}) %all-gather.9.cloned.1.call-update) | async-done | bytes 3145744 | tf_op jit(solution)/shard_map/all_gather | solution.py:39
  160.1 4.5 convolution_convert_fusion.7
  164.6 2.5 fusion.113
  169.5 3.5 convolution_convert_fusion.3
  173.1 38.0 %reduce-scatter.26.cloned.1.call-done = bf16[256,1536]{1,0:T(8,128)(2,1)} async-done(((bf16[1024,1536]{1,0:T(8,128)(2,1)}), bf16[256,1536]{1,0:T(8,128)(2,1)}) %reduce-scatter.26.cloned.1.call-update) | async-done | bytes 786448 | tf_op jit(solution)/shard_map/reduce_scatter | solution.py:47
  211.1 2.7 fusion.110
  218.1 27.7 %all-gather.11.cloned.1.call-done = bf16[1024,1536]{1,0:T(8,128)(2,1)} async-done(((bf16[256,1536]{1,0:T(8,128)(2,1)}), bf16[1024,1536]{1,0:T(8,128)(2,1)}) %all-gather.11.cloned.1.call-update) | async-done | bytes 3145744 | tf_op jit(solution)/shard_map/all_gather | solution.py:39
  245.8 9.7 fusion.114
  255.5 20.2 %all-gather.13.cloned.1.call-done = bf16[1024,1536]{1,0:T(8,128)(2,1)} async-done(((bf16[256,1536]{1,0:T(8,128)(2,1)}), bf16[1024,1536]{1,0:T(8,128)(2,1)}) %all-gather.13.cloned.1.call-update) | async-done | bytes 3145744 | tf_op jit(solution)/shard_map/all_gather | solution.py:43
  275.8 24.4 %add_convert_fusion.1 = (bf16[1024,1536]{1,0:T(8,128)(2,1)S(1)}, f32[1024,1536]{1,0:T(8,128)}) fusion(f32[1024,1536]{1,0:T(8,128)} %fusion.114, bf16[1024,1536]{1,0:T(8,128)(2,1)} %all-gather.13.cloned.1.call-done, bf16[1536,1536]{1,0:T(8,128)(2,1)} %param.48), kind=kOutput, calls=%fused_computation.13 | convolution fusion | flops 4945084416 | bytes 23592960 | tf_op jit(solution)/shard_map/dot_general | solution.py:33
  301.8 8.8 convolution_convert_fusion.1
  310.6 6.2 multiply_convert_fusion.2
  318.5 9.3 convolution_convert_fusion.2
  327.9 10.9 all-gather.15.cloned.1.call-start
  338.8 9.8 reduce-scatter.30.cloned.1.call-done
  348.6 2.3 fusion.42
  352.2 36.9 %reduce-scatter.28.cloned.1.call-done = bf16[256,1536]{1,0:T(8,128)(2,1)} async-done(((bf16[1024,1536]{1,0:T(8,128)(2,1)}), bf16[256,1536]{1,0:T(8,128)(2,1)}) %reduce-scatter.28.cloned.1.call-update) | async-done | bytes 786448 | tf_op jit(solution)/shard_map/reduce_scatter | solution.py:47
  389.1 3.8 fusion.108
  395.2 28.6 %all-gather.15.cloned.1.call-done = bf16[1024,1536]{1,0:T(8,128)(2,1)} async-done(((bf16[256,1536]{1,0:T(8,128)(2,1)}), bf16[1024,1536]{1,0:T(8,128)(2,1)}) %all-gather.15.cloned.1.call-update) | async-done | bytes 3145744 | tf_op jit(solution)/shard_map/all_gather | solution.py:43
  423.8 3.3 convolution_convert_fusion.6
  430.2 3.6 convolution_convert_fusion
  433.9 38.0 %reduce-scatter.32.cloned.1.call-done = bf16[256,1536]{1,0:T(8,128)(2,1)} async-done(((bf16[1024,1536]{1,0:T(8,128)(2,1)}), bf16[256,1536]{1,0:T(8,128)(2,1)}) %reduce-scatter.32.cloned.1.call-update) | async-done | bytes 786448 | tf_op jit(solution)/shard_map/reduce_scatter | solution.py:59
  471.9 3.0 fusion.47
  474.8 2.6 fusion.43
  488.3 20.1 %all-gather.17.cloned.1.call-done = bf16[1024,1536]{1,0:T(8,128)(2,1)} async-done(((bf16[256,1536]{1,0:T(8,128)(2,1)}), bf16[1024,1536]{1,0:T(8,128)(2,1)}) %all-gather.17.cloned.1.call-update) | async-done | bytes 3145744 | tf_op jit(solution)/shard_map/all_gather | solution.py:43
  508.4 3.4 convolution_convert_fusion.5
  511.9 4.0 fusion.59
  516.0 3.7 multiply_reduce_fusion.1
  519.6 6.6 multiply_convert_fusion.1
  528.7 6.2 multiply_reduce_fusion
  536.6 5.9 multiply_convert_fusion
  549.6 3.6 add_convert_fusion
  553.3 5.5 fusion.123
  559.0 5.4 fusion.122
  566.4 3.1 copy.77
  571.5 3.2 copy.75
  574.7 9.9 fusion.125
  584.7 9.9 fusion.124
  594.7 5.4 fusion.121
  600.4 5.1 fusion.120
  605.5 5.1 fusion.119
  610.8 5.2 fusion.118
  617.8 2.6 pad_maximum_fusion.2
  624.3 41.6 %all-reduce.2 = (f32[1536]{0:T(1024)}, f32[1536]{0:T(1024)}, f32[1536]{0:T(1024)}, f32[1536]{0:T(1024)}, f32[1536]{0:T(1024)}, /*index=5*/f32[1536]{0:T(1024)}, f32[4]{0:T(128)S(1)}) all-reduce(f32[1536]{0:T(1024)S(1)} %get-tuple-element.148, f32[1536]{0:T(1024)S(1)} %get-tuple-element.155, ...), channel_id=1, replica_groups=mesh['dp'=8,'tensor'=4] {'dp','tensor'}, use_global_device_ids=true, to_apply=%region_29.30 | all-reduce | flops 9220 | bytes 73760 | tf_op jit(solution)/shard_map/psum | solution.py:328
  666.4 2.9 add_convert_fusion.2
  669.3 68.0 %reduce-scatter.44.cloned.1.call-done = f32[192,384]{1,0:T(8,128)} async-done(((f32[1536,384]{1,0:T(8,128)}), f32[192,384]{1,0:T(8,128)}) %reduce-scatter.44.cloned.1.call-update) | async-done | bytes 294928 | tf_op jit(solution)/shard_map/reduce_scatter | solution.py:320
  737.3 72.6 %reduce-scatter.56.cloned.1.call-done = f32[192,384]{1,0:T(8,128)} async-done(((f32[1536,384]{1,0:T(8,128)}), f32[192,384]{1,0:T(8,128)}) %reduce-scatter.56.cloned.1.call-update) | async-done | bytes 294928
  809.9 72.6 %reduce-scatter.54.cloned.1.call-done = f32[192,384]{1,0:T(8,128)} async-done(((f32[1536,384]{1,0:T(8,128)}), f32[192,384]{1,0:T(8,128)}) %reduce-scatter.54.cloned.1.call-update) | async-done | bytes 294928
  882.5 164.8 %reduce-scatter.50.cloned.1.call-done = f32[1536,192]{0,1:T(8,128)} async-done(((f32[1536,1536]{0,1:T(8,128)}), f32[1536,192]{0,1:T(8,128)}) %reduce-scatter.50.cloned.1.call-update) | async-done | bytes 1179664 | tf_op jit(solution)/shard_map/reduce_scatter | solution.py:325
  1047.4 165.4 %reduce-scatter.48.cloned.1.call-done = f32[192,1536]{1,0:T(8,128)} async-done(((f32[1536,1536]{1,0:T(8,128)}), f32[192,1536]{1,0:T(8,128)}) %reduce-scatter.48.cloned.1.call-update) | async-done | bytes 1179664 | tf_op jit(solution)/shard_map/reduce_scatter | solution.py:324
  1212.8 73.2 %reduce-scatter.42.cloned.1.call-done = f32[384,192]{0,1:T(8,128)} async-done(((f32[384,1536]{0,1:T(8,128)}), f32[384,192]{0,1:T(8,128)}) %reduce-scatter.42.cloned.1.call-update) | async-done | bytes 294928 | tf_op jit(solution)/shard_map/reduce_scatter | solution.py:319
  1286.0 72.8 %reduce-scatter.40.cloned.1.call-done = f32[192,384]{1,0:T(8,128)} async-done(((f32[1536,384]{1,0:T(8,128)}), f32[192,384]{1,0:T(8,128)}) %reduce-scatter.40.cloned.1.call-update) | async-done | bytes 294928 | tf_op jit(solution)/shard_map/reduce_scatter | solution.py:318
  1358.9 73.0 %reduce-scatter.38.cloned.1.call-done = f32[192,384]{1,0:T(8,128)} async-done(((f32[1536,384]{1,0:T(8,128)}), f32[192,384]{1,0:T(8,128)}) %reduce-scatter.38.cloned.1.call-update) | async-done | bytes 294928 | tf_op jit(solution)/shard_map/reduce_scatter | solution.py:317
  1431.8 73.1 %reduce-scatter.36.cloned.1.call-done = f32[192,384]{1,0:T(8,128)} async-done(((f32[1536,384]{1,0:T(8,128)}), f32[192,384]{1,0:T(8,128)}) %reduce-scatter.36.cloned.1.call-update) | async-done | bytes 294928 | tf_op jit(solution)/shard_map/reduce_scatter | solution.py:316
  (279 shorter events, 67.2 us)
Async XLA Ops:
  7.2 162.3 %copy-start = (bf16[384,1536]{1,0:T(8,128)(2,1)S(1)}, bf16[384,1536]{1,0:T(8,128)(2,1)}, u32[]{:S(2)}) copy-start(bf16[384,1536]{1,0:T(8,128)(2,1)} %param.44) | copy-start | bytes 3538948
  7.2 35.3 %copy-start.25 = (bf16[1536,384]{1,0:T(8,128)(2,1)S(1)}, bf16[1536,384]{1,0:T(8,128)(2,1)}, u32[]{:S(2)}) copy-start(bf16[1536,384]{1,0:T(8,128)(2,1)} %param.36) | copy-start | bytes 3538948
  7.2 35.3 %all-gather.7.cloned.1.call-start = ((), (), s32[]{:S(2)}) async-start(), calls=%async_computation.17 | async-start | bytes 3932160 | tf_op jit(solution)/shard_map/all_gather | solution.py:39
  12.7 114.2 %reduce-scatter.24.cloned.1.call-start = ((), (), s32[]{:S(2)}) async-start(), calls=%async_computation.18 | async-start | bytes 3932160 | tf_op jit(solution)/shard_map/reduce_scatter | solution.py:47
  46.0 7.8 copy-start.16
  47.5 6.4 copy-start.23
  58.9 20.4 %copy-start.59 = (f32[6,512]{1,0:T(8,128)}, f32[6,512]{1,0:T(8,128)S(1)}, u32[]{:S(2)}) copy-start(f32[6,512]{1,0:T(8,128)S(1)} %get-tuple-element.177) | copy-start | bytes 36868
  58.9 16.8 %copy-start.29 = (bf16[1536,384]{1,0:T(8,128)(2,1)S(1)}, bf16[1536,384]{1,0:T(8,128)(2,1)}, u32[]{:S(2)}) copy-start(bf16[1536,384]{1,0:T(8,128)(2,1)} %param.37) | copy-start | bytes 3538948
  58.9 20.4 %copy-start.15 = (f32[6,512,512]{1,2,0:T(8,128)S(1)}, f32[6,512,512]{1,2,0:T(8,128)}, u32[]{:S(2)}) copy-start(f32[6,512,512]{1,2,0:T(8,128)} %get-tuple-element.178) | copy-start | bytes 18874372
  88.8 38.1 %copy-start.2 = (bf16[256,1536]{1,0:T(8,128)(2,1)S(1)}, bf16[256,1536]{1,0:T(8,128)(2,1)}, u32[]{:S(2)}) copy-start(bf16[256,1536]{1,0:T(8,128)(2,1)} %param.31) | copy-start | bytes 2359300
  88.8 41.2 %copy-start.42 = (f32[1536]{0:T(1024)S(1)}, f32[1536]{0:T(1024)}, u32[]{:S(2)}) copy-start(f32[1536]{0:T(1024)} %param.39) | copy-start | bytes 18436
  88.8 41.3 %copy-start.68 = (f32[1536]{0:T(1024)S(1)}, f32[1536]{0:T(1024)}, u32[]{:S(2)}) copy-start(f32[1536]{0:T(1024)} %param.40) | copy-start | bytes 18436
  88.8 42.9 %copy-start.21 = (bf16[1,64,1536]{2,1,0:T(8,128)(2,1)S(1)}, bf16[1,64,1536]{2,1,0:T(8,128)(2,1)}, u32[]{:S(2)}) copy-start(bf16[1,64,1536]{2,1,0:T(8,128)(2,1)} %param.32) | copy-start | bytes 589828
  88.9 71.2 %all-gather.9.cloned.1.call-start = ((), (), s32[]{:S(2)}) async-start(), calls=%async_computation.19 | async-start | bytes 3932160 | tf_op jit(solution)/shard_map/all_gather | solution.py:39
  128.4 5.7 copy-start.18
  131.5 79.6 %reduce-scatter.26.cloned.1.call-start = ((), (), s32[]{:S(2)}) async-start(), calls=%async_computation.20 | async-start | bytes 3932160 | tf_op jit(solution)/shard_map/reduce_scatter | solution.py:47
  167.1 5.9 copy-start.12
  173.0 42.2 %copy-start.43 = (f32[1536]{0:T(1024)S(1)}, f32[1536]{0:T(1024)}, u32[]{:S(2)}) copy-start(f32[1536]{0:T(1024)} %param.45) | copy-start | bytes 18436
  173.0 72.8 %all-gather.11.cloned.1.call-start = ((), (), s32[]{:S(2)}) async-start(), calls=%async_computation.21 | async-start | bytes 3932160 | tf_op jit(solution)/shard_map/all_gather | solution.py:39
  217.1 58.6 %all-gather.13.cloned.1.call-start = ((), (), s32[]{:S(2)}) async-start(), calls=%async_computation.23 | async-start | bytes 3932160 | tf_op jit(solution)/shard_map/all_gather | solution.py:43
  217.7 130.9 %reduce-scatter.30.cloned.1.call-start = ((), (), s32[]{:S(2)}) async-start(), calls=%async_computation.24 | async-start | bytes 3932160 | tf_op jit(solution)/shard_map/reduce_scatter | solution.py:59
  310.6 78.5 %reduce-scatter.28.cloned.1.call-start = ((), (), s32[]{:S(2)}) async-start(), calls=%async_computation.22 | async-start | bytes 3932160 | tf_op jit(solution)/shard_map/reduce_scatter | solution.py:47
  327.9 95.9 %all-gather.15.cloned.1.call-start = ((), (), s32[]{:S(2)}) async-start(), calls=%async_computation.25 | async-start | bytes 3932160 | tf_op jit(solution)/shard_map/all_gather | solution.py:43
  395.2 32.0 %copy-start.13 = (f32[6,1024,64]{1,2,0:T(8,128)S(1)}, f32[6,1024,64]{1,2,0:T(8,128)}, u32[]{:S(2)}) copy-start(f32[6,1024,64]{1,2,0:T(8,128)} %copy-done.12) | copy-start | bytes 4718596
  395.2 76.7 %reduce-scatter.32.cloned.1.call-start = ((), (), s32[]{:S(2)}) async-start(), calls=%async_computation.26 | async-start | bytes 3932160 | tf_op jit(solution)/shard_map/reduce_scatter | solution.py:59
  433.8 38.1 %copy-start.4 = (bf16[256,1536]{1,0:T(8,128)(2,1)S(1)}, bf16[256,1536]{1,0:T(8,128)(2,1)}, u32[]{:S(2)}) copy-start(bf16[256,1536]{1,0:T(8,128)(2,1)} %reduce-scatter.24.cloned.1.call-done) | copy-start | bytes 2359300
  433.8 38.1 %copy-start.45 = (f32[256]{0:T(256)S(1)}, f32[256]{0:T(256)}, u32[]{:S(2)}) copy-start(f32[256]{0:T(256)} %copy-done.44) | copy-start | bytes 3076
  433.8 41.0 %copy-start.66 = (f32[256]{0:T(256)S(1)}, f32[256]{0:T(256)}, u32[]{:S(2)}) copy-start(f32[256]{0:T(256)} %copy-done.65) | copy-start | bytes 3076
  433.8 41.1 %copy-start.58 = (f32[256]{0:T(256)S(1)}, f32[256]{0:T(256)}, u32[]{:S(2)}) copy-start(f32[256]{0:T(256)} %copy-done.57) | copy-start | bytes 3076
  433.8 43.6 %copy-start.6 = (f32[256,1536]{1,0:T(8,128)S(1)}, f32[256,1536]{1,0:T(8,128)}, u32[]{:S(2)}) copy-start(f32[256,1536]{1,0:T(8,128)} %copy-done.5) | copy-start | bytes 4718596
  433.8 43.6 %copy-start.62 = (f32[256]{0:T(256)S(1)}, f32[256]{0:T(256)}, u32[]{:S(2)}) copy-start(f32[256]{0:T(256)} %copy-done.61) | copy-start | bytes 3076
  433.8 74.6 %all-gather.17.cloned.1.call-start = ((), (), s32[]{:S(2)}) async-start(), calls=%async_computation.27 | async-start | bytes 3932160 | tf_op jit(solution)/shard_map/all_gather | solution.py:43
  471.9 5.6 copy-start.9
  471.9 5.6 copy-start.11
  479.8 136.3 %reduce-scatter.52.cloned.1.call-start = ((), (), s32[]{:S(2)}) async-start(), calls=%async_computation.37 | async-start | bytes 491520
  485.7 22.7 %copy-start.72 = (bf16[384,1536]{1,0:T(8,128)(2,1)S(1)}, bf16[384,1536]{1,0:T(8,128)(2,1)}, u32[]{:S(2)}) copy-start(bf16[384,1536]{1,0:T(8,128)(2,1)} %param.38) | copy-start | bytes 3538948
  488.2 23.7 %copy-start.60 = (f32[6,512]{1,0:T(8,128)S(1)}, f32[6,512]{1,0:T(8,128)}, u32[]{:S(2)}) copy-start(f32[6,512]{1,0:T(8,128)} %copy-done.59) | copy-start | bytes 36868
  488.2 132.2 %reduce-scatter.34.cloned.1.call-start = ((), (), s32[]{:S(2)}) async-start(), calls=%async_computation.28 | async-start | bytes 3932160 | tf_op jit(solution)/shard_map/reduce_scatter | solution.py:59
  508.4 7.5 slice-start.6
  519.6 6.6 copy-start.17
  519.6 7.2 copy-start.24
  519.6 8.3 slice-start.3
  519.6 8.3 slice-start.4
  553.3 116.0 %reduce-scatter.46.cloned.1.call-start = ((), (), s32[]{:S(2)}) async-start(), calls=%async_computation.34 | async-start | bytes 2654208 | tf_op jit(solution)/shard_map/reduce_scatter | solution.py:323
  558.8 5.7 copy-start.22
  558.8 5.7 copy-start.38
  558.8 178.5 %reduce-scatter.44.cloned.1.call-start = ((), (), s32[]{:S(2)}) async-start(), calls=%async_computation.33 | async-start | bytes 2654208 | tf_op jit(solution)/shard_map/reduce_scatter | solution.py:320
  564.5 245.4 %reduce-scatter.56.cloned.1.call-start = ((), (), s32[]{:S(2)}) async-start(), calls=%async_computation.39 | async-start | bytes 2654208
  569.6 313.0 %reduce-scatter.54.cloned.1.call-start = ((), (), s32[]{:S(2)}) async-start(), calls=%async_computation.38 | async-start | bytes 2654208
  574.7 472.7 %reduce-scatter.50.cloned.1.call-start = ((), (), s32[]{:S(2)}) async-start(), calls=%async_computation.36 | async-start | bytes 10616832 | tf_op jit(solution)/shard_map/reduce_scatter | solution.py:325
  584.6 628.2 %reduce-scatter.48.cloned.1.call-start = ((), (), s32[]{:S(2)}) async-start(), calls=%async_computation.35 | async-start | bytes 10616832 | tf_op jit(solution)/shard_map/reduce_scatter | solution.py:324
  594.6 691.4 %reduce-scatter.42.cloned.1.call-start = ((), (), s32[]{:S(2)}) async-start(), calls=%async_computation.32 | async-start | bytes 2654208 | tf_op jit(solution)/shard_map/reduce_scatter | solution.py:319
  600.1 758.8 %reduce-scatter.40.cloned.1.call-start = ((), (), s32[]{:S(2)}) async-start(), calls=%async_computation.31 | async-start | bytes 2654208 | tf_op jit(solution)/shard_map/reduce_scatter | solution.py:318
  605.5 826.3 %reduce-scatter.38.cloned.1.call-start = ((), (), s32[]{:S(2)}) async-start(), calls=%async_computation.30 | async-start | bytes 2654208 | tf_op jit(solution)/shard_map/reduce_scatter | solution.py:317
  610.7 9.7 copy-start.40
  610.7 9.7 copy-start.47
  610.7 894.2 %reduce-scatter.36.cloned.1.call-start = ((), (), s32[]{:S(2)}) async-start(), calls=%async_computation.29 | async-start | bytes 2654208 | tf_op jit(solution)/shard_map/reduce_scatter | solution.py:316
  616.0 6.3 copy-start.64
  616.0 6.3 copy-start.56
  616.0 8.2 copy-start.48
  616.0 8.2 copy-start.49
  616.0 8.3 copy-start.50
  620.4 46.0 %copy-start.7 = (bf16[256,1536]{1,0:T(8,128)(2,1)S(1)}, bf16[256,1536]{1,0:T(8,128)(2,1)}, u32[]{:S(2)}) copy-start(bf16[256,1536]{1,0:T(8,128)(2,1)} %reduce-scatter.34.cloned.1.call-done) | copy-start | bytes 2359300
  620.4 884.5 %copy-start.1 = (bf16[384,1536]{1,0:T(8,128)(2,1)S(1)}, bf16[384,1536]{1,0:T(8,128)(2,1)}, u32[]{:S(2)}) copy-start(bf16[384,1536]{1,0:T(8,128)(2,1)} %param.44) | copy-start | bytes 3538948
  (45 other events, 109.3 us)
Sparse Core Ops, SparseCore 0:
  12.8 29.6 all-gather.6
  89.0 37.8 reduce-scatter.23
  131.6 28.4 all-gather.8
  173.2 37.8 reduce-scatter.25
  217.3 28.4 all-gather.10
  247.2 28.4 all-gather.12
  310.7 37.8 reduce-scatter.29
  351.1 37.8 reduce-scatter.27
  395.3 28.4 all-gather.14
  433.9 37.8 reduce-scatter.31
  479.9 28.4 all-gather.16
  511.3 20.8 reduce-scatter.51
  553.4 37.8 reduce-scatter.33
  595.2 69.5 reduce-scatter.45
  668.7 68.5 reduce-scatter.43
  741.2 68.6 reduce-scatter.55
  813.8 68.6 reduce-scatter.53
  886.6 160.7 reduce-scatter.49
  1051.5 161.1 reduce-scatter.47
  1216.7 69.2 reduce-scatter.41
  1290.1 68.6 reduce-scatter.39
  1362.9 68.8 reduce-scatter.37
  1435.9 68.9 reduce-scatter.35
where the time goes:
time: 1520 us; the launch traced here: 1510 us
  waiting for transfers between devices  1150 us (76%)
  matrix products  192 us (13%)
  other arithmetic  78.1 us (5%)
  blocking collectives  41.6 us (3%)
  local copies, waits for them, and re-layouts  24.4 us (2%)
  between operations  15.3 us (1%)
    reduce_scatter x1, waiting for transfers between devices, body(): lax.psum_scatter(w_in_part, 'dp', scatter_dimension=0, tiled=True)  165 us
    reduce_scatter x1, waiting for transfers between devices, body(): lax.psum_scatter(w_out_part, 'dp', scatter_dimension=1, tiled=True)  165 us
    unnamed x26, waiting for transfers between devices  146 us
    reduce_scatter x3, waiting for transfers between devices, sum_branch(): lax.psum_scatter(product(values, weight_mat).astype(jnp.bfloat16), 'tenso...  113 us
    all_gather x3, waiting for transfers between devices, gather_normed(): return lax.all_gather(values, 'tensor', axis=0, tiled=True)  81.1 us
    reduce_scatter x1, waiting for transfers between devices, body(): lax.psum_scatter(w_o_part, 'dp', scatter_dimension=1, tiled=True)  73.2 us
    reduce_scatter x1, waiting for transfers between devices, body(): lax.psum_scatter(w_q_part, 'dp', scatter_dimension=0, tiled=True)  73.1 us
    reduce_scatter x1, waiting for transfers between devices, body(): lax.psum_scatter(w_k_part, 'dp', scatter_dimension=0, tiled=True)  73 us
  transfers between devices with their start and end apart: 23, of which 20 were waited for; matrix products, arithmetic and copies ran while one was open for 10% of the time, Pallas kernels for 0%

commit v1 on v0

--- a/solution.py
+++ b/solution.py
@@ -35,30 +35,80 @@
     )
 
 
-def gather_normed(values):
-    return lax.all_gather(values, "tensor", axis=0, tiled=True)
-
-
-def gather_grads(values):
-    return lax.all_gather(values, "tensor", axis=0, tiled=True)
-
-
-def sum_branch(values, weight_mat):
-    return lax.psum_scatter(
-        product(values, weight_mat).astype(jnp.bfloat16), "tensor", scatter_dimension=0, tiled=True
-    ).astype(jnp.float32)
-
-
-def sum_inputs(grad_list, weight_list):
-    own_rows = grad_list[0].shape[0] // lax.axis_size("tensor")
-    total_sum = jnp.zeros(
-        (lax.axis_size("tensor") * own_rows, weight_list[0].shape[0]), jnp.float32
-    )
-    for grad_mat, weight_mat in zip(grad_list, weight_list):
-        total_sum = total_sum + contract_cols(grad_mat, weight_mat)
-    return lax.psum_scatter(
-        total_sum.astype(jnp.bfloat16), "tensor", scatter_dimension=0, tiled=True
-    ).astype(jnp.float32)
+def exchange(values, flip):
+    return lax.ppermute(values, "tensor", [(i, i ^ flip) for i in range(4)])
+
+
+def gather_relative(values):
+    far = exchange(values, 2)
+    return values, exchange(values, 1), far, exchange(far, 1)
+
+
+def scatter_relative(near_own, near_other, far_mine, far_other):
+    over_link = exchange(far_mine + exchange(far_other, 1), 2)
+    return near_own.astype(jnp.float32) + exchange(near_other, 1) + over_link
+
+
+def swap_relative(blocks):
+    return [blocks[0]] + [exchange(blocks[flip], flip) for flip in (1, 2, 3)]
+
+
+def to_absolute(values, own_id):
+    rows = values.shape[0] // 4
+    return jnp.concatenate(
+        [lax.dynamic_slice_in_dim(values, (own_id ^ flip) * rows, rows, 0) for flip in range(4)]
+    )
+
+
+def scatter_product(far_pair, near_pair, own_rows):
+    far_part = far_pair().astype(jnp.bfloat16)
+    mine, other = far_part[:own_rows], far_part[own_rows:]
+    over_link = exchange(mine + exchange(other, 1), 2)
+    near_part = near_pair()
+    near_other = exchange(near_part[own_rows:].astype(jnp.bfloat16), 1)
+    return near_part[:own_rows] + near_other + over_link
+
+
+def sum_clips(part):
+    size = lax.axis_size("dp")
+    if size != 8:
+        return lax.psum_scatter(
+            part.astype(jnp.bfloat16), "dp", scatter_dimension=0, tiled=True
+        ).astype(jnp.float32)
+    own = lax.axis_index("dp")
+    own_z, own_y = own // 2, own % 2
+    rows = part.shape[0] // 8
+    halves = part.astype(jnp.bfloat16).reshape(4, 2, rows, part.shape[1])
+    sent = lax.dynamic_index_in_dim(halves, 1 - own_y, 1, keepdims=False)
+    kept = lax.dynamic_index_in_dim(halves, own_y, 1, keepdims=False)
+    kept = kept + lax.ppermute(sent, "dp", [(i, i ^ 1) for i in range(8)])
+    total = lax.dynamic_index_in_dim(kept, own_z, 0, keepdims=False).astype(jnp.float32)
+    for sign in (1, -1):
+        carried = None
+        for step in range(1, 4):
+            target = jnp.clip(own_z + sign * (4 - step), 0, 3)
+            block = lax.dynamic_index_in_dim(kept, target, 0, keepdims=False)
+            if carried is not None:
+                block = block + carried
+            senders = range(step) if sign > 0 else range(3, 3 - step, -1)
+            pairs = [(2 * z + y, 2 * (z + sign) + y) for z in senders for y in range(2)]
+            carried = lax.ppermute(block, "dp", pairs)
+        total = total + carried
+    return total
+
+
+def sum_everywhere(values):
+    if lax.axis_size("dp") != 8:
+        return lax.psum(values, ("dp", "tensor"))
+    for flip in (1, 2):
+        values = values + exchange(values, flip)
+    for flip in (1, 2, 4):
+        values = values + lax.ppermute(values, "dp", [(i, i ^ flip) for i in range(8)])
+    return values
+
+
+def after(values, *others):
+    return lax.optimization_barrier((values,) + others)[0]
 
 
 def block_scores(queries, all_keys, begin_row, end_row):
@@ -206,43 +256,90 @@
 ):
     clip_count = text_states.shape[0]
     text_len = text_states.shape[1]
-    model_width = layer_input.shape[1]
-    local_heads = w_q.shape[1] // HD
+    own_rows, model_width = layer_input.shape
+    local_width = w_q.shape[1]
+    local_heads = local_width // HD
+    own_id = lax.axis_index("tensor")
+    low = jnp.bfloat16
 
     def split_heads(matrix, length):
-        return matrix.astype(jnp.bfloat16).reshape(clip_count, length, local_heads, HD)
+        return matrix.astype(low).reshape(1, length, matrix.shape[1] // HD, HD)
 
     def merge_heads(tensor_four):
-        return tensor_four.reshape(clip_count * tensor_four.shape[1], local_heads * HD).astype(
-            jnp.bfloat16
-        )
+        return tensor_four.reshape(tensor_four.shape[1], -1).astype(low)
 
     stream = layer_input.astype(jnp.float32)
-    normed_one = layer_norm(stream, ln1_gain, ln1_bias).astype(jnp.bfloat16)
-    rows_one = gather_normed(normed_one)
-    queries = split_heads(product(rows_one, w_q), FRAMES)
-    all_keys = split_heads(product(rows_one, w_k), FRAMES)
-    all_values = split_heads(product(rows_one, w_v), FRAMES)
+    normed_one = layer_norm(stream, ln1_gain, ln1_bias).astype(low)
+    one = gather_relative(normed_one)
+    w_qkv = jnp.concatenate([w_q, w_k, w_v], axis=1)
+    near_one = jnp.concatenate(one[:2])
+    far_one = jnp.concatenate(one[2:])
+    rows_one = jnp.concatenate([near_one, far_one])
+    qkv = jnp.concatenate(
+        [product(near_one, w_qkv).astype(low), product(far_one, w_qkv).astype(low)]
+    )
+    qkv = to_absolute(qkv, own_id)
+    queries, all_keys, all_values = [
+        split_heads(qkv[:, i * local_width : (i + 1) * local_width], FRAMES) for i in range(3)
+    ]
     mixed_one, peak_list, sum_list = self_forward(queries, all_keys, all_values)
-    attended = merge_heads(mixed_one)
-    branch_one = sum_branch(attended, w_o)
+    attended = to_absolute(merge_heads(mixed_one), own_id)
+    branch_one = scatter_product(
+        lambda: product(attended[2 * own_rows :], w_o),
+        lambda: product(attended[: 2 * own_rows], w_o),
+        own_rows,
+    )
+
+    c_q_full = jnp.concatenate(gather_relative(after(c_q, one[2])), axis=1)
+    c_o_full = jnp.concatenate(gather_relative(after(c_o, one[2])), axis=0)
+    text_rows = text_states.reshape(clip_count * text_len, model_width)
+    text_kv = after(
+        jnp.concatenate([product(text_rows, c_k), product(text_rows, c_v)]).astype(low), one[2]
+    )
+    text_kv = jnp.concatenate(gather_relative(text_kv), axis=1)
+    text_keys = split_heads(text_kv[:text_len], text_len)
+    text_values = split_heads(text_kv[text_len:], text_len)
+    grad_rows = gather_relative(after(out_cotangent, c_o_full))
+    grad_near = jnp.concatenate(grad_rows[:2])
+    grad_far = jnp.concatenate(grad_rows[2:])
+    grad_three_rows = jnp.concatenate([grad_near, grad_far])
+
     hidden_one = stream + branch_one
-    normed_two = layer_norm(hidden_one, ln2_gain, ln2_bias).astype(jnp.bfloat16)
-    rows_two = gather_normed(normed_two)
-    cross_queries = split_heads(product(rows_two, c_q), FRAMES)
-    text_rows = text_states.reshape(clip_count * text_len, model_width)
-    text_keys = split_heads(product(text_rows, c_k), text_len)
-    text_values = split_heads(product(text_rows, c_v), text_len)
+    normed_two = layer_norm(hidden_one, ln2_gain, ln2_bias).astype(low)
+    cross_queries = split_heads(product(normed_two, c_q_full), own_rows)
     mixed_two, cross_weights = cross_forward(cross_queries, text_keys, text_values)
     crossed = merge_heads(mixed_two)
-    branch_two = sum_branch(crossed, c_o)
+    branch_two = product(crossed, c_o_full)
     hidden_two = hidden_one + branch_two
-    normed_three = layer_norm(hidden_two, ln3_gain, ln3_bias).astype(jnp.bfloat16)
-    rows_three = gather_normed(normed_three)
-    pre_act = product(rows_three, w_in)
-    activated = jax.nn.gelu(pre_act, approximate=False).astype(jnp.bfloat16)
-    branch_three = sum_branch(activated, w_out)
-    block_out = (hidden_two + branch_three).astype(jnp.bfloat16)
+    normed_three = layer_norm(hidden_two, ln3_gain, ln3_bias).astype(low)
+
+    three = gather_relative(normed_three)
+    near_three = jnp.concatenate(three[:2])
+    far_three = jnp.concatenate(three[2:])
+    act_parts, pre_grads = [], []
+    for rows, grads in ((near_three, grad_near), (far_three, grad_far)):
+        pre_act = product(rows, w_in)
+        gelu_value, gelu_back = jax.vjp(partial(jax.nn.gelu, approximate=False), pre_act)
+        act_parts.append(gelu_value.astype(low))
+        pre_grads.append(gelu_back(contract_cols(grads, w_out))[0].astype(low))
+    grad_normed_three = scatter_product(
+        lambda: contract_cols(pre_grads[1], w_in),
+        lambda: contract_cols(pre_grads[0], w_in),
+        own_rows,
+    )
+    rows_three = jnp.concatenate([near_three, far_three])
+    activated = jnp.concatenate(act_parts)
+    grad_pre = jnp.concatenate(pre_grads)
+    w_out_part = contract_rows(grad_three_rows, activated)
+    w_in_part = contract_rows(rows_three, grad_pre)
+    w_out_grad = sum_clips(w_out_part).T
+    w_in_grad = sum_clips(w_in_part)
+    branch_three = scatter_product(
+        lambda: product(after(act_parts[1], grad_normed_three), w_out),
+        lambda: product(act_parts[0], w_out),
+        own_rows,
+    )
+    block_out = (hidden_two + branch_three).astype(low)
     squares = jnp.stack(
         [
             jnp.sum(stream * stream),
@@ -251,93 +348,97 @@
             jnp.sum(branch_three * branch_three),
         ]
     )
-    square_totals = lax.psum(squares, ("dp", "tensor"))
+
     grad_out = out_cotangent.astype(jnp.float32)
-    grad_three_rows = gather_grads(out_cotangent)
-    w_out_part = contract_rows(activated, grad_three_rows)
-    grad_act = contract_cols(grad_three_rows, w_out)
-    gelu_value, gelu_back = jax.vjp(partial(jax.nn.gelu, approximate=False), pre_act)
-    grad_pre = gelu_back(grad_act)[0].astype(jnp.bfloat16)
-    w_in_part = contract_rows(rows_three, grad_pre)
-    grad_normed_three = sum_inputs((grad_pre,), (w_in,))
     norm_value, norm_back = jax.vjp(layer_norm, hidden_two, ln3_gain, ln3_bias)
     back_rows, ln3_gain_part, ln3_bias_part = norm_back(grad_normed_three)
     grad_two = grad_out + back_rows
-    grad_two_rows = gather_grads(grad_two.astype(jnp.bfloat16))
-    c_o_part = contract_rows(crossed, grad_two_rows)
-    grad_mixed_two = split_heads(contract_cols(grad_two_rows, c_o), FRAMES)
+    grad_two_low = grad_two.astype(low)
+    grad_mixed_two = split_heads(contract_cols(grad_two_low, c_o_full), own_rows)
     grad_cq, grad_tk, grad_tv = cross_backward(
         cross_queries, text_keys, text_values, cross_weights, grad_mixed_two
     )
     grad_cq = merge_heads(grad_cq)
-    grad_tk = merge_heads(grad_tk)
-    grad_tv = merge_heads(grad_tv)
-    c_q_part = contract_rows(rows_two, grad_cq)
-    c_k_part = contract_rows(text_rows, grad_tk)
-    c_v_part = contract_rows(text_rows, grad_tv)
-    text_term = (contract_cols(grad_tk, c_k) + contract_cols(grad_tv, c_v)).reshape(
-        clip_count, text_len, model_width
-    )
-    text_states_grad = lax.psum_scatter(
-        text_term.astype(jnp.bfloat16), "tensor", scatter_dimension=2, tiled=True
-    )
-    grad_normed_two = sum_inputs((grad_cq,), (c_q,))
+    grad_normed_two = contract_cols(grad_cq, c_q_full)
     norm_value, norm_back = jax.vjp(layer_norm, hidden_one, ln2_gain, ln2_bias)
     back_rows, ln2_gain_part, ln2_bias_part = norm_back(grad_normed_two)
     grad_one = grad_two + back_rows
-    grad_one_rows = gather_grads(grad_one.astype(jnp.bfloat16))
-    w_o_part = contract_rows(attended, grad_one_rows)
-    grad_mixed_one = split_heads(contract_cols(grad_one_rows, w_o), FRAMES)
+
+    one_grads = gather_relative(grad_one.astype(low))
+    grad_one_rows = jnp.concatenate(one_grads)
+    grad_mixed_one = jnp.concatenate(
+        [
+            contract_cols(jnp.concatenate(one_grads[:2]), w_o).astype(low),
+            contract_cols(jnp.concatenate(one_grads[2:]), w_o).astype(low),
+        ]
+    )
+    grad_mixed_one = split_heads(to_absolute(grad_mixed_one, own_id), FRAMES)
     grad_sq, grad_sk, grad_sv = self_backward(
         queries, all_keys, all_values, peak_list, sum_list, grad_mixed_one
     )
-    grad_sq = merge_heads(grad_sq)
-    grad_sk = merge_heads(grad_sk)
-    grad_sv = merge_heads(grad_sv)
-    w_q_part = contract_rows(rows_one, grad_sq)
-    w_k_part = contract_rows(rows_one, grad_sk)
-    w_v_part = contract_rows(rows_one, grad_sv)
-    grad_normed_one = sum_inputs((grad_sq, grad_sk, grad_sv), (w_q, w_k, w_v))
+    grad_qkv = jnp.concatenate([merge_heads(part) for part in (grad_sq, grad_sk, grad_sv)], axis=1)
+    grad_qkv = to_absolute(grad_qkv, own_id)
+    grad_normed_one = scatter_product(
+        lambda: contract_cols(grad_qkv[2 * own_rows :], w_qkv),
+        lambda: contract_cols(grad_qkv[: 2 * own_rows], w_qkv),
+        own_rows,
+    )
+    qkv_grad = sum_clips(contract_rows(rows_one, grad_qkv))
+    w_q_grad, w_k_grad, w_v_grad = jnp.split(qkv_grad, 3, axis=1)
     norm_value, norm_back = jax.vjp(layer_norm, stream, ln1_gain, ln1_bias)
     back_rows, ln1_gain_part, ln1_bias_part = norm_back(grad_normed_one)
-    input_grad = (grad_one + back_rows).astype(jnp.bfloat16)
-    (
-        w_q_grad,
-        w_k_grad,
-        w_v_grad,
-        w_o_grad,
-        c_q_grad,
-        c_k_grad,
-        c_v_grad,
-        c_o_grad,
-        w_in_grad,
-        w_out_grad,
-    ) = (
-        lax.psum_scatter(w_q_part, "dp", scatter_dimension=0, tiled=True),
-        lax.psum_scatter(w_k_part, "dp", scatter_dimension=0, tiled=True),
-        lax.psum_scatter(w_v_part, "dp", scatter_dimension=0, tiled=True),
-        lax.psum_scatter(w_o_part, "dp", scatter_dimension=1, tiled=True),
-        lax.psum_scatter(c_q_part, "dp", scatter_dimension=0, tiled=True),
-        lax.psum_scatter(c_k_part, "dp", scatter_dimension=0, tiled=True),
-        lax.psum_scatter(c_v_part, "dp", scatter_dimension=0, tiled=True),
-        lax.psum_scatter(c_o_part, "dp", scatter_dimension=1, tiled=True),
-        lax.psum_scatter(w_in_part, "dp", scatter_dimension=0, tiled=True),
-        lax.psum_scatter(w_out_part, "dp", scatter_dimension=1, tiled=True),
-    )
-    ln1_gain_grad, ln1_bias_grad, ln2_gain_grad, ln2_bias_grad, ln3_gain_grad, ln3_bias_grad = (
-        lax.psum(
-            (
-                ln1_gain_part,
-                ln1_bias_part,
-                ln2_gain_part,
-                ln2_bias_part,
-                ln3_gain_part,
-                ln3_bias_part,
-            ),
-            ("dp", "tensor"),
-        )
-    )
-    entry_count = layer_input.shape[0] * lax.axis_size("dp") * lax.axis_size("tensor") * model_width
+    input_grad = (grad_one + back_rows).astype(low)
+
+    def columns(matrix):
+        return [matrix[:, i * local_width : (i + 1) * local_width] for i in range(4)]
+
+    rows_two = jnp.concatenate(gather_relative(after(normed_two, one_grads[2])))
+    grad_two_rows = jnp.concatenate(gather_relative(after(grad_two_low, one_grads[2])))
+    crossed_rows = jnp.concatenate(swap_relative(columns(after(crossed, one_grads[2]))))
+    grad_cq_rows = jnp.concatenate(swap_relative(columns(after(grad_cq, one_grads[2]))))
+    grad_text = jnp.concatenate(
+        [part.reshape(text_len, -1) for part in (grad_tk, grad_tv)]
+    ).astype(jnp.float32)
+    grad_text = scatter_relative(*columns(grad_text)).astype(low)
+    grad_tk, grad_tv = grad_text[:text_len], grad_text[text_len:]
+    cross_grad = sum_clips(
+        jnp.concatenate(
+            [
+                contract_rows(grad_two_rows, crossed_rows).astype(low),
+                contract_rows(rows_two, grad_cq_rows).astype(low),
+                contract_rows(text_rows, grad_tk).astype(low),
+                contract_rows(text_rows, grad_tv).astype(low),
+                contract_rows(grad_one_rows, attended).astype(low),
+            ],
+            axis=1,
+        )
+    )
+    c_o_grad, c_q_grad, c_k_grad, c_v_grad, w_o_grad = jnp.split(cross_grad, 5, axis=1)
+    c_o_grad, w_o_grad = c_o_grad.T, w_o_grad.T
+    text_term = (contract_cols(grad_tk, c_k) + contract_cols(grad_tv, c_v)).astype(low)
+    text_states_grad = (
+        scatter_relative(
+            *[
+                lax.dynamic_slice_in_dim(text_term, (own_id ^ flip) * local_width, local_width, 1)
+                for flip in range(4)
+            ]
+        )
+        .astype(low)
+        .reshape(clip_count, text_len, local_width)
+    )
+
+    early = sum_everywhere(
+        jnp.concatenate(
+            [ln3_gain_part, ln3_bias_part, ln2_gain_part, ln2_bias_part, jnp.pad(squares, (0, 124))]
+        )
+    )
+    late = sum_everywhere(jnp.concatenate([ln1_gain_part, ln1_bias_part]))
+    ln3_gain_grad, ln3_bias_grad, ln2_gain_grad, ln2_bias_grad = [
+        early[i * model_width : (i + 1) * model_width] for i in range(4)
+    ]
+    ln1_gain_grad, ln1_bias_grad = late[:model_width], late[model_width:]
+    square_totals = early[4 * model_width : 4 * model_width + 4]
+    entry_count = own_rows * lax.axis_size("dp") * lax.axis_size("tensor") * model_width
     root_squares = jnp.sqrt(square_totals / entry_count)
     return (
         block_out,

time: 1520 us -> 745 us (0.49)
  waiting for transfers between devices: 1150 us -> 307 us
  starting transfers between devices: 12.8 us -> 86.2 us
  local copies, waits for them, and re-layouts: 24.4 us -> 69 us
  blocking collectives: 41.6 us -> 0 us
    reduce_scatter x14 -> x0, waiting for transfers between devices: 851 us -> none  [the longest x1 165 us: body(): lax.psum_scatter(w_in_part, 'dp', scatter_dimension=0, tiled=True)]
    ppermute x0 -> x89, waiting for transfers between devices: none -> 307 us  [the longest x24 91.3 us: sum_clips(): carried = lax.ppermute(block, 'dp', pairs)]
    all_gather x6 -> x0, waiting for transfers between devices: 150 us -> none  [the longest x3 81.1 us: gather_normed(): return lax.all_gather(values, 'tensor', axis=0, tiled=True)]
    unnamed x26 -> x0, waiting for transfers between devices: 146 us -> none
    ppermute x0 -> x89, starting transfers between devices: none -> 86.2 us  [the longest x24 49.2 us: sum_clips(): carried = lax.ppermute(block, 'dp', pairs)]
    psum x1 -> x0, blocking collectives: 41.6 us -> none  [body(): lax.psum((ln1_gain_part, ln1_bias_part, ln2_gain_part, ln2_bias_part, ln3...]
    dot_general x10 -> x12, matrix products: 40.9 us -> 63.8 us  [product(): return jnp.dot(left_mat, right_mat, preferred_element_type=jnp.float32)]
    dot_general x10 -> x8, matrix products: 55.3 us -> 34.3 us  [contract_rows(): lax.dot_general(left_mat, right_mat, (((0,), (0,)), ((), ())), preferred_...]
  transfers between devices with their start and end apart: 23 -> 89, of which waited for: 20 -> 29; matrix products, arithmetic and copies ran while one was open for 10% -> 41% of each run, Pallas kernels for 0% -> 0%
where the time goes in v1:
time: 745 us; the launch traced here: 735 us
  waiting for transfers between devices  307 us (41%)
  matrix products  186 us (25%)
  starting transfers between devices  86.2 us (12%)
  other arithmetic  82.5 us (11%)
  local copies, waits for them, and re-layouts  69 us (9%)
    ppermute x24, waiting for transfers between devices, sum_clips(): carried = lax.ppermute(block, 'dp', pairs)  91.3 us
    ppermute x6, waiting for transfers between devices, sum_everywhere(): lax.ppermute(values, 'dp', [(i, i ^ flip) for i in range(8)])  77.2 us
    ppermute x4, waiting for transfers between devices, sum_clips(): kept = kept + lax.ppermute(sent, 'dp', [(i, i ^ 1) for i in range(8)])  69.6 us
    ppermute x55, waiting for transfers between devices, exchange(): return lax.ppermute(values, 'tensor', [(i, i ^ flip) for i in range(4)])  69.4 us
    dot_general x12, matrix products, product(): return jnp.dot(left_mat, right_mat, preferred_element_type=jnp.float32)  63.8 us
    ppermute x24, starting transfers between devices, sum_clips(): carried = lax.ppermute(block, 'dp', pairs)  49.2 us
    dot_general x12, matrix products, contract_cols(): lax.dot_general(left_mat, right_mat, (((1,), (1,)), ((), ())), preferred_...  34.4 us
    dot_general x8, matrix products, contract_rows(): lax.dot_general(left_mat, right_mat, (((0,), (0,)), ((), ())), preferred_...  34.3 us
  transfers between devices with their start and end apart: 89, of which 29 were waited for; matrix products, arithmetic and copies ran while one was open for 41% of the time, Pallas kernels for 0%

profile of v1, /device:TPU:8, one launch (start us, length us, event | category | flops | bytes accessed | tf_op | source)
XLA Modules:
  0.0 734.6 jit_solution(9524210146126379123)
XLA Ops:
  16.8 10.1 %collective-permute-done.1 = bf16[256,1536]{1,0:T(8,128)(2,1)} collective-permute-done((bf16[256,1536]{1,0:T(8,128)(2,1)}, bf16[256,1536]{1,0:T(8,128)(2,1)}, u32[]{:S(2)}, u32[]{:S(2)}) %collective-permute-start.1) | collective-permute-done | bytes 786464 | tf_op jit(solution)/shard_map/ppermute | solution.py:39
  29.2 2.5 constant_dynamic-update-slice_fusion.10
  31.7 3.6 convolution_convert_fusion.5
  38.4 2.7 collective-permute-done.8
  44.2 3.4 convolution_convert_fusion.4
  47.6 3.1 fusion.231
  52.9 6.8 fusion.245
  59.6 16.8 %fusion.317 = (f32[6,512]{1,0:T(8,128)S(1)}, f32[6,512,1024]{2,1,0:T(8,128)}) fusion(f32[6,512,1024]{2,1,0:T(8,128)} %fusion.245, pred[512,1024]{1,0:T(8,128)(4,1)S(1)} %copy-done.58), kind=kOutput, calls=%fused_computation.500 | output fusion | flops 18875392 | bytes 25702400 | tf_op jit(solution)/shard_map/sub | solution.py:133
  76.4 6.6 fusion.318
  83.1 6.8 fusion.187
  97.0 2.7 constant_dynamic-update-slice_fusion.9
  101.5 2.5 constant_dynamic-update-slice_fusion.8
  106.4 2.5 constant_dynamic-update-slice_fusion.12
  109.0 11.5 %collective-permute-done.5 = bf16[256,1536]{1,0:T(8,128)(2,1)S(1)} collective-permute-done((bf16[256,1536]{1,0:T(8,128)(2,1)S(1)}, bf16[256,1536]{1,0:T(8,128)(2,1)S(1)}, u32[]{:S(2)}, u32[]{:S(2)}) %collective-permute-start.5) | collective-permute-done | bytes 786464 | tf_op jit(solution)/shard_map/ppermute | solution.py:39
  126.0 2.5 convolution_convert_fusion.12
  133.0 2.7 constant_dynamic-update-slice_fusion.11
  135.6 15.9 %fusion.308 = (f32[256]{0:T(256)S(1)}, f32[256,1536]{1,0:T(8,128)S(1)}, f32[]{:T(128)}) fusion(f32[256,1536]{1,0:T(8,128)S(1)} %copy-done.6, bf16[256,1536]{0,1:T(8,128)(2,1)S(1)} %bitcast.312, bf16[1536,1536]{1,0:T(8,128)(2,1)} %constant_dynamic-update-slice_fusion.11), kind=kOutput, calls=%fused_computation.491 | convolution fusion | flops 1209532160 | bytes 8651780 | tf_op jit(solution)/shard_map/dot_general | solution.py:23
  156.2 18.5 %collective-permute-done.17 = bf16[256,1536]{1,0:T(8,128)(2,1)} collective-permute-done((bf16[256,1536]{1,0:T(8,128)(2,1)}, bf16[256,1536]{1,0:T(8,128)(2,1)}, u32[]{:S(2)}, u32[]{:S(2)}) %collective-permute-start.17) | collective-permute-done | bytes 786464 | tf_op jit(solution)/shard_map/ppermute | solution.py:39
  174.6 11.0 %multiply_convert_fusion.3 = (bf16[512,1536]{1,0:T(8,128)(2,1)S(1)}, f32[512,1536]{1,0:T(8,128)S(1)}, f32[512,1536]{1,0:T(8,128)S(1)}) fusion(bf16[1536,1536]{1,0:T(8,128)(2,1)} %param.47, bf16[256,1536]{1,0:T(8,128)(2,1)} %collective-permute-done.15, bf16[256,1536]{1,0:T(8,128)(2,1)} %add_convert_fusion.4), kind=kOutput, calls=%fused_computation.98 | convolution fusion | flops 2470182912 | bytes 14155776 | tf_op jit(solution)/shard_map/dot_general | solution.py:23
  185.7 6.6 add_convert_fusion.1
  192.3 4.8 fusion.321
  198.7 4.5 fusion.320
  204.8 12.2 %multiply_convert_fusion.2 = (bf16[512,1536]{1,0:T(8,128)(2,1)}, f32[512,1536]{1,0:T(8,128)S(1)}, f32[512,1536]{1,0:T(8,128)}) fusion(bf16[1536,1536]{1,0:T(8,128)(2,1)S(1)} %bitcast.325, bf16[256,1536]{1,0:T(8,128)(2,1)S(1)} %collective-permute-done.18, bf16[256,1536]{1,0:T(8,128)(2,1)} %collective-permute-done.17), kind=kOutput, calls=%fused_computation.85 | convolution fusion | flops 2470182912 | bytes 14155776 | tf_op jit(solution)/shard_map/dot_general | solution.py:23
  217.9 5.3 add_convert_fusion
  223.2 2.6 convolution_convert_fusion.7
  226.2 6.8 convolution_convert_fusion.1
  236.2 7.7 %convolution_convert_fusion = bf16[1536,1536]{1,0:T(8,128)(2,1)S(1)} fusion(bf16[256,1536]{1,0:T(8,128)(2,1)} %copy-done.116, bf16[256,1536]{1,0:T(8,128)(2,1)} %copy-done.114, bf16[256,1536]{1,0:T(8,128)(2,1)} %copy-done.115, bf16[256,1536]{1,0:T(8,128)(2,1)S(1)} %copy-done.17, bf16[512,1536]{1,0:T(8,128)(2,1)} %get-tuple-element.97, ...), kind=kOutput, calls=%fused_computation.8 | convolution fusion | flops 4853071872 | bytes 11010048 | tf_op jit(solution)/shard_map/dot_general | solution.py:27
  244.7 10.6 %collective-permute-done.24 = bf16[256,1536]{1,0:T(8,128)(2,1)S(1)} collective-permute-done((bf16[256,1536]{1,0:T(8,128)(2,1)}, bf16[256,1536]{1,0:T(8,128)(2,1)S(1)}, u32[]{:S(2)}, u32[]{:S(2)}) %collective-permute-start.24) | collective-permute-done | bytes 786464 | tf_op jit(solution)/shard_map/ppermute | solution.py:39
  257.5 4.9 convolution_convert_fusion.6
  265.2 22.1 %collective-permute-done.75 = bf16[4,192,1536]{2,1,0:T(8,128)(2,1)S(1)} collective-permute-done((bf16[4,192,1536]{2,1,0:T(8,128)(2,1)S(1)}, bf16[4,192,1536]{2,1,0:T(8,128)(2,1)S(1)}, u32[]{:S(2)}, u32[]{:S(2)}) %collective-permute-start.75) | collective-permute-done | bytes 2359328 | tf_op jit(solution)/shard_map/ppermute | solution.py:84
  289.8 47.4 %collective-permute-done.82 = bf16[4,192,1536]{2,1,0:T(8,128)(2,1)S(1)} collective-permute-done((bf16[4,192,1536]{2,1,0:T(8,128)(2,1)S(1)}, bf16[4,192,1536]{2,1,0:T(8,128)(2,1)S(1)}, u32[]{:S(2)}, u32[]{:S(2)}) %collective-permute-start.82) | collective-permute-done | bytes 2359328 | tf_op jit(solution)/shard_map/ppermute | solution.py:84
  344.7 10.7 %collective-permute-done.83 = bf16[192,1536]{1,0:T(8,128)(2,1)S(1)} collective-permute-done((bf16[192,1536]{1,0:T(8,128)(2,1)S(1)}, bf16[192,1536]{1,0:T(8,128)(2,1)S(1)}, u32[]{:S(2)}, u32[]{:S(2)}) %collective-permute-start.83) | collective-permute-done | bytes 589856 | tf_op jit(solution)/shard_map/ppermute | solution.py:95
  359.1 2.4 multiply_reduce_fusion.2
  362.7 3.4 convolution_convert_fusion.11
  374.3 4.1 multiply_reduce_fusion.5
  384.5 3.1 collective-permute-start.84
  394.2 7.4 %collective-permute-done.84 = bf16[192,1536]{1,0:T(8,128)(2,1)S(1)} collective-permute-done((bf16[192,1536]{1,0:T(8,128)(2,1)S(1)}, bf16[192,1536]{1,0:T(8,128)(2,1)S(1)}, u32[]{:S(2)}, u32[]{:S(2)}) %collective-permute-start.84) | collective-permute-done | bytes 589856 | tf_op jit(solution)/shard_map/ppermute | solution.py:95
  404.8 5.4 collective-permute-done.38
  423.6 5.0 fusion.169
  428.6 6.7 multiply_reduce_fusion.1
  435.3 5.9 multiply_reduce_fusion
  441.2 6.3 multiply_convert_fusion.1
  452.2 6.3 multiply_convert_fusion
  466.8 6.0 convolution_convert_fusion.2
  478.6 4.6 collective-permute-done.55
  487.9 4.4 fusion.87
  492.9 2.6 collective-permute-start.78
  498.7 4.2 collective-permute-start.81
  504.6 3.9 fusion.90
  514.0 8.6 %copy.79 = bf16[1536,1920]{1,0:T(8,128)(2,1)} copy(bf16[1536,1920]{0,1:T(8,128)(2,1)} %fusion.93) | data formatting | bytes 11796480 | tf_op jit(solution)/shard_map/concatenate | solution.py:405
  534.1 4.2 collective-permute-start.88
  539.0 2.6 constant_dynamic-update-slice_fusion.17
  542.1 2.6 fusion.204
  546.3 3.4 collective-permute-done.85
  554.0 75.1 %collective-permute-done.41 = f32[3072]{0:T(1024)S(1)} collective-permute-done((f32[3072]{0:T(1024)S(1)}, f32[3072]{0:T(1024)S(1)}, u32[]{:S(2)}, u32[]{:S(2)}) %collective-permute-start.41) | collective-permute-done | bytes 12320 | tf_op jit(solution)/shard_map/ppermute | solution.py:106
  642.7 7.8 %collective-permute-done.45 = bf16[192,1152]{1,0:T(8,128)(2,1)S(1)} collective-permute-done((bf16[192,1152]{1,0:T(8,128)(2,1)S(1)}, bf16[192,1152]{1,0:T(8,128)(2,1)S(1)}, u32[]{:S(2)}, u32[]{:S(2)}) %collective-permute-start.45) | collective-permute-done | bytes 442400 | tf_op jit(solution)/shard_map/ppermute | solution.py:95
  653.2 13.1 %collective-permute-done.64 = bf16[192,1920]{1,0:T(8,128)(2,1)S(1)} collective-permute-done((bf16[192,1920]{1,0:T(8,128)(2,1)S(1)}, bf16[192,1920]{1,0:T(8,128)(2,1)S(1)}, u32[]{:S(2)}, u32[]{:S(2)}) %collective-permute-start.64) | collective-permute-done | bytes 737312 | tf_op jit(solution)/shard_map/ppermute | solution.py:95
  669.0 7.4 %collective-permute-done.46 = bf16[192,1152]{1,0:T(8,128)(2,1)S(1)} collective-permute-done((bf16[192,1152]{1,0:T(8,128)(2,1)S(1)}, bf16[192,1152]{1,0:T(8,128)(2,1)S(1)}, u32[]{:S(2)}, u32[]{:S(2)}) %collective-permute-start.46) | collective-permute-done | bytes 442400 | tf_op jit(solution)/shard_map/ppermute | solution.py:95
  677.8 11.9 %collective-permute-done.65 = bf16[192,1920]{1,0:T(8,128)(2,1)S(1)} collective-permute-done((bf16[192,1920]{1,0:T(8,128)(2,1)S(1)}, bf16[192,1920]{1,0:T(8,128)(2,1)S(1)}, u32[]{:S(2)}, u32[]{:S(2)}) %collective-permute-start.65) | collective-permute-done | bytes 737312 | tf_op jit(solution)/shard_map/ppermute | solution.py:95
  692.3 4.5 collective-permute-start.47
  698.8 3.9 collective-permute-start.66
  702.7 8.3 %collective-permute-done.68 = bf16[192,1920]{1,0:T(8,128)(2,1)S(1)} collective-permute-done((bf16[192,1920]{1,0:T(8,128)(2,1)S(1)}, bf16[192,1920]{1,0:T(8,128)(2,1)S(1)}, u32[]{:S(2)}, u32[]{:S(2)}) %collective-permute-start.68) | collective-permute-done | bytes 737312 | tf_op jit(solution)/shard_map/ppermute | solution.py:95
  713.1 7.5 %collective-permute-done.50 = bf16[192,1152]{1,0:T(8,128)(2,1)S(1)} collective-permute-done((bf16[192,1152]{1,0:T(8,128)(2,1)S(1)}, bf16[192,1152]{1,0:T(8,128)(2,1)S(1)}, u32[]{:S(2)}, u32[]{:S(2)}) %collective-permute-start.50) | collective-permute-done | bytes 442400 | tf_op jit(solution)/shard_map/ppermute | solution.py:95
  721.7 11.3 %collective-permute-done.69 = bf16[192,1920]{1,0:T(8,128)(2,1)S(1)} collective-permute-done((bf16[192,1920]{1,0:T(8,128)(2,1)S(1)}, bf16[192,1920]{1,0:T(8,128)(2,1)S(1)}, u32[]{:S(2)}, u32[]{:S(2)}) %collective-permute-start.69) | collective-permute-done | bytes 737312 | tf_op jit(solution)/shard_map/ppermute | solution.py:95
  (577 shorter events, 198.9 us)
Async XLA Ops:
  6.7 25.0 %collective-permute-start = (bf16[256,1536]{1,0:T(8,128)(2,1)}, bf16[256,1536]{1,0:T(8,128)(2,1)}, u32[]{:S(2)}, u32[]{:S(2)}) collective-permute-start(bf16[256,1536]{1,0:T(8,128)(2,1)} %fusion.116), channel_id=1, source_target_pairs={{0,1},{1,0},{2,3},{3,2},{4,5},{5,4},{6,7},{7,6},{8,9},{9,8},{10,11... | collective-permute-start | bytes 2359304 | tf_op jit(solution)/shard_map/ppermute | solution.py:39
  6.7 20.3 %collective-permute-start.1 = (bf16[256,1536]{1,0:T(8,128)(2,1)}, bf16[256,1536]{1,0:T(8,128)(2,1)}, u32[]{:S(2)}, u32[]{:S(2)}) collective-permute-start(bf16[256,1536]{1,0:T(8,128)(2,1)} %fusion.116), channel_id=1, source_target_pairs={{0,2},{1,3},{2,0},{3,1},{4,6},{5,7},{6,4},{7,5},{8,10},{9,11},{10,... | collective-permute-start | bytes 2359304 | tf_op jit(solution)/shard_map/ppermute | solution.py:39
  28.4 67.6 %collective-permute-start.9 = (bf16[1536,384]{1,0:T(8,128)(2,1)}, bf16[1536,384]{1,0:T(8,128)(2,1)}, u32[]{:S(2)}, u32[]{:S(2)}) collective-permute-start(bf16[1536,384]{1,0:T(8,128)(2,1)} %param.41), channel_id=1, source_target_pairs={{0,1},{1,0},{2,3},{3,2},{4,5},{5,4},{6,7},{7,6},{8,9},{9,8},{10,11... | collective-permute-start | bytes 3538952 | tf_op jit(solution)/shard_map/ppermute | solution.py:39
  28.6 67.9 %collective-permute-start.10 = (bf16[1536,384]{1,0:T(8,128)(2,1)}, bf16[1536,384]{1,0:T(8,128)(2,1)}, u32[]{:S(2)}, u32[]{:S(2)}) collective-permute-start(bf16[1536,384]{1,0:T(8,128)(2,1)} %param.41), channel_id=1, source_target_pairs={{0,2},{1,3},{2,0},{3,1},{4,6},{5,7},{6,4},{7,5},{8,10},{9,11},{10,... | collective-permute-start | bytes 3538952 | tf_op jit(solution)/shard_map/ppermute | solution.py:39
  37.7 66.4 %collective-permute-start.12 = (bf16[384,1536]{1,0:T(8,128)(2,1)}, bf16[384,1536]{1,0:T(8,128)(2,1)}, u32[]{:S(2)}, u32[]{:S(2)}) collective-permute-start(bf16[384,1536]{1,0:T(8,128)(2,1)} %param.44), channel_id=1, source_target_pairs={{0,1},{1,0},{2,3},{3,2},{4,5},{5,4},{6,7},{7,6},{8,9},{9,8},{10,11... | collective-permute-start | bytes 3538952 | tf_op jit(solution)/shard_map/ppermute | solution.py:39
  41.1 55.5 %collective-permute-start.13 = (bf16[384,1536]{1,0:T(8,128)(2,1)}, bf16[384,1536]{1,0:T(8,128)(2,1)}, u32[]{:S(2)}, u32[]{:S(2)}) collective-permute-start(bf16[384,1536]{1,0:T(8,128)(2,1)} %param.44), channel_id=1, source_target_pairs={{0,2},{1,3},{2,0},{3,1},{4,6},{5,7},{6,4},{7,5},{8,10},{9,11},{10,... | collective-permute-start | bytes 3538952 | tf_op jit(solution)/shard_map/ppermute | solution.py:39
  96.0 12.9 %collective-permute-start.3 = (bf16[256,1536]{1,0:T(8,128)(2,1)S(1)}, bf16[256,1536]{1,0:T(8,128)(2,1)S(1)}, u32[]{:S(2)}, u32[]{:S(2)}) collective-permute-start(bf16[256,1536]{1,0:T(8,128)(2,1)S(1)} %slice.449), channel_id=1, source_target_pairs={{0,1},{1,0},{2,3},{3,2},{4,5},{5,4},{6,7},{7,6},{8,9},{9,8},{10,11... | collective-permute-start | bytes 2359304 | tf_op jit(solution)/shard_map/ppermute | solution.py:39
  96.5 27.0 %collective-permute-start.11 = (bf16[1536,384]{1,0:T(8,128)(2,1)}, bf16[1536,384]{1,0:T(8,128)(2,1)S(1)}, u32[]{:S(2)}, u32[]{:S(2)}) collective-permute-start(bf16[1536,384]{1,0:T(8,128)(2,1)} %collective-permute-done.10), channel_id=1, source_target_pairs={{0,1},{1,0},{2,3},{3,2},{4,5},{5,4},{6,7},{7,6},{8,9},{9,8},{10,11... | collective-permute-start | bytes 3538952 | tf_op jit(solution)/shard_map/ppermute | solution.py:39
  96.6 36.3 %collective-permute-start.14 = (bf16[384,1536]{1,0:T(8,128)(2,1)}, bf16[384,1536]{1,0:T(8,128)(2,1)}, u32[]{:S(2)}, u32[]{:S(2)}) collective-permute-start(bf16[384,1536]{1,0:T(8,128)(2,1)} %collective-permute-done.13), channel_id=1, source_target_pairs={{0,1},{1,0},{2,3},{3,2},{4,5},{5,4},{6,7},{7,6},{8,9},{9,8},{10,11... | collective-permute-start | bytes 3538952 | tf_op jit(solution)/shard_map/ppermute | solution.py:39
  100.9 19.6 %collective-permute-start.5 = (bf16[256,1536]{1,0:T(8,128)(2,1)S(1)}, bf16[256,1536]{1,0:T(8,128)(2,1)S(1)}, u32[]{:S(2)}, u32[]{:S(2)}) collective-permute-start(bf16[256,1536]{1,0:T(8,128)(2,1)S(1)} %slice_add_fusion.7), channel_id=1, source_target_pairs={{0,2},{1,3},{2,0},{3,1},{4,6},{5,7},{6,4},{7,5},{8,10},{9,11},{10,... | collective-permute-start | bytes 2359304 | tf_op jit(solution)/shard_map/ppermute | solution.py:39
  153.9 20.7 %collective-permute-start.17 = (bf16[256,1536]{1,0:T(8,128)(2,1)}, bf16[256,1536]{1,0:T(8,128)(2,1)}, u32[]{:S(2)}, u32[]{:S(2)}) collective-permute-start(bf16[256,1536]{1,0:T(8,128)(2,1)} %add_convert_fusion.4), channel_id=1, source_target_pairs={{0,2},{1,3},{2,0},{3,1},{4,6},{5,7},{6,4},{7,5},{8,10},{9,11},{10,... | collective-permute-start | bytes 2359304 | tf_op jit(solution)/shard_map/ppermute | solution.py:39
  154.4 20.2 %collective-permute-start.15 = (bf16[256,1536]{1,0:T(8,128)(2,1)}, bf16[256,1536]{1,0:T(8,128)(2,1)}, u32[]{:S(2)}, u32[]{:S(2)}) collective-permute-start(bf16[256,1536]{1,0:T(8,128)(2,1)} %add_convert_fusion.4), channel_id=1, source_target_pairs={{0,1},{1,0},{2,3},{3,2},{4,5},{5,4},{6,7},{7,6},{8,9},{9,8},{10,11... | collective-permute-start | bytes 2359304 | tf_op jit(solution)/shard_map/ppermute | solution.py:39
  154.5 50.0 %collective-permute-start.21 = (bf16[256,1536]{1,0:T(8,128)(2,1)}, bf16[256,1536]{1,0:T(8,128)(2,1)S(1)}, u32[]{:S(2)}, u32[]{:S(2)}) collective-permute-start(bf16[256,1536]{1,0:T(8,128)(2,1)} %param.49), channel_id=1, source_target_pairs={{0,2},{1,3},{2,0},{3,1},{4,6},{5,7},{6,4},{7,5},{8,10},{9,11},{10,... | collective-permute-start | bytes 2359304 | tf_op jit(solution)/shard_map/ppermute | solution.py:39
  155.9 29.7 %collective-permute-start.19 = (bf16[256,1536]{1,0:T(8,128)(2,1)}, bf16[256,1536]{1,0:T(8,128)(2,1)S(1)}, u32[]{:S(2)}, u32[]{:S(2)}) collective-permute-start(bf16[256,1536]{1,0:T(8,128)(2,1)} %param.49), channel_id=1, source_target_pairs={{0,1},{1,0},{2,3},{3,2},{4,5},{5,4},{6,7},{7,6},{8,9},{9,8},{10,11... | collective-permute-start | bytes 2359304 | tf_op jit(solution)/shard_map/ppermute | solution.py:39
  174.6 30.2 %collective-permute-start.18 = (bf16[256,1536]{1,0:T(8,128)(2,1)}, bf16[256,1536]{1,0:T(8,128)(2,1)S(1)}, u32[]{:S(2)}, u32[]{:S(2)}) collective-permute-start(bf16[256,1536]{1,0:T(8,128)(2,1)} %collective-permute-done.17), channel_id=1, source_target_pairs={{0,1},{1,0},{2,3},{3,2},{4,5},{5,4},{6,7},{7,6},{8,9},{9,8},{10,11... | collective-permute-start | bytes 2359304 | tf_op jit(solution)/shard_map/ppermute | solution.py:39
  198.2 46.6 %collective-permute-start.20 = (bf16[256,1536]{1,0:T(8,128)(2,1)}, bf16[256,1536]{1,0:T(8,128)(2,1)}, u32[]{:S(2)}, u32[]{:S(2)}) collective-permute-start(bf16[256,1536]{1,0:T(8,128)(2,1)} %slice.447), channel_id=1, source_target_pairs={{0,1},{1,0},{2,3},{3,2},{4,5},{5,4},{6,7},{7,6},{8,9},{9,8},{10,11... | collective-permute-start | bytes 2359304 | tf_op jit(solution)/shard_map/ppermute | solution.py:39
  204.3 153.9 %collective-permute-start.16 = (bf16[256,1536]{1,0:T(8,128)(2,1)}, bf16[256,1536]{1,0:T(8,128)(2,1)S(1)}, u32[]{:S(2)}, u32[]{:S(2)}) collective-permute-start(bf16[256,1536]{1,0:T(8,128)(2,1)} %slice.448), channel_id=1, source_target_pairs={{0,1},{1,0},{2,3},{3,2},{4,5},{5,4},{6,7},{7,6},{8,9},{9,8},{10,11... | collective-permute-start | bytes 2359304 | tf_op jit(solution)/shard_map/ppermute | solution.py:39
  204.4 12.5 %collective-permute-start.22 = (bf16[256,1536]{1,0:T(8,128)(2,1)S(1)}, bf16[256,1536]{1,0:T(8,128)(2,1)S(1)}, u32[]{:S(2)}, u32[]{:S(2)}) collective-permute-start(bf16[256,1536]{1,0:T(8,128)(2,1)S(1)} %collective-permute-done.21), channel_id=1, source_target_pairs={{0,1},{1,0},{2,3},{3,2},{4,5},{5,4},{6,7},{7,6},{8,9},{9,8},{10,11... | collective-permute-start | bytes 2359304 | tf_op jit(solution)/shard_map/ppermute | solution.py:39
  233.1 54.2 %collective-permute-start.75 = (bf16[4,192,1536]{2,1,0:T(8,128)(2,1)S(1)}, bf16[4,192,1536]{2,1,0:T(8,128)(2,1)S(1)}, u32[]{:S(2)}, u32[]{:S(2)}) collective-permute-start(bf16[4,192,1536]{2,1,0:T(8,128)(2,1)S(1)} %dynamic-slice_bitcast_fusion.2), channel_id=1, source_target_pairs={{0,4},{4,0},{8,12},{12,8},{16,20},{20,16},{24,28},{28,24},{1,5},{5... | collective-permute-start | bytes 7077896 | tf_op jit(solution)/shard_map/ppermute | solution.py:84
  235.7 19.7 %collective-permute-start.24 = (bf16[256,1536]{1,0:T(8,128)(2,1)}, bf16[256,1536]{1,0:T(8,128)(2,1)S(1)}, u32[]{:S(2)}, u32[]{:S(2)}) collective-permute-start(bf16[256,1536]{1,0:T(8,128)(2,1)} %slice_add_fusion.6), channel_id=1, source_target_pairs={{0,2},{1,3},{2,0},{3,1},{4,6},{5,7},{6,4},{7,5},{8,10},{9,11},{10,... | collective-permute-start | bytes 2359304 | tf_op jit(solution)/shard_map/ppermute | solution.py:39
  244.2 93.1 %collective-permute-start.82 = (bf16[4,192,1536]{2,1,0:T(8,128)(2,1)S(1)}, bf16[4,192,1536]{2,1,0:T(8,128)(2,1)S(1)}, u32[]{:S(2)}, u32[]{:S(2)}) collective-permute-start(bf16[4,192,1536]{2,1,0:T(8,128)(2,1)S(1)} %dynamic-slice_bitcast_fusion.1), channel_id=1, source_target_pairs={{0,4},{4,0},{8,12},{12,8},{16,20},{20,16},{24,28},{28,24},{1,5},{5... | collective-permute-start | bytes 7077896 | tf_op jit(solution)/shard_map/ppermute | solution.py:84
  262.5 77.6 %collective-permute-start.25 = (bf16[256,1536]{1,0:T(8,128)(2,1)S(1)}, bf16[256,1536]{1,0:T(8,128)(2,1)S(1)}, u32[]{:S(2)}, u32[]{:S(2)}) collective-permute-start(bf16[256,1536]{1,0:T(8,128)(2,1)S(1)} %slice.333), channel_id=1, source_target_pairs={{0,1},{1,0},{2,3},{3,2},{4,5},{5,4},{6,7},{7,6},{8,9},{9,8},{10,11... | collective-permute-start | bytes 2359304 | tf_op jit(solution)/shard_map/ppermute | solution.py:39
  288.5 53.7 %collective-permute-start.76 = (bf16[192,1536]{1,0:T(8,128)(2,1)S(1)}, bf16[192,1536]{1,0:T(8,128)(2,1)S(1)}, u32[]{:S(2)}, u32[]{:S(2)}) collective-permute-start(bf16[192,1536]{1,0:T(8,128)(2,1)S(1)} %get-tuple-element.140), channel_id=1, source_target_pairs={{0,8},{4,12},{1,9},{5,13},{2,10},{6,14},{3,11},{7,15}} | collective-permute-start | bytes 1769480 | tf_op jit(solution)/shard_map/ppermute | solution.py:95
  338.6 16.7 %collective-permute-start.83 = (bf16[192,1536]{1,0:T(8,128)(2,1)S(1)}, bf16[192,1536]{1,0:T(8,128)(2,1)S(1)}, u32[]{:S(2)}, u32[]{:S(2)}) collective-permute-start(bf16[192,1536]{1,0:T(8,128)(2,1)S(1)} %get-tuple-element.136), channel_id=1, source_target_pairs={{0,8},{4,12},{1,9},{5,13},{2,10},{6,14},{3,11},{7,15}} | collective-permute-start | bytes 1769480 | tf_op jit(solution)/shard_map/ppermute | solution.py:95
  340.2 19.0 %collective-permute-start.26 = (bf16[256,1536]{1,0:T(8,128)(2,1)S(1)}, bf16[256,1536]{1,0:T(8,128)(2,1)S(1)}, u32[]{:S(2)}, u32[]{:S(2)}) collective-permute-start(bf16[256,1536]{1,0:T(8,128)(2,1)S(1)} %slice_add_fusion.5), channel_id=1, source_target_pairs={{0,2},{1,3},{2,0},{3,1},{4,6},{5,7},{6,4},{7,5},{8,10},{9,11},{10,... | collective-permute-start | bytes 2359304 | tf_op jit(solution)/shard_map/ppermute | solution.py:39
  340.8 48.3 %collective-permute-start.79 = (bf16[192,1536]{1,0:T(8,128)(2,1)}, bf16[192,1536]{1,0:T(8,128)(2,1)}, u32[]{:S(2)}, u32[]{:S(2)}) collective-permute-start(bf16[192,1536]{1,0:T(8,128)(2,1)} %get-tuple-element.141), channel_id=1, source_target_pairs={{24,16},{28,20},{25,17},{29,21},{26,18},{30,22},{27,19},{31,23}} | collective-permute-start | bytes 1769480 | tf_op jit(solution)/shard_map/ppermute | solution.py:95
  342.3 50.6 %collective-permute-start.86 = (bf16[192,1536]{1,0:T(8,128)(2,1)}, bf16[192,1536]{1,0:T(8,128)(2,1)}, u32[]{:S(2)}, u32[]{:S(2)}) collective-permute-start(bf16[192,1536]{1,0:T(8,128)(2,1)} %get-tuple-element.137), channel_id=1, source_target_pairs={{24,16},{28,20},{25,17},{29,21},{26,18},{30,22},{27,19},{31,23}} | collective-permute-start | bytes 1769480 | tf_op jit(solution)/shard_map/ppermute | solution.py:95
  355.3 34.7 %collective-permute-start.77 = (bf16[192,1536]{1,0:T(8,128)(2,1)}, bf16[192,1536]{1,0:T(8,128)(2,1)}, u32[]{:S(2)}, u32[]{:S(2)}) collective-permute-start(bf16[192,1536]{1,0:T(8,128)(2,1)} %bitcast_add_fusion.16), channel_id=1, source_target_pairs={{0,8},{4,12},{8,16},{12,20},{1,9},{5,13},{9,17},{13,21},{2,10},{6,... | collective-permute-start | bytes 1769480 | tf_op jit(solution)/shard_map/ppermute | solution.py:95
  384.5 17.1 %collective-permute-start.84 = (bf16[192,1536]{1,0:T(8,128)(2,1)S(1)}, bf16[192,1536]{1,0:T(8,128)(2,1)S(1)}, u32[]{:S(2)}, u32[]{:S(2)}) collective-permute-start(bf16[192,1536]{1,0:T(8,128)(2,1)S(1)} %copy-done.57), channel_id=1, source_target_pairs={{0,8},{4,12},{8,16},{12,20},{1,9},{5,13},{9,17},{13,21},{2,10},{6,... | collective-permute-start | bytes 1769480 | tf_op jit(solution)/shard_map/ppermute | solution.py:95
  387.8 26.2 %collective-permute-start.27 = (bf16[256,1536]{1,0:T(8,128)(2,1)S(1)}, bf16[256,1536]{1,0:T(8,128)(2,1)S(1)}, u32[]{:S(2)}, u32[]{:S(2)}) collective-permute-start(bf16[256,1536]{1,0:T(8,128)(2,1)S(1)} %fusion.301), channel_id=1, source_target_pairs={{0,1},{1,0},{2,3},{3,2},{4,5},{5,4},{6,7},{7,6},{8,9},{9,8},{10,11... | collective-permute-start | bytes 2359304 | tf_op jit(solution)/shard_map/ppermute | solution.py:39
  389.1 21.7 %collective-permute-start.28 = (bf16[256,1536]{1,0:T(8,128)(2,1)S(1)}, bf16[256,1536]{1,0:T(8,128)(2,1)S(1)}, u32[]{:S(2)}, u32[]{:S(2)}) collective-permute-start(bf16[256,1536]{1,0:T(8,128)(2,1)S(1)} %fusion.301), channel_id=1, source_target_pairs={{0,2},{1,3},{2,0},{3,1},{4,6},{5,7},{6,4},{7,5},{8,10},{9,11},{10,... | collective-permute-start | bytes 2359304 | tf_op jit(solution)/shard_map/ppermute | solution.py:39
  392.6 12.3 %collective-permute-start.36 = (bf16[64,384]{1,0:T(8,128)(2,1)S(1)}, bf16[64,384]{1,0:T(8,128)(2,1)S(1)}, u32[]{:S(2)}, u32[]{:S(2)}) collective-permute-start(bf16[64,384]{1,0:T(8,128)(2,1)S(1)} %get-tuple-element.188), channel_id=1, source_target_pairs={{0,1},{1,0},{2,3},{3,2},{4,5},{5,4},{6,7},{7,6},{8,9},{9,8},{10,11... | collective-permute-start | bytes 147464 | tf_op jit(solution)/shard_map/ppermute | solution.py:39
  392.9 22.9 %collective-permute-start.80 = (bf16[192,1536]{1,0:T(8,128)(2,1)S(1)}, bf16[192,1536]{1,0:T(8,128)(2,1)S(1)}, u32[]{:S(2)}, u32[]{:S(2)}) collective-permute-start(bf16[192,1536]{1,0:T(8,128)(2,1)S(1)} %get-tuple-element.139), channel_id=1, source_target_pairs={{24,16},{28,20},{16,8},{20,12},{25,17},{29,21},{17,9},{21,13},{26,... | collective-permute-start | bytes 1769480 | tf_op jit(solution)/shard_map/ppermute | solution.py:95
  410.8 66.4 %collective-permute-start.52 = (bf16[256,1536]{1,0:T(8,128)(2,1)}, bf16[256,1536]{1,0:T(8,128)(2,1)}, u32[]{:S(2)}, u32[]{:S(2)}) collective-permute-start(bf16[256,1536]{1,0:T(8,128)(2,1)} %fusion.205), channel_id=1, source_target_pairs={{0,2},{1,3},{2,0},{3,1},{4,6},{5,7},{6,4},{7,5},{8,10},{9,11},{10,... | collective-permute-start | bytes 2359304 | tf_op jit(solution)/shard_map/ppermute | solution.py:39
  411.7 75.1 %collective-permute-start.51 = (bf16[256,1536]{1,0:T(8,128)(2,1)}, bf16[256,1536]{1,0:T(8,128)(2,1)}, u32[]{:S(2)}, u32[]{:S(2)}) collective-permute-start(bf16[256,1536]{1,0:T(8,128)(2,1)} %fusion.205), channel_id=1, source_target_pairs={{0,1},{1,0},{2,3},{3,2},{4,5},{5,4},{6,7},{7,6},{8,9},{9,8},{10,11... | collective-permute-start | bytes 2359304 | tf_op jit(solution)/shard_map/ppermute | solution.py:39
  414.0 62.0 %collective-permute-start.56 = (bf16[256,384]{0,1:T(8,128)(2,1)}, bf16[256,384]{0,1:T(8,128)(2,1)}, u32[]{:S(2)}, u32[]{:S(2)}) collective-permute-start(bf16[256,384]{0,1:T(8,128)(2,1)} %get-tuple-element.175), channel_id=1, source_target_pairs={{0,3},{1,2},{2,1},{3,0},{4,7},{5,6},{6,5},{7,4},{8,11},{9,10},{10,... | collective-permute-start | bytes 589832 | tf_op jit(solution)/shard_map/ppermute | solution.py:39
  415.8 67.4 %collective-permute-start.58 = (bf16[256,1536]{1,0:T(8,128)(2,1)}, bf16[256,1536]{1,0:T(8,128)(2,1)}, u32[]{:S(2)}, u32[]{:S(2)}) collective-permute-start(bf16[256,1536]{1,0:T(8,128)(2,1)} %add_convert_fusion.5), channel_id=1, source_target_pairs={{0,2},{1,3},{2,0},{3,1},{4,6},{5,7},{6,4},{7,5},{8,10},{9,11},{10,... | collective-permute-start | bytes 2359304 | tf_op jit(solution)/shard_map/ppermute | solution.py:39
  466.5 17.2 %collective-permute-start.31 = (bf16[256,1536]{1,0:T(8,128)(2,1)S(1)}, bf16[256,1536]{1,0:T(8,128)(2,1)S(1)}, u32[]{:S(2)}, u32[]{:S(2)}) collective-permute-start(bf16[256,1536]{1,0:T(8,128)(2,1)S(1)} %slice.339), channel_id=1, source_target_pairs={{0,1},{1,0},{2,3},{3,2},{4,5},{5,4},{6,7},{7,6},{8,9},{9,8},{10,11... | collective-permute-start | bytes 2359304 | tf_op jit(solution)/shard_map/ppermute | solution.py:39
  483.2 19.7 %collective-permute-start.57 = (bf16[256,1536]{1,0:T(8,128)(2,1)}, bf16[256,1536]{1,0:T(8,128)(2,1)S(1)}, u32[]{:S(2)}, u32[]{:S(2)}) collective-permute-start(bf16[256,1536]{1,0:T(8,128)(2,1)} %add_convert_fusion.5), channel_id=1, source_target_pairs={{0,1},{1,0},{2,3},{3,2},{4,5},{5,4},{6,7},{7,6},{8,9},{9,8},{10,11... | collective-permute-start | bytes 2359304 | tf_op jit(solution)/shard_map/ppermute | solution.py:39
  483.7 19.3 %collective-permute-start.59 = (bf16[256,1536]{1,0:T(8,128)(2,1)}, bf16[256,1536]{1,0:T(8,128)(2,1)S(1)}, u32[]{:S(2)}, u32[]{:S(2)}) collective-permute-start(bf16[256,1536]{1,0:T(8,128)(2,1)} %collective-permute-done.58), channel_id=1, source_target_pairs={{0,1},{1,0},{2,3},{3,2},{4,5},{5,4},{6,7},{7,6},{8,9},{9,8},{10,11... | collective-permute-start | bytes 2359304 | tf_op jit(solution)/shard_map/ppermute | solution.py:39
  492.9 41.3 %collective-permute-start.78 = (bf16[192,1536]{1,0:T(8,128)(2,1)}, bf16[192,1536]{1,0:T(8,128)(2,1)}, u32[]{:S(2)}, u32[]{:S(2)}) collective-permute-start(bf16[192,1536]{1,0:T(8,128)(2,1)} %get-tuple-element.138), channel_id=1, source_target_pairs={{0,8},{4,12},{8,16},{12,20},{16,24},{20,28},{1,9},{5,13},{9,17},{1... | collective-permute-start | bytes 1769480 | tf_op jit(solution)/shard_map/ppermute | solution.py:95
  497.4 33.2 %collective-permute-start.87 = (bf16[192,1536]{1,0:T(8,128)(2,1)}, bf16[192,1536]{1,0:T(8,128)(2,1)}, u32[]{:S(2)}, u32[]{:S(2)}) collective-permute-start(bf16[192,1536]{1,0:T(8,128)(2,1)} %get-tuple-element.135), channel_id=1, source_target_pairs={{24,16},{28,20},{16,8},{20,12},{25,17},{29,21},{17,9},{21,13},{26,... | collective-permute-start | bytes 1769480 | tf_op jit(solution)/shard_map/ppermute | solution.py:95
  498.7 39.6 %collective-permute-start.81 = (bf16[192,1536]{1,0:T(8,128)(2,1)}, bf16[192,1536]{1,0:T(8,128)(2,1)}, u32[]{:S(2)}, u32[]{:S(2)}) collective-permute-start(bf16[192,1536]{1,0:T(8,128)(2,1)} %bitcast_add_fusion.15), channel_id=1, source_target_pairs={{24,16},{28,20},{16,8},{20,12},{8,0},{12,4},{25,17},{29,21},{17,9}... | collective-permute-start | bytes 1769480 | tf_op jit(solution)/shard_map/ppermute | solution.py:95
  502.9 22.0 %collective-permute-start.30 = (bf16[256,1536]{1,0:T(8,128)(2,1)}, bf16[256,1536]{1,0:T(8,128)(2,1)}, u32[]{:S(2)}, u32[]{:S(2)}) collective-permute-start(bf16[256,1536]{1,0:T(8,128)(2,1)} %slice.446), channel_id=1, source_target_pairs={{0,1},{1,0},{2,3},{3,2},{4,5},{5,4},{6,7},{7,6},{8,9},{9,8},{10,11... | collective-permute-start | bytes 2359304 | tf_op jit(solution)/shard_map/ppermute | solution.py:39
  503.0 23.5 %collective-permute-start.32 = (bf16[256,1536]{1,0:T(8,128)(2,1)}, bf16[256,1536]{1,0:T(8,128)(2,1)}, u32[]{:S(2)}, u32[]{:S(2)}) collective-permute-start(bf16[256,1536]{1,0:T(8,128)(2,1)} %slice_add_fusion.4), channel_id=1, source_target_pairs={{0,2},{1,3},{2,0},{3,1},{4,6},{5,7},{6,4},{7,5},{8,10},{9,11},{10,... | collective-permute-start | bytes 2359304 | tf_op jit(solution)/shard_map/ppermute | solution.py:39
  525.0 110.2 %collective-permute-start.44 = (bf16[4,192,1152]{2,1,0:T(8,128)(2,1)S(1)}, bf16[4,192,1152]{2,1,0:T(8,128)(2,1)S(1)}, u32[]{:S(2)}, u32[]{:S(2)}) collective-permute-start(bf16[4,192,1152]{2,1,0:T(8,128)(2,1)S(1)} %copy-done.38), channel_id=1, source_target_pairs={{0,4},{4,0},{8,12},{12,8},{16,20},{20,16},{24,28},{28,24},{1,5},{5... | collective-permute-start | bytes 5308424 | tf_op jit(solution)/shard_map/ppermute | solution.py:84
  526.5 110.3 %collective-permute-start.63 = (bf16[4,192,1920]{2,1,0:T(8,128)(2,1)S(1)}, bf16[4,192,1920]{2,1,0:T(8,128)(2,1)S(1)}, u32[]{:S(2)}, u32[]{:S(2)}) collective-permute-start(bf16[4,192,1920]{2,1,0:T(8,128)(2,1)S(1)} %dynamic-slice_bitcast_fusion), channel_id=1, source_target_pairs={{0,4},{4,0},{8,12},{12,8},{16,20},{20,16},{24,28},{28,24},{1,5},{5... | collective-permute-start | bytes 8847368 | tf_op jit(solution)/shard_map/ppermute | solution.py:84
  532.0 17.7 %collective-permute-start.85 = (bf16[192,1536]{1,0:T(8,128)(2,1)S(1)}, bf16[192,1536]{1,0:T(8,128)(2,1)S(1)}, u32[]{:S(2)}, u32[]{:S(2)}) collective-permute-start(bf16[192,1536]{1,0:T(8,128)(2,1)S(1)} %copy-done.56), channel_id=1, source_target_pairs={{0,8},{4,12},{8,16},{12,20},{16,24},{20,28},{1,9},{5,13},{9,17},{1... | collective-permute-start | bytes 1769480 | tf_op jit(solution)/shard_map/ppermute | solution.py:95
  534.1 18.6 %collective-permute-start.88 = (bf16[192,1536]{1,0:T(8,128)(2,1)S(1)}, bf16[192,1536]{1,0:T(8,128)(2,1)S(1)}, u32[]{:S(2)}, u32[]{:S(2)}) collective-permute-start(bf16[192,1536]{1,0:T(8,128)(2,1)S(1)} %bitcast_add_fusion.11), channel_id=1, source_target_pairs={{24,16},{28,20},{16,8},{20,12},{8,0},{12,4},{25,17},{29,21},{17,9}... | collective-permute-start | bytes 1769480 | tf_op jit(solution)/shard_map/ppermute | solution.py:95
  544.7 84.4 %collective-permute-start.41 = (f32[3072]{0:T(1024)S(1)}, f32[3072]{0:T(1024)S(1)}, u32[]{:S(2)}, u32[]{:S(2)}) collective-permute-start(f32[3072]{0:T(1024)S(1)} %add.460), channel_id=1, source_target_pairs={{0,4},{4,0},{8,12},{12,8},{16,20},{20,16},{24,28},{28,24},{1,5},{5... | collective-permute-start | bytes 36872 | tf_op jit(solution)/shard_map/ppermute | solution.py:106
  549.7 79.4 %collective-permute-start.71 = (f32[6272]{0:T(1024)S(1)}, f32[6272]{0:T(1024)S(1)}, u32[]{:S(2)}, u32[]{:S(2)}) collective-permute-start(f32[6272]{0:T(1024)S(1)} %add.488), channel_id=1, source_target_pairs={{0,2},{1,3},{2,0},{3,1},{4,6},{5,7},{6,4},{7,5},{8,10},{9,11},{10,... | collective-permute-start | bytes 75272 | tf_op jit(solution)/shard_map/ppermute | solution.py:39
  635.5 14.9 %collective-permute-start.45 = (bf16[192,1152]{1,0:T(8,128)(2,1)S(1)}, bf16[192,1152]{1,0:T(8,128)(2,1)S(1)}, u32[]{:S(2)}, u32[]{:S(2)}) collective-permute-start(bf16[192,1152]{1,0:T(8,128)(2,1)S(1)} %get-tuple-element.155), channel_id=1, source_target_pairs={{0,8},{4,12},{1,9},{5,13},{2,10},{6,14},{3,11},{7,15}} | collective-permute-start | bytes 1327112 | tf_op jit(solution)/shard_map/ppermute | solution.py:95
  637.3 28.9 %collective-permute-start.64 = (bf16[192,1920]{1,0:T(8,128)(2,1)S(1)}, bf16[192,1920]{1,0:T(8,128)(2,1)S(1)}, u32[]{:S(2)}, u32[]{:S(2)}) collective-permute-start(bf16[192,1920]{1,0:T(8,128)(2,1)S(1)} %get-tuple-element.132), channel_id=1, source_target_pairs={{0,8},{4,12},{1,9},{5,13},{2,10},{6,14},{3,11},{7,15}} | collective-permute-start | bytes 2211848 | tf_op jit(solution)/shard_map/ppermute | solution.py:95
  640.5 28.4 %collective-permute-start.74 = (f32[6272]{0:T(1024)S(1)}, f32[6272]{0:T(1024)S(1)}, u32[]{:S(2)}, u32[]{:S(2)}) collective-permute-start(f32[6272]{0:T(1024)S(1)} %add.491), channel_id=1, source_target_pairs={{0,16},{4,20},{8,24},{12,28},{16,0},{20,4},{24,8},{28,12},{1,17},{... | collective-permute-start | bytes 75272 | tf_op jit(solution)/shard_map/ppermute | solution.py:106
  642.0 27.0 %collective-permute-start.48 = (bf16[192,1152]{1,0:T(8,128)(2,1)S(1)}, bf16[192,1152]{1,0:T(8,128)(2,1)S(1)}, u32[]{:S(2)}, u32[]{:S(2)}) collective-permute-start(bf16[192,1152]{1,0:T(8,128)(2,1)S(1)} %get-tuple-element.156), channel_id=1, source_target_pairs={{24,16},{28,20},{25,17},{29,21},{26,18},{30,22},{27,19},{31,23}} | collective-permute-start | bytes 1327112 | tf_op jit(solution)/shard_map/ppermute | solution.py:95
  650.5 25.8 %collective-permute-start.46 = (bf16[192,1152]{1,0:T(8,128)(2,1)S(1)}, bf16[192,1152]{1,0:T(8,128)(2,1)S(1)}, u32[]{:S(2)}, u32[]{:S(2)}) collective-permute-start(bf16[192,1152]{1,0:T(8,128)(2,1)S(1)} %bitcast_add_fusion.20), channel_id=1, source_target_pairs={{0,8},{4,12},{8,16},{12,20},{1,9},{5,13},{9,17},{13,21},{2,10},{6,... | collective-permute-start | bytes 1327112 | tf_op jit(solution)/shard_map/ppermute | solution.py:95
  652.5 25.3 %collective-permute-start.67 = (bf16[192,1920]{1,0:T(8,128)(2,1)S(1)}, bf16[192,1920]{1,0:T(8,128)(2,1)S(1)}, u32[]{:S(2)}, u32[]{:S(2)}) collective-permute-start(bf16[192,1920]{1,0:T(8,128)(2,1)S(1)} %get-tuple-element.133), channel_id=1, source_target_pairs={{24,16},{28,20},{25,17},{29,21},{26,18},{30,22},{27,19},{31,23}} | collective-permute-start | bytes 2211848 | tf_op jit(solution)/shard_map/ppermute | solution.py:95
  666.4 23.3 %collective-permute-start.65 = (bf16[192,1920]{1,0:T(8,128)(2,1)S(1)}, bf16[192,1920]{1,0:T(8,128)(2,1)S(1)}, u32[]{:S(2)}, u32[]{:S(2)}) collective-permute-start(bf16[192,1920]{1,0:T(8,128)(2,1)S(1)} %bitcast_add_fusion.8), channel_id=1, source_target_pairs={{0,8},{4,12},{8,16},{12,20},{1,9},{5,13},{9,17},{13,21},{2,10},{6,... | collective-permute-start | bytes 2211848 | tf_op jit(solution)/shard_map/ppermute | solution.py:95
  676.5 20.3 %collective-permute-start.49 = (bf16[192,1152]{1,0:T(8,128)(2,1)S(1)}, bf16[192,1152]{1,0:T(8,128)(2,1)S(1)}, u32[]{:S(2)}, u32[]{:S(2)}) collective-permute-start(bf16[192,1152]{1,0:T(8,128)(2,1)S(1)} %get-tuple-element.154), channel_id=1, source_target_pairs={{24,16},{28,20},{16,8},{20,12},{25,17},{29,21},{17,9},{21,13},{26,... | collective-permute-start | bytes 1327112 | tf_op jit(solution)/shard_map/ppermute | solution.py:95
  689.8 21.3 %collective-permute-start.68 = (bf16[192,1920]{1,0:T(8,128)(2,1)S(1)}, bf16[192,1920]{1,0:T(8,128)(2,1)S(1)}, u32[]{:S(2)}, u32[]{:S(2)}) collective-permute-start(bf16[192,1920]{1,0:T(8,128)(2,1)S(1)} %get-tuple-element.131), channel_id=1, source_target_pairs={{24,16},{28,20},{16,8},{20,12},{25,17},{29,21},{17,9},{21,13},{26,... | collective-permute-start | bytes 2211848 | tf_op jit(solution)/shard_map/ppermute | solution.py:95
  692.3 20.8 %collective-permute-start.47 = (bf16[192,1152]{1,0:T(8,128)(2,1)S(1)}, bf16[192,1152]{1,0:T(8,128)(2,1)S(1)}, u32[]{:S(2)}, u32[]{:S(2)}) collective-permute-start(bf16[192,1152]{1,0:T(8,128)(2,1)S(1)} %get-tuple-element.153), channel_id=1, source_target_pairs={{0,8},{4,12},{8,16},{12,20},{16,24},{20,28},{1,9},{5,13},{9,17},{1... | collective-permute-start | bytes 1327112 | tf_op jit(solution)/shard_map/ppermute | solution.py:95
  696.9 23.7 %collective-permute-start.50 = (bf16[192,1152]{1,0:T(8,128)(2,1)S(1)}, bf16[192,1152]{1,0:T(8,128)(2,1)S(1)}, u32[]{:S(2)}, u32[]{:S(2)}) collective-permute-start(bf16[192,1152]{1,0:T(8,128)(2,1)S(1)} %bitcast_add_fusion.19), channel_id=1, source_target_pairs={{24,16},{28,20},{16,8},{20,12},{8,0},{12,4},{25,17},{29,21},{17,9}... | collective-permute-start | bytes 1327112 | tf_op jit(solution)/shard_map/ppermute | solution.py:95
  698.8 22.8 %collective-permute-start.66 = (bf16[192,1920]{1,0:T(8,128)(2,1)S(1)}, bf16[192,1920]{1,0:T(8,128)(2,1)S(1)}, u32[]{:S(2)}, u32[]{:S(2)}) collective-permute-start(bf16[192,1920]{1,0:T(8,128)(2,1)S(1)} %get-tuple-element.130), channel_id=1, source_target_pairs={{0,8},{4,12},{8,16},{12,20},{16,24},{20,28},{1,9},{5,13},{9,17},{1... | collective-permute-start | bytes 2211848 | tf_op jit(solution)/shard_map/ppermute | solution.py:95
  711.2 21.8 %collective-permute-start.69 = (bf16[192,1920]{1,0:T(8,128)(2,1)S(1)}, bf16[192,1920]{1,0:T(8,128)(2,1)S(1)}, u32[]{:S(2)}, u32[]{:S(2)}) collective-permute-start(bf16[192,1920]{1,0:T(8,128)(2,1)S(1)} %bitcast_add_fusion.7), channel_id=1, source_target_pairs={{24,16},{28,20},{16,8},{20,12},{8,0},{12,4},{25,17},{29,21},{17,9}... | collective-permute-start | bytes 2211848 | tf_op jit(solution)/shard_map/ppermute | solution.py:95
  (158 other events, 1682.1 us)

commit v2 on v1

--- a/solution.py
+++ b/solution.py
@@ -3,10 +3,12 @@
 import jax
 import jax.numpy as jnp
 from jax import lax
+from jax.experimental import pallas as pl
+from jax.experimental.pallas import tpu as pltpu
 from jax.sharding import PartitionSpec as P
 
+
 HD = 64
-FRAMES = 1024
 
 
 norm_eps = 1e-05
@@ -51,13 +53,6 @@
 
 def swap_relative(blocks):
     return [blocks[0]] + [exchange(blocks[flip], flip) for flip in (1, 2, 3)]
-
-
-def to_absolute(values, own_id):
-    rows = values.shape[0] // 4
-    return jnp.concatenate(
-        [lax.dynamic_slice_in_dim(values, (own_id ^ flip) * rows, rows, 0) for flip in range(4)]
-    )
 
 
 def scatter_product(far_pair, near_pair, own_rows):
@@ -69,32 +64,39 @@
     return near_part[:own_rows] + near_other + over_link
 
 
-def sum_clips(part):
-    size = lax.axis_size("dp")
-    if size != 8:
-        return lax.psum_scatter(
-            part.astype(jnp.bfloat16), "dp", scatter_dimension=0, tiled=True
-        ).astype(jnp.float32)
-    own = lax.axis_index("dp")
-    own_z, own_y = own // 2, own % 2
-    rows = part.shape[0] // 8
-    halves = part.astype(jnp.bfloat16).reshape(4, 2, rows, part.shape[1])
-    sent = lax.dynamic_index_in_dim(halves, 1 - own_y, 1, keepdims=False)
-    kept = lax.dynamic_index_in_dim(halves, own_y, 1, keepdims=False)
-    kept = kept + lax.ppermute(sent, "dp", [(i, i ^ 1) for i in range(8)])
+def swap_y(values):
+    return lax.ppermute(values, "dp", [(i, i ^ 1) for i in range(8)])
+
+
+def sum_line(kept):
+    own_z = lax.axis_index("dp") // 2
     total = lax.dynamic_index_in_dim(kept, own_z, 0, keepdims=False).astype(jnp.float32)
-    for sign in (1, -1):
-        carried = None
-        for step in range(1, 4):
+    carried = {}
+    for step in range(1, 4):
+        for sign in (1, -1):
             target = jnp.clip(own_z + sign * (4 - step), 0, 3)
             block = lax.dynamic_index_in_dim(kept, target, 0, keepdims=False)
-            if carried is not None:
-                block = block + carried
+            if step > 1:
+                block = block + carried[sign]
             senders = range(step) if sign > 0 else range(3, 3 - step, -1)
             pairs = [(2 * z + y, 2 * (z + sign) + y) for z in senders for y in range(2)]
-            carried = lax.ppermute(block, "dp", pairs)
-        total = total + carried
-    return total
+            carried[sign] = lax.ppermute(block, "dp", pairs)
+    return total + carried[1] + carried[-1]
+
+
+def sum_clips(part, line_first=False):
+    size = lax.axis_size("dp")
+    part = part.astype(jnp.bfloat16)
+    if size != 8:
+        return lax.psum_scatter(part, "dp", scatter_dimension=0, tiled=True).astype(jnp.float32)
+    own_y = lax.axis_index("dp") % 2
+    halves = part.reshape(4, 2, part.shape[0] // 8, part.shape[1])
+    if line_first:
+        halves = sum_line(halves)[None]
+    sent = lax.dynamic_index_in_dim(halves, 1 - own_y, 1, keepdims=False).astype(jnp.bfloat16)
+    kept = lax.dynamic_index_in_dim(halves, own_y, 1, keepdims=False)
+    kept = kept + swap_y(sent)
+    return kept[0] if line_first else sum_line(kept)
 
 
 def sum_everywhere(values):
@@ -108,89 +110,134 @@
 
 
 def after(values, *others):
-    return lax.optimization_barrier((values,) + others)[0]
-
-
-def block_scores(queries, all_keys, begin_row, end_row):
-    scores = jnp.einsum(
-        "cqhd,ckhd->chqk",
-        queries[:, begin_row:end_row],
-        all_keys[:, :end_row],
-        preferred_element_type=jnp.float32,
-    ) * HD ** (-0.5)
-    row_ids = begin_row + lax.broadcasted_iota(jnp.int32, (end_row - begin_row, end_row), 0)
-    col_ids = lax.broadcasted_iota(jnp.int32, (end_row - begin_row, end_row), 1)
-    return jnp.where(col_ids <= row_ids, scores, -1e30)
-
-
-def self_forward(queries, all_keys, all_values):
-    block_rows = min(512, FRAMES)
-    outputs, peak_list, sum_list = ([], [], [])
-    for begin_row in range(0, FRAMES, block_rows):
-        end_row = begin_row + block_rows
-        scores = block_scores(queries, all_keys, begin_row, end_row)
-        row_peak = jnp.max(scores, axis=-1, keepdims=True)
-        exp_scores = jnp.exp(scores - row_peak)
-        row_sum = jnp.sum(exp_scores, axis=-1, keepdims=True)
-        weights = (exp_scores / row_sum).astype(jnp.bfloat16)
-        outputs.append(
-            jnp.einsum(
-                "chqk,ckhd->cqhd",
-                weights,
-                all_values[:, :end_row],
-                preferred_element_type=jnp.float32,
-            )
-        )
-        peak_list.append(row_peak)
-        sum_list.append(row_sum)
-    return (jnp.concatenate(outputs, axis=1), peak_list, sum_list)
-
-
-def self_backward(queries, all_keys, all_values, peak_list, sum_list, grad_mixed):
-    block_rows = min(512, FRAMES)
-    score_scale = HD ** (-0.5)
-    query_parts = []
-    grad_keys = jnp.zeros(all_keys.shape, jnp.float32)
-    grad_values = jnp.zeros(all_values.shape, jnp.float32)
-    for block_id, begin_row in enumerate(range(0, FRAMES, block_rows)):
-        end_row = begin_row + block_rows
-        scores = block_scores(queries, all_keys, begin_row, end_row)
-        weights = jnp.exp(scores - peak_list[block_id]) / sum_list[block_id]
-        grad_weights = jnp.einsum(
-            "cqhd,ckhd->chqk",
-            grad_mixed[:, begin_row:end_row],
-            all_values[:, :end_row],
-            preferred_element_type=jnp.float32,
-        )
-        row_dot = jnp.sum(weights * grad_weights, axis=-1, keepdims=True)
-        grad_scores = (weights * (grad_weights - row_dot)).astype(jnp.bfloat16)
-        query_parts.append(
-            jnp.einsum(
-                "chqk,ckhd->cqhd",
-                grad_scores,
-                all_keys[:, :end_row],
-                preferred_element_type=jnp.float32,
-            )
-            * score_scale
-        )
-        grad_keys = grad_keys.at[:, :end_row].add(
-            jnp.einsum(
-                "chqk,cqhd->ckhd",
-                grad_scores,
-                queries[:, begin_row:end_row],
-                preferred_element_type=jnp.float32,
-            )
-            * score_scale
-        )
-        grad_values = grad_values.at[:, :end_row].add(
-            jnp.einsum(
-                "chqk,cqhd->ckhd",
-                weights.astype(jnp.bfloat16),
-                grad_mixed[:, begin_row:end_row],
-                preferred_element_type=jnp.float32,
-            )
-        )
-    return (jnp.concatenate(query_parts, axis=1), grad_keys, grad_values)
+    return lax.optimization_barrier((values,) + others)[0] if others else values
+
+
+def attention_piece(q_block, k_ref, block_id, rows, cols, own_id, masked):
+    keys = k_ref[pl.ds(pl.multiple_of((block_id ^ own_id) * rows, rows), rows), cols]
+    scores = contract_cols(q_block, keys)
+    if masked:
+        row_ids = lax.broadcasted_iota(jnp.int32, (rows, rows), 0)
+        col_ids = lax.broadcasted_iota(jnp.int32, (rows, rows), 1)
+        scores = jnp.where(col_ids <= row_ids, scores, -1e30)
+    return scores
+
+
+def attention_weights(q_block, k_ref, block_id, rows, cols, own_id):
+    pieces = [
+        attention_piece(q_block, k_ref, other, rows, cols, own_id, other == block_id)
+        for other in range(block_id + 1)
+    ]
+    peak = pieces[0].max(axis=1, keepdims=True)
+    for piece in pieces[1:]:
+        peak = jnp.maximum(peak, piece.max(axis=1, keepdims=True))
+    pieces = [jnp.exp(piece - peak) for piece in pieces]
+    total = pieces[0].sum(axis=1, keepdims=True)
+    for piece in pieces[1:]:
+        total = total + piece.sum(axis=1, keepdims=True)
+    share = 1.0 / total
+    return [piece * share for piece in pieces]
+
+
+def forward_kernel(rows, id_ref, q_ref, k_ref, v_ref, out_ref):
+    own_id = id_ref[0]
+    for head in range(q_ref.shape[1] // HD):
+        cols = slice(head * HD, (head + 1) * HD)
+        for block_id in range(4):
+            here = pl.ds(pl.multiple_of((block_id ^ own_id) * rows, rows), rows)
+            q_block = q_ref[here, cols] * jnp.bfloat16(HD**-0.5)
+            weights = attention_weights(q_block, k_ref, block_id, rows, cols, own_id)
+            mixed = jnp.zeros((rows, HD), jnp.float32)
+            for other, piece in enumerate(weights):
+                there = pl.ds(pl.multiple_of((other ^ own_id) * rows, rows), rows)
+                mixed = mixed + product(piece.astype(jnp.bfloat16), v_ref[there, cols])
+            out_ref[here, cols] = mixed.astype(jnp.bfloat16)
+
+
+def backward_kernel(
+    rows, id_ref, q_ref, k_ref, v_ref, grad_ref, dq_ref, dk_ref, dv_ref, dk_sum, dv_sum
+):
+    own_id = id_ref[0]
+    for head in range(q_ref.shape[1] // HD):
+        cols = slice(head * HD, (head + 1) * HD)
+        for block_id in range(3, -1, -1):
+            here = pl.ds(pl.multiple_of((block_id ^ own_id) * rows, rows), rows)
+            q_block = q_ref[here, cols] * jnp.bfloat16(HD**-0.5)
+            grads = grad_ref[here, cols]
+            weights = attention_weights(q_block, k_ref, block_id, rows, cols, own_id)
+            theres = [
+                pl.ds(pl.multiple_of((other ^ own_id) * rows, rows), rows)
+                for other in range(block_id + 1)
+            ]
+            weight_grads = [contract_cols(grads, v_ref[there, cols]) for there in theres]
+            row_dot = jnp.zeros((rows, 1), jnp.float32)
+            for piece, piece_grad in zip(weights, weight_grads):
+                row_dot = row_dot + (piece * piece_grad).sum(axis=1, keepdims=True)
+            dq = jnp.zeros((rows, HD), jnp.float32)
+            for other, there in enumerate(theres):
+                piece = weights[other]
+                score_grad = (piece * (weight_grads[other] - row_dot)).astype(jnp.bfloat16)
+                dq = dq + product(score_grad, k_ref[there, cols])
+                dk = contract_rows(score_grad, q_block)
+                dv = contract_rows(piece.astype(jnp.bfloat16), grads)
+                held = pl.ds(other * rows, rows)
+                if block_id == 3:
+                    dk_sum[held, cols] = dk
+                    dv_sum[held, cols] = dv
+                else:
+                    dk_sum[held, cols] += dk
+                    dv_sum[held, cols] += dv
+            dq_ref[here, cols] = (dq * HD**-0.5).astype(jnp.bfloat16)
+    for block_id in range(4):
+        here = pl.ds(pl.multiple_of((block_id ^ own_id) * rows, rows), rows)
+        dk_ref[here, :] = dk_sum[pl.ds(block_id * rows, rows), :].astype(jnp.bfloat16)
+        dv_ref[here, :] = dv_sum[pl.ds(block_id * rows, rows), :].astype(jnp.bfloat16)
+
+
+def pair_spec(length, first):
+    return pl.BlockSpec((length, 2 * HD), lambda i, ids: (0, first + i))
+
+
+def self_forward(qkv, own_id, rows):
+    length, pairs = qkv.shape[0], qkv.shape[1] // (6 * HD)
+    return pl.pallas_call(
+        partial(forward_kernel, rows),
+        out_shape=jax.ShapeDtypeStruct((length, pairs * 2 * HD), jnp.bfloat16),
+        grid_spec=pltpu.PrefetchScalarGridSpec(
+            num_scalar_prefetch=1,
+            grid=(pairs,),
+            in_specs=[pair_spec(length, part * pairs) for part in range(3)],
+            out_specs=pair_spec(length, 0),
+        ),
+        cost_estimate=pl.CostEstimate(
+            flops=pairs * 8 * HD * length * length * 5 // 8,
+            bytes_accessed=pairs * 16 * HD * length,
+            transcendentals=pairs * 2 * length * length * 5 // 8,
+        ),
+        name="self_forward",
+    )(own_id.reshape(1), qkv, qkv, qkv)
+
+
+def self_backward(qkv, grads, own_id, rows):
+    length, pairs = qkv.shape[0], qkv.shape[1] // (6 * HD)
+    return pl.pallas_call(
+        partial(backward_kernel, rows),
+        out_shape=[jax.ShapeDtypeStruct((length, pairs * 2 * HD), jnp.bfloat16)] * 3,
+        grid_spec=pltpu.PrefetchScalarGridSpec(
+            num_scalar_prefetch=1,
+            grid=(pairs,),
+            in_specs=[pair_spec(length, part * pairs) for part in range(3)]
+            + [pair_spec(length, 0)],
+            out_specs=[pair_spec(length, 0)] * 3,
+            scratch_shapes=[pltpu.VMEM((length, 2 * HD), jnp.float32)] * 2,
+        ),
+        cost_estimate=pl.CostEstimate(
+            flops=pairs * 20 * HD * length * length * 5 // 8,
+            bytes_accessed=pairs * 28 * HD * length,
+            transcendentals=pairs * 2 * length * length * 5 // 8,
+        ),
+        name="self_backward",
+    )(own_id.reshape(1), qkv, qkv, qkv, grads)
 
 
 def cross_forward(queries, all_keys, all_values):
@@ -233,7 +280,7 @@
     return (grad_queries, grad_keys, grad_values)
 
 
-def body(
+def layer(
     layer_input,
     text_states,
     ln1_gain,
@@ -258,7 +305,6 @@
     text_len = text_states.shape[1]
     own_rows, model_width = layer_input.shape
     local_width = w_q.shape[1]
-    local_heads = local_width // HD
     own_id = lax.axis_index("tensor")
     low = jnp.bfloat16
 
@@ -272,18 +318,9 @@
     normed_one = layer_norm(stream, ln1_gain, ln1_bias).astype(low)
     one = gather_relative(normed_one)
     w_qkv = jnp.concatenate([w_q, w_k, w_v], axis=1)
-    near_one = jnp.concatenate(one[:2])
-    far_one = jnp.concatenate(one[2:])
-    rows_one = jnp.concatenate([near_one, far_one])
-    qkv = jnp.concatenate(
-        [product(near_one, w_qkv).astype(low), product(far_one, w_qkv).astype(low)]
-    )
-    qkv = to_absolute(qkv, own_id)
-    queries, all_keys, all_values = [
-        split_heads(qkv[:, i * local_width : (i + 1) * local_width], FRAMES) for i in range(3)
-    ]
-    mixed_one, peak_list, sum_list = self_forward(queries, all_keys, all_values)
-    attended = to_absolute(merge_heads(mixed_one), own_id)
+    rows_one = jnp.concatenate(one)
+    qkv = product(rows_one, w_qkv).astype(low)
+    attended = self_forward(qkv, own_id, own_rows)
     branch_one = scatter_product(
         lambda: product(attended[2 * own_rows :], w_o),
         lambda: product(attended[: 2 * own_rows], w_o),
@@ -302,7 +339,6 @@
     grad_rows = gather_relative(after(out_cotangent, c_o_full))
     grad_near = jnp.concatenate(grad_rows[:2])
     grad_far = jnp.concatenate(grad_rows[2:])
-    grad_three_rows = jnp.concatenate([grad_near, grad_far])
 
     hidden_one = stream + branch_one
     normed_two = layer_norm(hidden_one, ln2_gain, ln2_bias).astype(low)
@@ -327,27 +363,8 @@
         lambda: contract_cols(pre_grads[0], w_in),
         own_rows,
     )
-    rows_three = jnp.concatenate([near_three, far_three])
-    activated = jnp.concatenate(act_parts)
-    grad_pre = jnp.concatenate(pre_grads)
-    w_out_part = contract_rows(grad_three_rows, activated)
-    w_in_part = contract_rows(rows_three, grad_pre)
-    w_out_grad = sum_clips(w_out_part).T
-    w_in_grad = sum_clips(w_in_part)
-    branch_three = scatter_product(
-        lambda: product(after(act_parts[1], grad_normed_three), w_out),
-        lambda: product(act_parts[0], w_out),
-        own_rows,
-    )
-    block_out = (hidden_two + branch_three).astype(low)
-    squares = jnp.stack(
-        [
-            jnp.sum(stream * stream),
-            jnp.sum(branch_one * branch_one),
-            jnp.sum(branch_two * branch_two),
-            jnp.sum(branch_three * branch_three),
-        ]
-    )
+    w_out_part = contract_rows(grad_near, act_parts[0]) + contract_rows(grad_far, act_parts[1])
+    w_in_part = contract_rows(near_three, pre_grads[0]) + contract_rows(far_three, pre_grads[1])
 
     grad_out = out_cotangent.astype(jnp.float32)
     norm_value, norm_back = jax.vjp(layer_norm, hidden_two, ln3_gain, ln3_bias)
@@ -366,24 +383,24 @@
 
     one_grads = gather_relative(grad_one.astype(low))
     grad_one_rows = jnp.concatenate(one_grads)
-    grad_mixed_one = jnp.concatenate(
-        [
-            contract_cols(jnp.concatenate(one_grads[:2]), w_o).astype(low),
-            contract_cols(jnp.concatenate(one_grads[2:]), w_o).astype(low),
-        ]
-    )
-    grad_mixed_one = split_heads(to_absolute(grad_mixed_one, own_id), FRAMES)
-    grad_sq, grad_sk, grad_sv = self_backward(
-        queries, all_keys, all_values, peak_list, sum_list, grad_mixed_one
-    )
-    grad_qkv = jnp.concatenate([merge_heads(part) for part in (grad_sq, grad_sk, grad_sv)], axis=1)
-    grad_qkv = to_absolute(grad_qkv, own_id)
+    arrived = one_grads[3]
+    branch_three = scatter_product(
+        lambda: product(after(act_parts[1], arrived), w_out),
+        lambda: product(act_parts[0], w_out),
+        own_rows,
+    )
+    grad_mixed_one = contract_cols(grad_one_rows, w_o).astype(low)
+    qkv_grads = self_backward(qkv, grad_mixed_one, own_id, own_rows)
+    grad_qkv = jnp.concatenate(qkv_grads, axis=1)
     grad_normed_one = scatter_product(
         lambda: contract_cols(grad_qkv[2 * own_rows :], w_qkv),
         lambda: contract_cols(grad_qkv[: 2 * own_rows], w_qkv),
         own_rows,
     )
-    qkv_grad = sum_clips(contract_rows(rows_one, grad_qkv))
+    w_out_grad = sum_clips(w_out_part).T
+    w_in_grad = sum_clips(w_in_part, line_first=True)
+    w_qkv_part = contract_rows(rows_one, grad_qkv)
+    qkv_grad = sum_clips(w_qkv_part)
     w_q_grad, w_k_grad, w_v_grad = jnp.split(qkv_grad, 3, axis=1)
     norm_value, norm_back = jax.vjp(layer_norm, stream, ln1_gain, ln1_bias)
     back_rows, ln1_gain_part, ln1_bias_part = norm_back(grad_normed_one)
@@ -392,29 +409,36 @@
     def columns(matrix):
         return [matrix[:, i * local_width : (i + 1) * local_width] for i in range(4)]
 
-    rows_two = jnp.concatenate(gather_relative(after(normed_two, one_grads[2])))
-    grad_two_rows = jnp.concatenate(gather_relative(after(grad_two_low, one_grads[2])))
-    crossed_rows = jnp.concatenate(swap_relative(columns(after(crossed, one_grads[2]))))
+    rows_two = jnp.concatenate(gather_relative(after(normed_two, three[2])))
+    crossed_rows = jnp.concatenate(swap_relative(columns(after(crossed, three[2]))))
+    grad_two_rows = jnp.concatenate(gather_relative(grad_two_low))
     grad_cq_rows = jnp.concatenate(swap_relative(columns(after(grad_cq, one_grads[2]))))
     grad_text = jnp.concatenate(
         [part.reshape(text_len, -1) for part in (grad_tk, grad_tv)]
     ).astype(jnp.float32)
     grad_text = scatter_relative(*columns(grad_text)).astype(low)
     grad_tk, grad_tv = grad_text[:text_len], grad_text[text_len:]
+    back_grad = sum_clips(
+        jnp.concatenate(
+            [
+                contract_rows(grad_two_rows, crossed_rows).astype(low),
+                contract_rows(grad_one_rows, attended).astype(low),
+            ],
+            axis=1,
+        ),
+    )
     cross_grad = sum_clips(
         jnp.concatenate(
             [
-                contract_rows(grad_two_rows, crossed_rows).astype(low),
                 contract_rows(rows_two, grad_cq_rows).astype(low),
                 contract_rows(text_rows, grad_tk).astype(low),
                 contract_rows(text_rows, grad_tv).astype(low),
-                contract_rows(grad_one_rows, attended).astype(low),
             ],
             axis=1,
-        )
-    )
-    c_o_grad, c_q_grad, c_k_grad, c_v_grad, w_o_grad = jnp.split(cross_grad, 5, axis=1)
-    c_o_grad, w_o_grad = c_o_grad.T, w_o_grad.T
+        ),
+    )
+    c_o_grad, w_o_grad = [part.T for part in jnp.split(back_grad, 2, axis=1)]
+    c_q_grad, c_k_grad, c_v_grad = jnp.split(cross_grad, 3, axis=1)
     text_term = (contract_cols(grad_tk, c_k) + contract_cols(grad_tv, c_v)).astype(low)
     text_states_grad = (
         scatter_relative(
@@ -425,6 +449,16 @@
         )
         .astype(low)
         .reshape(clip_count, text_len, local_width)
+    )
+
+    block_out = (hidden_two + branch_three).astype(low)
+    squares = jnp.stack(
+        [
+            jnp.sum(stream * stream),
+            jnp.sum(branch_one * branch_one),
+            jnp.sum(branch_two * branch_two),
+            jnp.sum(branch_three * branch_three),
+        ]
     )
 
     early = sum_everywhere(
@@ -466,7 +500,7 @@
 
 def solution(mesh):
     return jax.shard_map(
-        body,
+        layer,
         mesh=mesh,
         in_specs=(
             P(("dp", "tensor"), None),

time: 745 us -> 665 us (0.89)
  matrix products: 186 us -> 132 us
  waiting for transfers between devices: 307 us -> 255 us
  Pallas kernels: 0 us -> 42.6 us
  other arithmetic: 82.5 us -> 47.5 us
  starting transfers between devices: 86.2 us -> 109 us
    ppermute x6, waiting for transfers between devices: 77.2 us -> 18.8 us  [sum_everywhere(): lax.ppermute(values, 'dp', [(i, i ^ flip) for i in range(8)])]
    ppermute x55, waiting for transfers between devices: 69.4 us -> 116 us  [exchange(): return lax.ppermute(values, 'tensor', [(i, i ^ flip) for i in range(4)])]
    pallas_call x0 -> x2, Pallas kernels: none -> 42.6 us  [the longest x1 27.3 us: self_backward(): pl.pallas_call(partial(backward_kernel, rows), out_shape=[jax.ShapeDtypeS...]
    ppermute x28 -> x35, waiting for transfers between devices: 161 us -> 121 us  [the longest x30 113 us: sum_line(): carried[sign] = lax.ppermute(block, 'dp', pairs)]
    dot_general x11 -> x0, matrix products: 39.6 us -> none  [the longest x2 12.6 us: self_backward(): jnp.einsum('cqhd,ckhd->chqk', grad_mixed[:, begin_row:end_row], all_value...]
    ppermute x28 -> x35, starting transfers between devices: 53.3 us -> 79.5 us  [the longest x30 73.4 us: sum_line(): carried[sign] = lax.ppermute(block, 'dp', pairs)]
    dot_general x12 -> x11, matrix products: 63.8 us -> 42.4 us  [product(): return jnp.dot(left_mat, right_mat, preferred_element_type=jnp.float32)]
    sub x1 -> x0, other arithmetic: 16.8 us -> none  [self_forward(): exp_scores = jnp.exp(scores - row_peak)]
  transfers between devices with their start and end apart: 89 -> 96, of which waited for: 29 -> 31; matrix products, arithmetic and copies ran while one was open for 41% -> 34% of each run, Pallas kernels for 0% -> 6%
where the time goes in v2:
time: 665 us; the launch traced here: 656 us
  waiting for transfers between devices  255 us (38%)
  matrix products  132 us (20%)
  starting transfers between devices  109 us (16%)
  local copies, waits for them, and re-layouts  66.6 us (10%)
  other arithmetic  47.5 us (7%)
  Pallas kernels  42.6 us (6%)
    ppermute x55, waiting for transfers between devices, exchange(): return lax.ppermute(values, 'tensor', [(i, i ^ flip) for i in range(4)])  116 us
    ppermute x30, waiting for transfers between devices, sum_line(): carried[sign] = lax.ppermute(block, 'dp', pairs)  113 us
    ppermute x30, starting transfers between devices, sum_line(): carried[sign] = lax.ppermute(block, 'dp', pairs)  73.4 us
    dot_general x11, matrix products, product(): return jnp.dot(left_mat, right_mat, preferred_element_type=jnp.float32)  42.4 us
    dot_general x10, matrix products, contract_rows(): lax.dot_general(left_mat, right_mat, (((0,), (0,)), ((), ())), preferred_...  41.2 us
    dot_general x11, matrix products, contract_cols(): lax.dot_general(left_mat, right_mat, (((1,), (1,)), ((), ())), preferred_...  40.8 us
    unnamed x216, local copies, waits for them, and re-layouts  29 us
    pallas_call x1, Pallas kernels, self_backward(): pl.pallas_call(partial(backward_kernel, rows), out_shape=[jax.ShapeDtypeS...  27.3 us
  transfers between devices with their start and end apart: 96, of which 31 were waited for; matrix products, arithmetic and copies ran while one was open for 34% of the time, Pallas kernels for 6%

profile of v2, /device:TPU:8, one launch (start us, length us, event | category | flops | bytes accessed | tf_op | source)
XLA Modules:
  0.0 655.8 jit_solution(9144046103767572296)
XLA Ops:
  12.4 13.9 %collective-permute-done.1 = bf16[256,1536]{1,0:T(8,128)(2,1)} collective-permute-done((bf16[256,1536]{1,0:T(8,128)(2,1)}, bf16[256,1536]{1,0:T(8,128)(2,1)}, u32[]{:S(2)}, u32[]{:S(2)}) %collective-permute-start.1) | collective-permute-done | bytes 786464 | tf_op jit(solution)/shard_map/ppermute | solution.py:41
  36.8 7.5 %convolution_convert_fusion.1.q_ref.k_ref.v_ref = bf16[1024,1152]{1,0:T(8,128)(2,1)} fusion(bf16[1536,1152]{1,0:T(8,128)(2,1)S(1)} %constant_dynamic-update-slice_fusion, bf16[256,1536]{1,0:T(8,128)(2,1)S(1)} %collective-permute-done.2, bf16[256,1536]{1,0:T(8,128)(2,1)} %collective-permute-done.1, bf16[256,1536]{1,0:T(8,128)(2,1)} %collective-permute-done, ...), kind=kOutput, calls=%fused_computation.6 | convolution fusion | flops 3637641216 | bytes 9043968 | tf_op jit(solution)/shard_map/dot_general | solution.py:25
  44.3 15.3 %self_forward.1 = bf16[1024,384]{1,0:T(8,128)(2,1)} custom-call(s32[1]{0:T(128)} %bitcast.id_ref, bf16[1024,1152]{1,0:T(8,128)(2,1)} %convolution_convert_fusion.1.q_ref.k_ref.v_ref, bf16[1024,1152]{1,0:T(8,128)(2,1)} %convolution_convert_fusion.1.q_ref.k_ref.v_ref, bf16[1024,1152]{1,0:T(8,128)(2,1)} %convolution_convert_fusion.1.q_ref.k_ref.v_ref), custom_call_target="tpu_custom_call" | custom-call | flops 1006632960 | bytes 3145728 | tf_op jit(solution)/shard_map/self_forward/pallas_call | solution.py:203
  68.9 18.0 %collective-permute-done.13 = bf16[384,1536]{1,0:T(8,128)(2,1)} collective-permute-done((bf16[384,1536]{1,0:T(8,128)(2,1)}, bf16[384,1536]{1,0:T(8,128)(2,1)}, u32[]{:S(2)}, u32[]{:S(2)}) %collective-permute-start.13) | collective-permute-done | bytes 1179680 | tf_op jit(solution)/shard_map/ppermute | solution.py:41
  98.7 11.9 %collective-permute-done.5 = bf16[256,1536]{1,0:T(8,128)(2,1)S(1)} collective-permute-done((bf16[256,1536]{1,0:T(8,128)(2,1)S(1)}, bf16[256,1536]{1,0:T(8,128)(2,1)S(1)}, u32[]{:S(2)}, u32[]{:S(2)}) %collective-permute-start.5) | collective-permute-done | bytes 786464 | tf_op jit(solution)/shard_map/ppermute | solution.py:41
  118.9 2.6 fusion.139
  123.2 2.7 constant_dynamic-update-slice_fusion.11
  125.9 4.6 fusion.130
  135.3 11.6 %multiply_convert_fusion.1 = (bf16[512,1536]{1,0:T(8,128)(2,1)S(1)}, f32[512,1536]{1,0:T(8,128)S(1)}, f32[512,1536]{1,0:T(8,128)S(1)}) fusion(bf16[1536,1536]{1,0:T(8,128)(2,1)} %param.35, bf16[256,1536]{1,0:T(8,128)(2,1)} %collective-permute-done.15, bf16[256,1536]{1,0:T(8,128)(2,1)} %add_convert_fusion.6), kind=kOutput, calls=%fused_computation.43 | convolution fusion | flops 2470182912 | bytes 14155776 | tf_op jit(solution)/shard_map/dot_general | solution.py:25
  147.0 3.4 add_convert_fusion.3
  150.4 4.6 fusion.142
  155.1 2.6 fusion.140
  159.6 10.5 %collective-permute-done.21 = bf16[256,1536]{1,0:T(8,128)(2,1)S(1)} collective-permute-done((bf16[256,1536]{1,0:T(8,128)(2,1)S(1)}, bf16[256,1536]{1,0:T(8,128)(2,1)S(1)}, u32[]{:S(2)}, u32[]{:S(2)}) %collective-permute-start.21) | collective-permute-done | bytes 786464 | tf_op jit(solution)/shard_map/ppermute | solution.py:41
  170.3 6.7 %fusion.62 = f32[1536,1536]{1,0:T(8,128)} fusion(bf16[512,1536]{1,0:T(8,128)(2,1)S(1)} %add_convert_fusion.3, bf16[256,1536]{1,0:T(8,128)(2,1)} %collective-permute-done.15, bf16[256,1536]{1,0:T(8,128)(2,1)} %add_convert_fusion.6), kind=kOutput, calls=%fused_computation.156 | convolution fusion | flops 2419064832 | bytes 12582912 | tf_op jit(solution)/shard_map/dot_general | solution.py:29
  177.8 5.5 fusion.143
  183.5 2.6 fusion.141
  186.1 9.8 %add_convert_fusion.2 = (bf16[512,1536]{1,0:T(8,128)(2,1)S(1)}, f32[512,1536]{1,0:T(8,128)S(1)}) fusion(f32[512,1536]{1,0:T(8,128)S(1)} %fusion.141, bf16[512,1536]{1,0:T(8,128)(2,1)S(1)} %constant_dynamic-update-slice_fusion.19, bf16[1536,1536]{1,0:T(8,128)(2,1)S(1)} %bitcast.239), kind=kOutput, calls=%fused_computation.28 | convolution fusion | flops 2472542208 | bytes 14155776 | tf_op jit(solution)/shard_map/dot_general | solution.py:35
  196.7 2.6 convolution_convert_fusion.4
  199.9 5.3 add_convert_fusion.1
  207.8 5.5 add_convert_fusion
  217.6 18.7 %collective-permute-done.82 = bf16[2,192,1536]{2,1,0:T(8,128)(2,1)S(1)} collective-permute-done((bf16[2,192,1536]{2,1,0:T(8,128)(2,1)S(1)}, bf16[2,192,1536]{2,1,0:T(8,128)(2,1)S(1)}, u32[]{:S(2)}, u32[]{:S(2)}) %collective-permute-start.82) | collective-permute-done | bytes 1179680 | tf_op jit(solution)/shard_map/ppermute | solution.py:83
  241.7 3.4 convolution_convert_fusion.9
  253.3 4.1 multiply_reduce_fusion.3
  262.6 21.5 %collective-permute-done.35 = f32[128,384]{0,1:T(8,128)S(1)} collective-permute-done((f32[128,384]{0,1:T(8,128)S(1)}, f32[128,384]{0,1:T(8,128)S(1)}, u32[]{:S(2)}, u32[]{:S(2)}) %collective-permute-start.35) | collective-permute-done | bytes 196640 | tf_op jit(solution)/shard_map/ppermute | solution.py:41
  298.4 21.2 %collective-permute-done.83 = bf16[2,192,1536]{2,1,0:T(8,128)(2,1)S(1)} collective-permute-done((bf16[2,192,1536]{2,1,0:T(8,128)(2,1)S(1)}, bf16[2,192,1536]{2,1,0:T(8,128)(2,1)S(1)}, u32[]{:S(2)}, u32[]{:S(2)}) %collective-permute-start.83) | collective-permute-done | bytes 1179680 | tf_op jit(solution)/shard_map/ppermute | solution.py:83
  326.1 2.7 fusion.29
  330.8 5.8 copy.58
  336.6 2.9 dynamic-slice_bitcast_fusion.1
  339.5 2.6 collective-permute-done.90
  347.9 4.5 convolution_convert_fusion.11.grad_ref
  352.4 27.3 %self_backward.1 = (bf16[1024,384]{1,0:T(8,128)(2,1)}, bf16[1024,384]{1,0:T(8,128)(2,1)}, bf16[1024,384]{1,0:T(8,128)(2,1)}) custom-call(s32[1]{0:T(128)} %bitcast.id_ref, bf16[1024,1152]{1,0:T(8,128)(2,1)} %convolution_convert_fusion.1.q_ref.k_ref.v_ref, bf16[1024,1152]{1,0:T(8,128)(2,1)} %convolution_convert_fusion.1.q_ref.k_ref.v_ref, ...), custom_call_target="tpu_custom_call" | custom-call | flops 2516582400 | bytes 5505024 | tf_op jit(solution)/shard_map/self_backward/pallas_call | solution.py:223
  382.8 3.4 convolution_convert_fusion.2
  386.2 7.8 %convolution_convert_fusion = bf16[1536,1152]{1,0:T(8,128)(2,1)} fusion(bf16[1024,1152]{1,0:T(8,128)(2,1)S(1)} %constant_dynamic-update-slice_fusion.21, bf16[256,1536]{1,0:T(8,128)(2,1)S(1)} %copy-done.83, bf16[256,1536]{1,0:T(8,128)(2,1)} %collective-permute-done.1, bf16[256,1536]{1,0:T(8,128)(2,1)} %collective-permute-done, bf16[256,1536]{1,0:T(8,128)(2,1)} %fusion.47), kind=kOutput, calls=%fused_computation.3 | convolution fusion | flops 3638231040 | bytes 9043968 | tf_op jit(solution)/shard_map/dot_general | solution.py:29
  394.0 3.8 fusion.58
  397.8 3.3 convolution_convert_fusion.8
  405.5 4.4 collective-permute-start.91
  410.0 3.5 fusion.32
  415.0 4.4 copy.57
  421.4 5.4 convolution_convert_fusion.3
  429.3 2.5 collective-permute-done.86
  438.1 13.5 %collective-permute-start.84 = (bf16[2,192,1536]{2,1,0:T(8,128)(2,1)S(1)}, bf16[2,192,1536]{2,1,0:T(8,128)(2,1)S(1)}, u32[]{:S(2)}, u32[]{:S(2)}) collective-permute-start(bf16[2,192,1536]{2,1,0:T(8,128)(2,1)S(1)} %copy-done.42), channel_id=1, source_target_pairs={{0,8},{4,12},{8,16},{12,20},{16,24},{20,28},{1,9},{5,13},{9,17},{1... | collective-permute-start | bytes 3538952 | tf_op jit(solution)/shard_map/ppermute | solution.py:83
  451.7 11.5 %collective-permute-done.94 = bf16[192,1536]{1,0:T(8,128)(2,1)S(1)} collective-permute-done((bf16[192,1536]{1,0:T(8,128)(2,1)S(1)}, bf16[192,1536]{1,0:T(8,128)(2,1)S(1)}, u32[]{:S(2)}, u32[]{:S(2)}) %collective-permute-start.94) | collective-permute-done | bytes 589856 | tf_op jit(solution)/shard_map/ppermute | solution.py:83
  463.3 7.2 %collective-permute-done.57 = bf16[4,192,768]{2,1,0:T(8,128)(2,1)S(1)} collective-permute-done((bf16[4,192,768]{2,1,0:T(8,128)(2,1)S(1)}, bf16[4,192,768]{2,1,0:T(8,128)(2,1)S(1)}, u32[]{:S(2)}, u32[]{:S(2)}) %collective-permute-start.57) | collective-permute-done | bytes 1179680 | tf_op jit(solution)/shard_map/ppermute | solution.py:68
  475.8 7.3 %collective-permute-done.58 = bf16[192,768]{1,0:T(8,128)(2,1)S(1)} collective-permute-done((bf16[192,768]{1,0:T(8,128)(2,1)S(1)}, bf16[192,768]{1,0:T(8,128)(2,1)S(1)}, u32[]{:S(2)}, u32[]{:S(2)}) %collective-permute-start.58) | collective-permute-done | bytes 294944 | tf_op jit(solution)/shard_map/ppermute | solution.py:83
  486.7 14.1 %collective-permute-done.87 = bf16[2,192,1536]{2,1,0:T(8,128)(2,1)S(1)} collective-permute-done((bf16[2,192,1536]{2,1,0:T(8,128)(2,1)S(1)}, bf16[2,192,1536]{2,1,0:T(8,128)(2,1)S(1)}, u32[]{:S(2)}, u32[]{:S(2)}) %collective-permute-start.87) | collective-permute-done | bytes 1179680 | tf_op jit(solution)/shard_map/ppermute | solution.py:83
  503.4 17.8 %collective-permute-done.32 = bf16[256,1536]{1,0:T(8,128)(2,1)S(1)} collective-permute-done((bf16[256,1536]{1,0:T(8,128)(2,1)S(1)}, bf16[256,1536]{1,0:T(8,128)(2,1)S(1)}, u32[]{:S(2)}, u32[]{:S(2)}) %collective-permute-start.32) | collective-permute-done | bytes 786464 | tf_op jit(solution)/shard_map/ppermute | solution.py:41
  525.4 10.8 %collective-permute-done.28 = bf16[256,1536]{1,0:T(8,128)(2,1)S(1)} collective-permute-done((bf16[256,1536]{1,0:T(8,128)(2,1)S(1)}, bf16[256,1536]{1,0:T(8,128)(2,1)S(1)}, u32[]{:S(2)}, u32[]{:S(2)}) %collective-permute-start.28) | collective-permute-done | bytes 786464 | tf_op jit(solution)/shard_map/ppermute | solution.py:41
  536.2 3.0 multiply_reduce_fusion
  539.2 2.5 constant_dynamic-update-slice_fusion.25
  542.4 3.2 collective-permute-done.40
  552.3 2.7 collective-permute-start.42
  556.8 6.4 collective-permute-done.42
  564.2 8.2 %collective-permute-done.43 = f32[3072]{0:T(1024)S(1)} collective-permute-done((f32[3072]{0:T(1024)S(1)}, f32[3072]{0:T(1024)S(1)}, u32[]{:S(2)}, u32[]{:S(2)}) %collective-permute-start.43) | collective-permute-done | bytes 12320 | tf_op jit(solution)/shard_map/ppermute | solution.py:108
  575.1 4.1 collective-permute-done.68
  580.6 6.3 collective-permute-start.77
  588.2 4.6 collective-permute-start.60
  593.1 2.6 collective-permute-done.62
  597.7 4.6 collective-permute-start.63
  606.6 2.8 collective-permute-start.78
  612.4 13.8 %collective-permute-done.46 = bf16[192,1152]{1,0:T(8,128)(2,1)S(1)} collective-permute-done((bf16[192,1152]{1,0:T(8,128)(2,1)S(1)}, bf16[192,1152]{1,0:T(8,128)(2,1)S(1)}, u32[]{:S(2)}, u32[]{:S(2)}) %collective-permute-start.46) | collective-permute-done | bytes 442400 | tf_op jit(solution)/shard_map/ppermute | solution.py:83
  629.6 4.6 collective-permute-start.47
  634.2 7.1 %collective-permute-done.49 = bf16[192,1152]{1,0:T(8,128)(2,1)S(1)} collective-permute-done((bf16[192,1152]{1,0:T(8,128)(2,1)S(1)}, bf16[192,1152]{1,0:T(8,128)(2,1)S(1)}, u32[]{:S(2)}, u32[]{:S(2)}) %collective-permute-start.49) | collective-permute-done | bytes 442400 | tf_op jit(solution)/shard_map/ppermute | solution.py:83
  643.3 6.6 collective-permute-done.81
  650.9 3.7 collective-permute-done.50
  (514 shorter events, 183.3 us)
Async XLA Ops:
  6.6 19.6 %collective-permute-start.1 = (bf16[256,1536]{1,0:T(8,128)(2,1)}, bf16[256,1536]{1,0:T(8,128)(2,1)}, u32[]{:S(2)}, u32[]{:S(2)}) collective-permute-start(bf16[256,1536]{1,0:T(8,128)(2,1)} %fusion.47), channel_id=1, source_target_pairs={{0,2},{1,3},{2,0},{3,1},{4,6},{5,7},{6,4},{7,5},{8,10},{9,11},{10,... | collective-permute-start | bytes 2359304 | tf_op jit(solution)/shard_map/ppermute | solution.py:41
  8.1 27.1 %collective-permute-start = (bf16[256,1536]{1,0:T(8,128)(2,1)}, bf16[256,1536]{1,0:T(8,128)(2,1)}, u32[]{:S(2)}, u32[]{:S(2)}) collective-permute-start(bf16[256,1536]{1,0:T(8,128)(2,1)} %fusion.47), channel_id=1, source_target_pairs={{0,1},{1,0},{2,3},{3,2},{4,5},{5,4},{6,7},{7,6},{8,9},{9,8},{10,11... | collective-permute-start | bytes 2359304 | tf_op jit(solution)/shard_map/ppermute | solution.py:41
  30.4 37.8 %collective-permute-start.9 = (bf16[1536,384]{1,0:T(8,128)(2,1)}, bf16[1536,384]{1,0:T(8,128)(2,1)}, u32[]{:S(2)}, u32[]{:S(2)}) collective-permute-start(bf16[1536,384]{1,0:T(8,128)(2,1)} %param.29), channel_id=1, source_target_pairs={{0,1},{1,0},{2,3},{3,2},{4,5},{5,4},{6,7},{7,6},{8,9},{9,8},{10,11... | collective-permute-start | bytes 3538952 | tf_op jit(solution)/shard_map/ppermute | solution.py:41
  33.1 35.7 %collective-permute-start.10 = (bf16[1536,384]{1,0:T(8,128)(2,1)}, bf16[1536,384]{1,0:T(8,128)(2,1)}, u32[]{:S(2)}, u32[]{:S(2)}) collective-permute-start(bf16[1536,384]{1,0:T(8,128)(2,1)} %param.29), channel_id=1, source_target_pairs={{0,2},{1,3},{2,0},{3,1},{4,6},{5,7},{6,4},{7,5},{8,10},{9,11},{10,... | collective-permute-start | bytes 3538952 | tf_op jit(solution)/shard_map/ppermute | solution.py:41
  35.0 58.7 %collective-permute-start.12 = (bf16[384,1536]{1,0:T(8,128)(2,1)}, bf16[384,1536]{1,0:T(8,128)(2,1)}, u32[]{:S(2)}, u32[]{:S(2)}) collective-permute-start(bf16[384,1536]{1,0:T(8,128)(2,1)} %param.32), channel_id=1, source_target_pairs={{0,1},{1,0},{2,3},{3,2},{4,5},{5,4},{6,7},{7,6},{8,9},{9,8},{10,11... | collective-permute-start | bytes 3538952 | tf_op jit(solution)/shard_map/ppermute | solution.py:41
  35.2 51.7 %collective-permute-start.13 = (bf16[384,1536]{1,0:T(8,128)(2,1)}, bf16[384,1536]{1,0:T(8,128)(2,1)}, u32[]{:S(2)}, u32[]{:S(2)}) collective-permute-start(bf16[384,1536]{1,0:T(8,128)(2,1)} %param.32), channel_id=1, source_target_pairs={{0,2},{1,3},{2,0},{3,1},{4,6},{5,7},{6,4},{7,5},{8,10},{9,11},{10,... | collective-permute-start | bytes 3538952 | tf_op jit(solution)/shard_map/ppermute | solution.py:41
  62.6 26.8 %collective-permute-start.4 = (bf16[256,1536]{1,0:T(8,128)(2,1)}, bf16[256,1536]{1,0:T(8,128)(2,1)}, u32[]{:S(2)}, u32[]{:S(2)}) collective-permute-start(bf16[256,1536]{1,0:T(8,128)(2,1)} %slice.181), channel_id=1, source_target_pairs={{0,1},{1,0},{2,3},{3,2},{4,5},{5,4},{6,7},{7,6},{8,9},{9,8},{10,11... | collective-permute-start | bytes 2359304 | tf_op jit(solution)/shard_map/ppermute | solution.py:41
  68.3 30.4 %collective-permute-start.3 = (bf16[256,1536]{1,0:T(8,128)(2,1)S(1)}, bf16[256,1536]{1,0:T(8,128)(2,1)S(1)}, u32[]{:S(2)}, u32[]{:S(2)}) collective-permute-start(bf16[256,1536]{1,0:T(8,128)(2,1)S(1)} %slice.289), channel_id=1, source_target_pairs={{0,1},{1,0},{2,3},{3,2},{4,5},{5,4},{6,7},{7,6},{8,9},{9,8},{10,11... | collective-permute-start | bytes 2359304 | tf_op jit(solution)/shard_map/ppermute | solution.py:41
  68.8 44.8 %collective-permute-start.11 = (bf16[1536,384]{1,0:T(8,128)(2,1)}, bf16[1536,384]{1,0:T(8,128)(2,1)S(1)}, u32[]{:S(2)}, u32[]{:S(2)}) collective-permute-start(bf16[1536,384]{1,0:T(8,128)(2,1)} %collective-permute-done.10), channel_id=1, source_target_pairs={{0,1},{1,0},{2,3},{3,2},{4,5},{5,4},{6,7},{7,6},{8,9},{9,8},{10,11... | collective-permute-start | bytes 3538952 | tf_op jit(solution)/shard_map/ppermute | solution.py:41
  86.9 36.3 %collective-permute-start.14 = (bf16[384,1536]{1,0:T(8,128)(2,1)}, bf16[384,1536]{1,0:T(8,128)(2,1)}, u32[]{:S(2)}, u32[]{:S(2)}) collective-permute-start(bf16[384,1536]{1,0:T(8,128)(2,1)} %collective-permute-done.13), channel_id=1, source_target_pairs={{0,1},{1,0},{2,3},{3,2},{4,5},{5,4},{6,7},{7,6},{8,9},{9,8},{10,11... | collective-permute-start | bytes 3538952 | tf_op jit(solution)/shard_map/ppermute | solution.py:41
  90.6 20.0 %collective-permute-start.5 = (bf16[256,1536]{1,0:T(8,128)(2,1)S(1)}, bf16[256,1536]{1,0:T(8,128)(2,1)S(1)}, u32[]{:S(2)}, u32[]{:S(2)}) collective-permute-start(bf16[256,1536]{1,0:T(8,128)(2,1)S(1)} %slice_add_fusion.7), channel_id=1, source_target_pairs={{0,2},{1,3},{2,0},{3,1},{4,6},{5,7},{6,4},{7,5},{8,10},{9,11},{10,... | collective-permute-start | bytes 2359304 | tf_op jit(solution)/shard_map/ppermute | solution.py:41
  132.6 26.1 %collective-permute-start.17 = (bf16[256,1536]{1,0:T(8,128)(2,1)}, bf16[256,1536]{1,0:T(8,128)(2,1)S(1)}, u32[]{:S(2)}, u32[]{:S(2)}) collective-permute-start(bf16[256,1536]{1,0:T(8,128)(2,1)} %add_convert_fusion.6), channel_id=1, source_target_pairs={{0,2},{1,3},{2,0},{3,1},{4,6},{5,7},{6,4},{7,5},{8,10},{9,11},{10,... | collective-permute-start | bytes 2359304 | tf_op jit(solution)/shard_map/ppermute | solution.py:41
  133.2 36.9 %collective-permute-start.21 = (bf16[256,1536]{1,0:T(8,128)(2,1)S(1)}, bf16[256,1536]{1,0:T(8,128)(2,1)S(1)}, u32[]{:S(2)}, u32[]{:S(2)}) collective-permute-start(bf16[256,1536]{1,0:T(8,128)(2,1)S(1)} %copy-done.15), channel_id=1, source_target_pairs={{0,2},{1,3},{2,0},{3,1},{4,6},{5,7},{6,4},{7,5},{8,10},{9,11},{10,... | collective-permute-start | bytes 2359304 | tf_op jit(solution)/shard_map/ppermute | solution.py:41
  155.0 82.4 %collective-permute-start.20 = (bf16[256,1536]{1,0:T(8,128)(2,1)S(1)}, bf16[256,1536]{1,0:T(8,128)(2,1)S(1)}, u32[]{:S(2)}, u32[]{:S(2)}) collective-permute-start(bf16[256,1536]{1,0:T(8,128)(2,1)S(1)} %slice.287), channel_id=1, source_target_pairs={{0,1},{1,0},{2,3},{3,2},{4,5},{5,4},{6,7},{7,6},{8,9},{9,8},{10,11... | collective-permute-start | bytes 2359304 | tf_op jit(solution)/shard_map/ppermute | solution.py:41
  158.8 135.2 %collective-permute-start.70 = (bf16[256,1536]{1,0:T(8,128)(2,1)}, bf16[256,1536]{1,0:T(8,128)(2,1)}, u32[]{:S(2)}, u32[]{:S(2)}) collective-permute-start(bf16[256,1536]{1,0:T(8,128)(2,1)} %add_convert_fusion.7), channel_id=1, source_target_pairs={{0,2},{1,3},{2,0},{3,1},{4,6},{5,7},{6,4},{7,5},{8,10},{9,11},{10,... | collective-permute-start | bytes 2359304 | tf_op jit(solution)/shard_map/ppermute | solution.py:41
  159.3 24.0 %collective-permute-start.18 = (bf16[256,1536]{1,0:T(8,128)(2,1)S(1)}, bf16[256,1536]{1,0:T(8,128)(2,1)S(1)}, u32[]{:S(2)}, u32[]{:S(2)}) collective-permute-start(bf16[256,1536]{1,0:T(8,128)(2,1)S(1)} %collective-permute-done.17), channel_id=1, source_target_pairs={{0,1},{1,0},{2,3},{3,2},{4,5},{5,4},{6,7},{7,6},{8,9},{9,8},{10,11... | collective-permute-start | bytes 2359304 | tf_op jit(solution)/shard_map/ppermute | solution.py:41
  170.2 15.9 %collective-permute-start.22 = (bf16[256,1536]{1,0:T(8,128)(2,1)S(1)}, bf16[256,1536]{1,0:T(8,128)(2,1)S(1)}, u32[]{:S(2)}, u32[]{:S(2)}) collective-permute-start(bf16[256,1536]{1,0:T(8,128)(2,1)S(1)} %collective-permute-done.21), channel_id=1, source_target_pairs={{0,1},{1,0},{2,3},{3,2},{4,5},{5,4},{6,7},{7,6},{8,9},{9,8},{10,11... | collective-permute-start | bytes 2359304 | tf_op jit(solution)/shard_map/ppermute | solution.py:41
  206.5 29.8 %collective-permute-start.82 = (bf16[2,192,1536]{2,1,0:T(8,128)(2,1)S(1)}, bf16[2,192,1536]{2,1,0:T(8,128)(2,1)S(1)}, u32[]{:S(2)}, u32[]{:S(2)}) collective-permute-start(bf16[2,192,1536]{2,1,0:T(8,128)(2,1)S(1)} %get-tuple-element.69), channel_id=1, source_target_pairs={{0,8},{4,12},{1,9},{5,13},{2,10},{6,14},{3,11},{7,15}} | collective-permute-start | bytes 3538952 | tf_op jit(solution)/shard_map/ppermute | solution.py:83
  213.4 24.1 %collective-permute-start.24 = (bf16[256,1536]{1,0:T(8,128)(2,1)S(1)}, bf16[256,1536]{1,0:T(8,128)(2,1)S(1)}, u32[]{:S(2)}, u32[]{:S(2)}) collective-permute-start(bf16[256,1536]{1,0:T(8,128)(2,1)S(1)} %slice_add_fusion.6), channel_id=1, source_target_pairs={{0,2},{1,3},{2,0},{3,1},{4,6},{5,7},{6,4},{7,5},{8,10},{9,11},{10,... | collective-permute-start | bytes 2359304 | tf_op jit(solution)/shard_map/ppermute | solution.py:41
  216.1 78.5 %collective-permute-start.89 = (bf16[4,192,1536]{2,1,0:T(8,128)(2,1)}, bf16[4,192,1536]{2,1,0:T(8,128)(2,1)}, u32[]{:S(2)}, u32[]{:S(2)}) collective-permute-start(bf16[4,192,1536]{2,1,0:T(8,128)(2,1)} %dynamic-slice_bitcast_fusion), channel_id=1, source_target_pairs={{0,4},{4,0},{8,12},{12,8},{16,20},{20,16},{24,28},{28,24},{1,5},{5... | collective-permute-start | bytes 7077896 | tf_op jit(solution)/shard_map/ppermute | solution.py:68
  260.3 33.8 %collective-permute-start.25 = (bf16[256,1536]{1,0:T(8,128)(2,1)}, bf16[256,1536]{1,0:T(8,128)(2,1)}, u32[]{:S(2)}, u32[]{:S(2)}) collective-permute-start(bf16[256,1536]{1,0:T(8,128)(2,1)} %fusion.123), channel_id=1, source_target_pairs={{0,2},{1,3},{2,0},{3,1},{4,6},{5,7},{6,4},{7,5},{8,10},{9,11},{10,... | collective-permute-start | bytes 2359304 | tf_op jit(solution)/shard_map/ppermute | solution.py:41
  260.9 23.1 %collective-permute-start.35 = (f32[128,384]{0,1:T(8,128)S(1)}, f32[128,384]{0,1:T(8,128)S(1)}, u32[]{:S(2)}, u32[]{:S(2)}) collective-permute-start(f32[128,384]{0,1:T(8,128)S(1)} %fusion.92), channel_id=1, source_target_pairs={{0,2},{1,3},{2,0},{3,1},{4,6},{5,7},{6,4},{7,5},{8,10},{9,11},{10,... | collective-permute-start | bytes 589832 | tf_op jit(solution)/shard_map/ppermute | solution.py:41
  290.8 28.8 %collective-permute-start.83 = (bf16[2,192,1536]{2,1,0:T(8,128)(2,1)S(1)}, bf16[2,192,1536]{2,1,0:T(8,128)(2,1)S(1)}, u32[]{:S(2)}, u32[]{:S(2)}) collective-permute-start(bf16[2,192,1536]{2,1,0:T(8,128)(2,1)S(1)} %copy-done.41), channel_id=1, source_target_pairs={{0,8},{4,12},{8,16},{12,20},{1,9},{5,13},{9,17},{13,21},{2,10},{6,... | collective-permute-start | bytes 3538952 | tf_op jit(solution)/shard_map/ppermute | solution.py:83
  294.0 28.3 %collective-permute-start.69 = (bf16[256,1536]{1,0:T(8,128)(2,1)}, bf16[256,1536]{1,0:T(8,128)(2,1)S(1)}, u32[]{:S(2)}, u32[]{:S(2)}) collective-permute-start(bf16[256,1536]{1,0:T(8,128)(2,1)} %add_convert_fusion.7), channel_id=1, source_target_pairs={{0,1},{1,0},{2,3},{3,2},{4,5},{5,4},{6,7},{7,6},{8,9},{9,8},{10,11... | collective-permute-start | bytes 2359304 | tf_op jit(solution)/shard_map/ppermute | solution.py:41
  294.0 28.9 %collective-permute-start.71 = (bf16[256,1536]{1,0:T(8,128)(2,1)}, bf16[256,1536]{1,0:T(8,128)(2,1)S(1)}, u32[]{:S(2)}, u32[]{:S(2)}) collective-permute-start(bf16[256,1536]{1,0:T(8,128)(2,1)} %collective-permute-done.70), channel_id=1, source_target_pairs={{0,1},{1,0},{2,3},{3,2},{4,5},{5,4},{6,7},{7,6},{8,9},{9,8},{10,11... | collective-permute-start | bytes 2359304 | tf_op jit(solution)/shard_map/ppermute | solution.py:41
  294.6 28.4 %collective-permute-start.74 = (bf16[256,384]{0,1:T(8,128)(2,1)S(1)}, bf16[256,384]{0,1:T(8,128)(2,1)S(1)}, u32[]{:S(2)}, u32[]{:S(2)}) collective-permute-start(bf16[256,384]{0,1:T(8,128)(2,1)S(1)} %get-tuple-element.100), channel_id=1, source_target_pairs={{0,3},{1,2},{2,1},{3,0},{4,7},{5,6},{6,5},{7,4},{8,11},{9,10},{10,... | collective-permute-start | bytes 589832 | tf_op jit(solution)/shard_map/ppermute | solution.py:41
  296.8 27.7 %collective-permute-start.73 = (bf16[256,384]{0,1:T(8,128)(2,1)S(1)}, bf16[256,384]{0,1:T(8,128)(2,1)S(1)}, u32[]{:S(2)}, u32[]{:S(2)}) collective-permute-start(bf16[256,384]{0,1:T(8,128)(2,1)S(1)} %get-tuple-element.101), channel_id=1, source_target_pairs={{0,2},{1,3},{2,0},{3,1},{4,6},{5,7},{6,4},{7,5},{8,10},{9,11},{10,... | collective-permute-start | bytes 589832 | tf_op jit(solution)/shard_map/ppermute | solution.py:41
  322.3 78.8 %collective-permute-start.56 = (bf16[256,384]{0,1:T(8,128)(2,1)}, bf16[256,384]{0,1:T(8,128)(2,1)}, u32[]{:S(2)}, u32[]{:S(2)}) collective-permute-start(bf16[256,384]{0,1:T(8,128)(2,1)} %get-tuple-element.104), channel_id=1, source_target_pairs={{0,3},{1,2},{2,1},{3,0},{4,7},{5,6},{6,5},{7,4},{8,11},{9,10},{10,... | collective-permute-start | bytes 589832 | tf_op jit(solution)/shard_map/ppermute | solution.py:41
  323.0 21.9 %collective-permute-start.29 = (bf16[256,1536]{1,0:T(8,128)(2,1)}, bf16[256,1536]{1,0:T(8,128)(2,1)}, u32[]{:S(2)}, u32[]{:S(2)}) collective-permute-start(bf16[256,1536]{1,0:T(8,128)(2,1)} %fusion.123), channel_id=1, source_target_pairs={{0,1},{1,0},{2,3},{3,2},{4,5},{5,4},{6,7},{7,6},{8,9},{9,8},{10,11... | collective-permute-start | bytes 2359304 | tf_op jit(solution)/shard_map/ppermute | solution.py:41
  323.0 24.4 %collective-permute-start.52 = (bf16[256,1536]{1,0:T(8,128)(2,1)}, bf16[256,1536]{1,0:T(8,128)(2,1)}, u32[]{:S(2)}, u32[]{:S(2)}) collective-permute-start(bf16[256,1536]{1,0:T(8,128)(2,1)} %fusion.64), channel_id=1, source_target_pairs={{0,2},{1,3},{2,0},{3,1},{4,6},{5,7},{6,4},{7,5},{8,10},{9,11},{10,... | collective-permute-start | bytes 2359304 | tf_op jit(solution)/shard_map/ppermute | solution.py:41
  324.5 17.6 %collective-permute-start.90 = (bf16[192,1536]{1,0:T(8,128)(2,1)}, bf16[192,1536]{1,0:T(8,128)(2,1)}, u32[]{:S(2)}, u32[]{:S(2)}) collective-permute-start(bf16[192,1536]{1,0:T(8,128)(2,1)} %get-tuple-element.76), channel_id=1, source_target_pairs={{0,8},{4,12},{1,9},{5,13},{2,10},{6,14},{3,11},{7,15}} | collective-permute-start | bytes 1769480 | tf_op jit(solution)/shard_map/ppermute | solution.py:83
  325.8 21.5 %collective-permute-start.26 = (bf16[256,1536]{1,0:T(8,128)(2,1)}, bf16[256,1536]{1,0:T(8,128)(2,1)}, u32[]{:S(2)}, u32[]{:S(2)}) collective-permute-start(bf16[256,1536]{1,0:T(8,128)(2,1)} %collective-permute-done.25), channel_id=1, source_target_pairs={{0,1},{1,0},{2,3},{3,2},{4,5},{5,4},{6,7},{7,6},{8,9},{9,8},{10,11... | collective-permute-start | bytes 2359304 | tf_op jit(solution)/shard_map/ppermute | solution.py:41
  342.1 59.1 %collective-permute-start.55 = (bf16[256,384]{0,1:T(8,128)(2,1)}, bf16[256,384]{0,1:T(8,128)(2,1)}, u32[]{:S(2)}, u32[]{:S(2)}) collective-permute-start(bf16[256,384]{0,1:T(8,128)(2,1)} %get-tuple-element.105), channel_id=1, source_target_pairs={{0,2},{1,3},{2,0},{3,1},{4,6},{5,7},{6,4},{7,5},{8,10},{9,11},{10,... | collective-permute-start | bytes 589832 | tf_op jit(solution)/shard_map/ppermute | solution.py:41
  344.8 57.7 %collective-permute-start.54 = (bf16[256,384]{0,1:T(8,128)(2,1)}, bf16[256,384]{0,1:T(8,128)(2,1)}, u32[]{:S(2)}, u32[]{:S(2)}) collective-permute-start(bf16[256,384]{0,1:T(8,128)(2,1)} %get-tuple-element.106), channel_id=1, source_target_pairs={{0,1},{1,0},{2,3},{3,2},{4,5},{5,4},{6,7},{7,6},{8,9},{9,8},{10,11... | collective-permute-start | bytes 589832 | tf_op jit(solution)/shard_map/ppermute | solution.py:41
  347.4 56.7 %collective-permute-start.51 = (bf16[256,1536]{1,0:T(8,128)(2,1)}, bf16[256,1536]{1,0:T(8,128)(2,1)}, u32[]{:S(2)}, u32[]{:S(2)}) collective-permute-start(bf16[256,1536]{1,0:T(8,128)(2,1)} %fusion.64), channel_id=1, source_target_pairs={{0,1},{1,0},{2,3},{3,2},{4,5},{5,4},{6,7},{7,6},{8,9},{9,8},{10,11... | collective-permute-start | bytes 2359304 | tf_op jit(solution)/shard_map/ppermute | solution.py:41
  347.4 58.1 %collective-permute-start.53 = (bf16[256,1536]{1,0:T(8,128)(2,1)}, bf16[256,1536]{1,0:T(8,128)(2,1)}, u32[]{:S(2)}, u32[]{:S(2)}) collective-permute-start(bf16[256,1536]{1,0:T(8,128)(2,1)} %collective-permute-done.52), channel_id=1, source_target_pairs={{0,1},{1,0},{2,3},{3,2},{4,5},{5,4},{6,7},{7,6},{8,9},{9,8},{10,11... | collective-permute-start | bytes 2359304 | tf_op jit(solution)/shard_map/ppermute | solution.py:41
  401.1 124.1 %collective-permute-start.16 = (bf16[256,1536]{1,0:T(8,128)(2,1)}, bf16[256,1536]{1,0:T(8,128)(2,1)}, u32[]{:S(2)}, u32[]{:S(2)}) collective-permute-start(bf16[256,1536]{1,0:T(8,128)(2,1)} %slice.288), channel_id=1, source_target_pairs={{0,1},{1,0},{2,3},{3,2},{4,5},{5,4},{6,7},{7,6},{8,9},{9,8},{10,11... | collective-permute-start | bytes 2359304 | tf_op jit(solution)/shard_map/ppermute | solution.py:41
  401.2 30.6 %collective-permute-start.86 = (bf16[2,192,1536]{2,1,0:T(8,128)(2,1)}, bf16[2,192,1536]{2,1,0:T(8,128)(2,1)}, u32[]{:S(2)}, u32[]{:S(2)}) collective-permute-start(bf16[2,192,1536]{2,1,0:T(8,128)(2,1)} %get-tuple-element.68), channel_id=1, source_target_pairs={{24,16},{28,20},{16,8},{20,12},{25,17},{29,21},{17,9},{21,13},{26,... | collective-permute-start | bytes 3538952 | tf_op jit(solution)/shard_map/ppermute | solution.py:83
  402.6 30.7 %collective-permute-start.93 = (bf16[192,1536]{1,0:T(8,128)(2,1)}, bf16[192,1536]{1,0:T(8,128)(2,1)}, u32[]{:S(2)}, u32[]{:S(2)}) collective-permute-start(bf16[192,1536]{1,0:T(8,128)(2,1)} %get-tuple-element.77), channel_id=1, source_target_pairs={{24,16},{28,20},{25,17},{29,21},{26,18},{30,22},{27,19},{31,23}} | collective-permute-start | bytes 1769480 | tf_op jit(solution)/shard_map/ppermute | solution.py:83
  404.0 68.6 %collective-permute-start.75 = (bf16[4,192,1152]{2,1,0:T(8,128)(2,1)}, bf16[4,192,1152]{2,1,0:T(8,128)(2,1)}, u32[]{:S(2)}, u32[]{:S(2)}) collective-permute-start(bf16[4,192,1152]{2,1,0:T(8,128)(2,1)} %dynamic-slice_bitcast_fusion.1), channel_id=1, source_target_pairs={{0,4},{4,0},{8,12},{12,8},{16,20},{20,16},{24,28},{28,24},{1,5},{5... | collective-permute-start | bytes 5308424 | tf_op jit(solution)/shard_map/ppermute | solution.py:68
  405.5 28.3 %collective-permute-start.91 = (bf16[192,1536]{1,0:T(8,128)(2,1)}, bf16[192,1536]{1,0:T(8,128)(2,1)}, u32[]{:S(2)}, u32[]{:S(2)}) collective-permute-start(bf16[192,1536]{1,0:T(8,128)(2,1)} %bitcast_add_fusion.10), channel_id=1, source_target_pairs={{0,8},{4,12},{8,16},{12,20},{1,9},{5,13},{9,17},{13,21},{2,10},{6,... | collective-permute-start | bytes 1769480 | tf_op jit(solution)/shard_map/ppermute | solution.py:83
  433.8 36.7 %collective-permute-start.57 = (bf16[4,192,768]{2,1,0:T(8,128)(2,1)S(1)}, bf16[4,192,768]{2,1,0:T(8,128)(2,1)S(1)}, u32[]{:S(2)}, u32[]{:S(2)}) collective-permute-start(bf16[4,192,768]{2,1,0:T(8,128)(2,1)S(1)} %dynamic-slice_bitcast_fusion.5), channel_id=1, source_target_pairs={{0,4},{4,0},{8,12},{12,8},{16,20},{20,16},{24,28},{28,24},{1,5},{5... | collective-permute-start | bytes 3538952 | tf_op jit(solution)/shard_map/ppermute | solution.py:68
  436.7 26.6 %collective-permute-start.94 = (bf16[192,1536]{1,0:T(8,128)(2,1)S(1)}, bf16[192,1536]{1,0:T(8,128)(2,1)S(1)}, u32[]{:S(2)}, u32[]{:S(2)}) collective-permute-start(bf16[192,1536]{1,0:T(8,128)(2,1)S(1)} %get-tuple-element.75), channel_id=1, source_target_pairs={{24,16},{28,20},{16,8},{20,12},{25,17},{29,21},{17,9},{21,13},{26,... | collective-permute-start | bytes 1769480 | tf_op jit(solution)/shard_map/ppermute | solution.py:83
  438.1 46.5 %collective-permute-start.84 = (bf16[2,192,1536]{2,1,0:T(8,128)(2,1)S(1)}, bf16[2,192,1536]{2,1,0:T(8,128)(2,1)S(1)}, u32[]{:S(2)}, u32[]{:S(2)}) collective-permute-start(bf16[2,192,1536]{2,1,0:T(8,128)(2,1)S(1)} %copy-done.42), channel_id=1, source_target_pairs={{0,8},{4,12},{8,16},{12,20},{16,24},{20,28},{1,9},{5,13},{9,17},{1... | collective-permute-start | bytes 3538952 | tf_op jit(solution)/shard_map/ppermute | solution.py:83
  463.2 38.6 %collective-permute-start.30 = (bf16[256,1536]{1,0:T(8,128)(2,1)S(1)}, bf16[256,1536]{1,0:T(8,128)(2,1)S(1)}, u32[]{:S(2)}, u32[]{:S(2)}) collective-permute-start(bf16[256,1536]{1,0:T(8,128)(2,1)S(1)} %slice.286), channel_id=1, source_target_pairs={{0,1},{1,0},{2,3},{3,2},{4,5},{5,4},{6,7},{7,6},{8,9},{9,8},{10,11... | collective-permute-start | bytes 2359304 | tf_op jit(solution)/shard_map/ppermute | solution.py:41
  470.5 30.3 %collective-permute-start.87 = (bf16[2,192,1536]{2,1,0:T(8,128)(2,1)S(1)}, bf16[2,192,1536]{2,1,0:T(8,128)(2,1)S(1)}, u32[]{:S(2)}, u32[]{:S(2)}) collective-permute-start(bf16[2,192,1536]{2,1,0:T(8,128)(2,1)S(1)} %bitcast_add_fusion.4), channel_id=1, source_target_pairs={{24,16},{28,20},{16,8},{20,12},{8,0},{12,4},{25,17},{29,21},{17,9}... | collective-permute-start | bytes 3538952 | tf_op jit(solution)/shard_map/ppermute | solution.py:83
  483.1 105.1 %collective-permute-start.44 = (bf16[4,192,1152]{2,1,0:T(8,128)(2,1)S(1)}, bf16[4,192,1152]{2,1,0:T(8,128)(2,1)S(1)}, u32[]{:S(2)}, u32[]{:S(2)}) collective-permute-start(bf16[4,192,1152]{2,1,0:T(8,128)(2,1)S(1)} %dynamic-slice_bitcast_fusion.2), channel_id=1, source_target_pairs={{0,4},{4,0},{8,12},{12,8},{16,20},{20,16},{24,28},{28,24},{1,5},{5... | collective-permute-start | bytes 5308424 | tf_op jit(solution)/shard_map/ppermute | solution.py:68
  484.7 67.6 %collective-permute-start.92 = (bf16[192,1536]{1,0:T(8,128)(2,1)S(1)}, bf16[192,1536]{1,0:T(8,128)(2,1)S(1)}, u32[]{:S(2)}, u32[]{:S(2)}) collective-permute-start(bf16[192,1536]{1,0:T(8,128)(2,1)S(1)} %get-tuple-element.74), channel_id=1, source_target_pairs={{0,8},{4,12},{8,16},{12,20},{16,24},{20,28},{1,9},{5,13},{9,17},{1... | collective-permute-start | bytes 1769480 | tf_op jit(solution)/shard_map/ppermute | solution.py:83
  500.8 20.4 %collective-permute-start.32 = (bf16[256,1536]{1,0:T(8,128)(2,1)S(1)}, bf16[256,1536]{1,0:T(8,128)(2,1)S(1)}, u32[]{:S(2)}, u32[]{:S(2)}) collective-permute-start(bf16[256,1536]{1,0:T(8,128)(2,1)S(1)} %slice_add_fusion.4), channel_id=1, source_target_pairs={{0,2},{1,3},{2,0},{3,1},{4,6},{5,7},{6,4},{7,5},{8,10},{9,11},{10,... | collective-permute-start | bytes 2359304 | tf_op jit(solution)/shard_map/ppermute | solution.py:41
  501.8 34.3 %collective-permute-start.28 = (bf16[256,1536]{1,0:T(8,128)(2,1)S(1)}, bf16[256,1536]{1,0:T(8,128)(2,1)S(1)}, u32[]{:S(2)}, u32[]{:S(2)}) collective-permute-start(bf16[256,1536]{1,0:T(8,128)(2,1)S(1)} %slice_add_fusion.5), channel_id=1, source_target_pairs={{0,2},{1,3},{2,0},{3,1},{4,6},{5,7},{6,4},{7,5},{8,10},{9,11},{10,... | collective-permute-start | bytes 2359304 | tf_op jit(solution)/shard_map/ppermute | solution.py:41
  521.2 33.8 %collective-permute-start.95 = (bf16[192,1536]{1,0:T(8,128)(2,1)S(1)}, bf16[192,1536]{1,0:T(8,128)(2,1)S(1)}, u32[]{:S(2)}, u32[]{:S(2)}) collective-permute-start(bf16[192,1536]{1,0:T(8,128)(2,1)S(1)} %bitcast_add_fusion.9), channel_id=1, source_target_pairs={{24,16},{28,20},{16,8},{20,12},{8,0},{12,4},{25,17},{29,21},{17,9}... | collective-permute-start | bytes 1769480 | tf_op jit(solution)/shard_map/ppermute | solution.py:83
  525.3 16.5 %collective-permute-start.39 = (f32[3072]{0:T(1024)S(1)}, f32[3072]{0:T(1024)S(1)}, u32[]{:S(2)}, u32[]{:S(2)}) collective-permute-start(f32[3072]{0:T(1024)S(1)} %pad_maximum_fusion.13), channel_id=1, source_target_pairs={{0,1},{1,0},{2,3},{3,2},{4,5},{5,4},{6,7},{7,6},{8,9},{9,8},{10,11... | collective-permute-start | bytes 36872 | tf_op jit(solution)/shard_map/ppermute | solution.py:41
  549.4 31.2 %collective-permute-start.61 = (bf16[192,768]{1,0:T(8,128)(2,1)S(1)}, bf16[192,768]{1,0:T(8,128)(2,1)S(1)}, u32[]{:S(2)}, u32[]{:S(2)}) collective-permute-start(bf16[192,768]{1,0:T(8,128)(2,1)S(1)} %get-tuple-element.92), channel_id=1, source_target_pairs={{24,16},{28,20},{25,17},{29,21},{26,18},{30,22},{27,19},{31,23}} | collective-permute-start | bytes 884744 | tf_op jit(solution)/shard_map/ppermute | solution.py:83
  563.3 33.8 %collective-permute-start.79 = (bf16[192,1152]{1,0:T(8,128)(2,1)S(1)}, bf16[192,1152]{1,0:T(8,128)(2,1)S(1)}, u32[]{:S(2)}, u32[]{:S(2)}) collective-permute-start(bf16[192,1152]{1,0:T(8,128)(2,1)S(1)} %get-tuple-element.81), channel_id=1, source_target_pairs={{24,16},{28,20},{25,17},{29,21},{26,18},{30,22},{27,19},{31,23}} | collective-permute-start | bytes 1327112 | tf_op jit(solution)/shard_map/ppermute | solution.py:83
  579.2 23.2 %collective-permute-start.88 = (bf16[1,192,1536]{2,1,0:T(8,128)(2,1)S(1)}, bf16[1,192,1536]{2,1,0:T(8,128)(2,1)S(1)}, u32[]{:S(2)}, u32[]{:S(2)}) collective-permute-start(bf16[1,192,1536]{2,1,0:T(8,128)(2,1)S(1)} %dynamic-slice_convert_fusion), channel_id=1, source_target_pairs={{0,4},{4,0},{8,12},{12,8},{16,20},{20,16},{24,28},{28,24},{1,5},{5... | collective-permute-start | bytes 1769480 | tf_op jit(solution)/shard_map/ppermute | solution.py:68
  580.6 17.2 %collective-permute-start.77 = (bf16[192,1152]{1,0:T(8,128)(2,1)S(1)}, bf16[192,1152]{1,0:T(8,128)(2,1)S(1)}, u32[]{:S(2)}, u32[]{:S(2)}) collective-permute-start(bf16[192,1152]{1,0:T(8,128)(2,1)S(1)} %bitcast_add_fusion.14), channel_id=1, source_target_pairs={{0,8},{4,12},{8,16},{12,20},{1,9},{5,13},{9,17},{13,21},{2,10},{6,... | collective-permute-start | bytes 1327112 | tf_op jit(solution)/shard_map/ppermute | solution.py:83
  588.2 21.3 %collective-permute-start.60 = (bf16[192,768]{1,0:T(8,128)(2,1)S(1)}, bf16[192,768]{1,0:T(8,128)(2,1)S(1)}, u32[]{:S(2)}, u32[]{:S(2)}) collective-permute-start(bf16[192,768]{1,0:T(8,128)(2,1)S(1)} %get-tuple-element.89), channel_id=1, source_target_pairs={{0,8},{4,12},{8,16},{12,20},{16,24},{20,28},{1,9},{5,13},{9,17},{1... | collective-permute-start | bytes 884744 | tf_op jit(solution)/shard_map/ppermute | solution.py:83
  597.0 15.4 %collective-permute-start.48 = (bf16[192,1152]{1,0:T(8,128)(2,1)S(1)}, bf16[192,1152]{1,0:T(8,128)(2,1)S(1)}, u32[]{:S(2)}, u32[]{:S(2)}) collective-permute-start(bf16[192,1152]{1,0:T(8,128)(2,1)S(1)} %get-tuple-element.85), channel_id=1, source_target_pairs={{24,16},{28,20},{25,17},{29,21},{26,18},{30,22},{27,19},{31,23}} | collective-permute-start | bytes 1327112 | tf_op jit(solution)/shard_map/ppermute | solution.py:83
  602.4 25.2 %collective-permute-start.80 = (bf16[192,1152]{1,0:T(8,128)(2,1)S(1)}, bf16[192,1152]{1,0:T(8,128)(2,1)S(1)}, u32[]{:S(2)}, u32[]{:S(2)}) collective-permute-start(bf16[192,1152]{1,0:T(8,128)(2,1)S(1)} %get-tuple-element.79), channel_id=1, source_target_pairs={{24,16},{28,20},{16,8},{20,12},{25,17},{29,21},{17,9},{21,13},{26,... | collective-permute-start | bytes 1327112 | tf_op jit(solution)/shard_map/ppermute | solution.py:83
  606.6 36.6 %collective-permute-start.78 = (bf16[192,1152]{1,0:T(8,128)(2,1)S(1)}, bf16[192,1152]{1,0:T(8,128)(2,1)S(1)}, u32[]{:S(2)}, u32[]{:S(2)}) collective-permute-start(bf16[192,1152]{1,0:T(8,128)(2,1)S(1)} %get-tuple-element.78), channel_id=1, source_target_pairs={{0,8},{4,12},{8,16},{12,20},{16,24},{20,28},{1,9},{5,13},{9,17},{1... | collective-permute-start | bytes 1327112 | tf_op jit(solution)/shard_map/ppermute | solution.py:83
  609.5 16.7 %collective-permute-start.46 = (bf16[192,1152]{1,0:T(8,128)(2,1)S(1)}, bf16[192,1152]{1,0:T(8,128)(2,1)S(1)}, u32[]{:S(2)}, u32[]{:S(2)}) collective-permute-start(bf16[192,1152]{1,0:T(8,128)(2,1)S(1)} %bitcast_add_fusion.18), channel_id=1, source_target_pairs={{0,8},{4,12},{8,16},{12,20},{1,9},{5,13},{9,17},{13,21},{2,10},{6,... | collective-permute-start | bytes 1327112 | tf_op jit(solution)/shard_map/ppermute | solution.py:83
  626.3 14.9 %collective-permute-start.49 = (bf16[192,1152]{1,0:T(8,128)(2,1)S(1)}, bf16[192,1152]{1,0:T(8,128)(2,1)S(1)}, u32[]{:S(2)}, u32[]{:S(2)}) collective-permute-start(bf16[192,1152]{1,0:T(8,128)(2,1)S(1)} %get-tuple-element.83), channel_id=1, source_target_pairs={{24,16},{28,20},{16,8},{20,12},{25,17},{29,21},{17,9},{21,13},{26,... | collective-permute-start | bytes 1327112 | tf_op jit(solution)/shard_map/ppermute | solution.py:83
  627.7 22.1 %collective-permute-start.81 = (bf16[192,1152]{1,0:T(8,128)(2,1)S(1)}, bf16[192,1152]{1,0:T(8,128)(2,1)S(1)}, u32[]{:S(2)}, u32[]{:S(2)}) collective-permute-start(bf16[192,1152]{1,0:T(8,128)(2,1)S(1)} %bitcast_add_fusion.13), channel_id=1, source_target_pairs={{24,16},{28,20},{16,8},{20,12},{8,0},{12,4},{25,17},{29,21},{17,9}... | collective-permute-start | bytes 1327112 | tf_op jit(solution)/shard_map/ppermute | solution.py:83
  629.6 21.3 %collective-permute-start.47 = (bf16[192,1152]{1,0:T(8,128)(2,1)S(1)}, bf16[192,1152]{1,0:T(8,128)(2,1)S(1)}, u32[]{:S(2)}, u32[]{:S(2)}) collective-permute-start(bf16[192,1152]{1,0:T(8,128)(2,1)S(1)} %get-tuple-element.82), channel_id=1, source_target_pairs={{0,8},{4,12},{8,16},{12,20},{16,24},{20,28},{1,9},{5,13},{9,17},{1... | collective-permute-start | bytes 1327112 | tf_op jit(solution)/shard_map/ppermute | solution.py:83
  (130 other events, 1268.7 us)

commit v3 on v2

--- a/solution.py
+++ b/solution.py
@@ -51,6 +51,19 @@
     return near_own.astype(jnp.float32) + exchange(near_other, 1) + over_link
 
 
+def gather_weight(values, axis):
+    if lax.axis_size("dp") != 8:
+        return jnp.concatenate(gather_relative(values), axis=axis)
+    own_y = lax.axis_index("dp") % 2
+    half = values.shape[0] // 2
+    first = exchange(lax.dynamic_slice_in_dim(values, own_y * half, half, 0), 2)
+    second = swap_y(first)
+    far = jnp.concatenate(
+        [jnp.where(own_y == 0, first, second), jnp.where(own_y == 0, second, first)]
+    )
+    return jnp.concatenate([values, exchange(values, 1), far, exchange(far, 1)], axis=axis)
+
+
 def swap_relative(blocks):
     return [blocks[0]] + [exchange(blocks[flip], flip) for flip in (1, 2, 3)]
 
@@ -58,7 +71,8 @@
 def scatter_product(far_pair, near_pair, own_rows):
     far_part = far_pair().astype(jnp.bfloat16)
     mine, other = far_part[:own_rows], far_part[own_rows:]
-    over_link = exchange(mine + exchange(other, 1), 2)
+    both_mine = mine + exchange(other, 1)
+    over_link = exchange(both_mine, 2)
     near_part = near_pair()
     near_other = exchange(near_part[own_rows:].astype(jnp.bfloat16), 1)
     return near_part[:own_rows] + near_other + over_link
@@ -68,35 +82,53 @@
     return lax.ppermute(values, "dp", [(i, i ^ 1) for i in range(8)])
 
 
-def sum_line(kept):
+def sum_line(kept, axis):
     own_z = lax.axis_index("dp") // 2
-    total = lax.dynamic_index_in_dim(kept, own_z, 0, keepdims=False).astype(jnp.float32)
-    carried = {}
+    total = lax.dynamic_index_in_dim(kept, own_z, axis, keepdims=False).astype(jnp.float32)
+    carried = None
     for step in range(1, 4):
+        blocks = []
         for sign in (1, -1):
             target = jnp.clip(own_z + sign * (4 - step), 0, 3)
-            block = lax.dynamic_index_in_dim(kept, target, 0, keepdims=False)
-            if step > 1:
-                block = block + carried[sign]
+            blocks.append(lax.dynamic_index_in_dim(kept, target, axis, keepdims=False))
+        if carried is not None:
+            carried = lax.optimization_barrier(carried)
+            blocks = [block + held for block, held in zip(blocks, carried)]
+        blocks = lax.optimization_barrier(tuple(blocks))
+        carried = []
+        for block, sign in zip(blocks, (1, -1)):
             senders = range(step) if sign > 0 else range(3, 3 - step, -1)
             pairs = [(2 * z + y, 2 * (z + sign) + y) for z in senders for y in range(2)]
-            carried[sign] = lax.ppermute(block, "dp", pairs)
-    return total + carried[1] + carried[-1]
-
-
-def sum_clips(part, line_first=False):
+            carried.append(lax.ppermute(block, "dp", pairs))
+        carried = tuple(carried)
+    return total + carried[0] + carried[1]
+
+
+def sum_clips(parts, line_first=False):
     size = lax.axis_size("dp")
-    part = part.astype(jnp.bfloat16)
+    parts = [part.astype(jnp.bfloat16) for part in parts]
     if size != 8:
-        return lax.psum_scatter(part, "dp", scatter_dimension=0, tiled=True).astype(jnp.float32)
+        return jnp.stack(
+            [
+                lax.psum_scatter(part, "dp", scatter_dimension=0, tiled=True).astype(jnp.float32)
+                for part in parts
+            ]
+        )
     own_y = lax.axis_index("dp") % 2
-    halves = part.reshape(4, 2, part.shape[0] // 8, part.shape[1])
+    rows, width = parts[0].shape[0] // 8, parts[0].shape[1]
     if line_first:
-        halves = sum_line(halves)[None]
-    sent = lax.dynamic_index_in_dim(halves, 1 - own_y, 1, keepdims=False).astype(jnp.bfloat16)
-    kept = lax.dynamic_index_in_dim(halves, own_y, 1, keepdims=False)
-    kept = kept + swap_y(sent)
-    return kept[0] if line_first else sum_line(kept)
+        halves = [sum_line(parts[0].reshape(4, 2, rows, width), 0)[None]]
+    else:
+        halves = [part.reshape(4, 2, rows, width) for part in parts]
+
+    def pick(place, kind):
+        return jnp.stack(
+            [lax.dynamic_index_in_dim(half, place, 1, keepdims=False).astype(kind) for half in halves]
+        )
+
+    other = swap_y(pick(1 - own_y, jnp.bfloat16))
+    kept = pick(own_y, halves[0].dtype) + other
+    return kept[0] if line_first else sum_line(kept, 1)
 
 
 def sum_everywhere(values):
@@ -104,7 +136,7 @@
         return lax.psum(values, ("dp", "tensor"))
     for flip in (1, 2):
         values = values + exchange(values, flip)
-    for flip in (1, 2, 4):
+    for flip in (2, 4, 1):
         values = values + lax.ppermute(values, "dp", [(i, i ^ flip) for i in range(8)])
     return values
 
@@ -327,8 +359,8 @@
         own_rows,
     )
 
-    c_q_full = jnp.concatenate(gather_relative(after(c_q, one[2])), axis=1)
-    c_o_full = jnp.concatenate(gather_relative(after(c_o, one[2])), axis=0)
+    c_q_full = gather_weight(after(c_q, one[2]), 1)
+    c_o_full = gather_weight(after(c_o, one[2]), 0)
     text_rows = text_states.reshape(clip_count * text_len, model_width)
     text_kv = after(
         jnp.concatenate([product(text_rows, c_k), product(text_rows, c_v)]).astype(low), one[2]
@@ -336,7 +368,7 @@
     text_kv = jnp.concatenate(gather_relative(text_kv), axis=1)
     text_keys = split_heads(text_kv[:text_len], text_len)
     text_values = split_heads(text_kv[text_len:], text_len)
-    grad_rows = gather_relative(after(out_cotangent, c_o_full))
+    grad_rows = gather_relative(after(out_cotangent, branch_one))
     grad_near = jnp.concatenate(grad_rows[:2])
     grad_far = jnp.concatenate(grad_rows[2:])
 
@@ -397,10 +429,10 @@
         lambda: contract_cols(grad_qkv[: 2 * own_rows], w_qkv),
         own_rows,
     )
-    w_out_grad = sum_clips(w_out_part).T
-    w_in_grad = sum_clips(w_in_part, line_first=True)
+    w_out_grad = sum_clips([w_out_part])[0].T
+    w_in_grad = sum_clips([w_in_part], line_first=True)[0]
     w_qkv_part = contract_rows(rows_one, grad_qkv)
-    qkv_grad = sum_clips(w_qkv_part)
+    qkv_grad = sum_clips([w_qkv_part])[0]
     w_q_grad, w_k_grad, w_v_grad = jnp.split(qkv_grad, 3, axis=1)
     norm_value, norm_back = jax.vjp(layer_norm, stream, ln1_gain, ln1_bias)
     back_rows, ln1_gain_part, ln1_bias_part = norm_back(grad_normed_one)
@@ -412,33 +444,22 @@
     rows_two = jnp.concatenate(gather_relative(after(normed_two, three[2])))
     crossed_rows = jnp.concatenate(swap_relative(columns(after(crossed, three[2]))))
     grad_two_rows = jnp.concatenate(gather_relative(grad_two_low))
-    grad_cq_rows = jnp.concatenate(swap_relative(columns(after(grad_cq, one_grads[2]))))
+    grad_cq_rows = jnp.concatenate(swap_relative(columns(grad_cq)))
     grad_text = jnp.concatenate(
         [part.reshape(text_len, -1) for part in (grad_tk, grad_tv)]
     ).astype(jnp.float32)
     grad_text = scatter_relative(*columns(grad_text)).astype(low)
     grad_tk, grad_tv = grad_text[:text_len], grad_text[text_len:]
-    back_grad = sum_clips(
-        jnp.concatenate(
-            [
-                contract_rows(grad_two_rows, crossed_rows).astype(low),
-                contract_rows(grad_one_rows, attended).astype(low),
-            ],
-            axis=1,
-        ),
-    )
-    cross_grad = sum_clips(
-        jnp.concatenate(
-            [
-                contract_rows(rows_two, grad_cq_rows).astype(low),
-                contract_rows(text_rows, grad_tk).astype(low),
-                contract_rows(text_rows, grad_tv).astype(low),
-            ],
-            axis=1,
-        ),
-    )
-    c_o_grad, w_o_grad = [part.T for part in jnp.split(back_grad, 2, axis=1)]
-    c_q_grad, c_k_grad, c_v_grad = jnp.split(cross_grad, 3, axis=1)
+    c_o_grad, w_o_grad, c_q_grad, c_k_grad, c_v_grad = sum_clips(
+        [
+            contract_rows(grad_two_rows, crossed_rows),
+            contract_rows(grad_one_rows, attended),
+            contract_rows(rows_two, grad_cq_rows),
+            contract_rows(text_rows, grad_tk),
+            contract_rows(text_rows, grad_tv),
+        ],
+    )
+    c_o_grad, w_o_grad = c_o_grad.T, w_o_grad.T
     text_term = (contract_cols(grad_tk, c_k) + contract_cols(grad_tv, c_v)).astype(low)
     text_states_grad = (
         scatter_relative(
@@ -461,17 +482,23 @@
         ]
     )
 
-    early = sum_everywhere(
+    totals = sum_everywhere(
         jnp.concatenate(
-            [ln3_gain_part, ln3_bias_part, ln2_gain_part, ln2_bias_part, jnp.pad(squares, (0, 124))]
-        )
-    )
-    late = sum_everywhere(jnp.concatenate([ln1_gain_part, ln1_bias_part]))
-    ln3_gain_grad, ln3_bias_grad, ln2_gain_grad, ln2_bias_grad = [
-        early[i * model_width : (i + 1) * model_width] for i in range(4)
+            [
+                ln3_gain_part,
+                ln3_bias_part,
+                ln2_gain_part,
+                ln2_bias_part,
+                ln1_gain_part,
+                ln1_bias_part,
+                jnp.pad(squares, (0, 124)),
+            ]
+        ),
+    )
+    ln3_gain_grad, ln3_bias_grad, ln2_gain_grad, ln2_bias_grad, ln1_gain_grad, ln1_bias_grad = [
+        totals[i * model_width : (i + 1) * model_width] for i in range(6)
     ]
-    ln1_gain_grad, ln1_bias_grad = late[:model_width], late[model_width:]
-    square_totals = early[4 * model_width : 4 * model_width + 4]
+    square_totals = totals[6 * model_width : 6 * model_width + 4]
     entry_count = own_rows * lax.axis_size("dp") * lax.axis_size("tensor") * model_width
     root_squares = jnp.sqrt(square_totals / entry_count)
     return (

time: 665 us -> 650 us (0.977)
  waiting for transfers between devices: 255 us -> 284 us
  local copies, waits for them, and re-layouts: 66.6 us -> 43.2 us
  starting transfers between devices: 109 us -> 89.5 us
    ppermute x5 -> x6, waiting for transfers between devices: 7.21 us -> 82.1 us  [swap_y(): return lax.ppermute(values, 'dp', [(i, i ^ 1) for i in range(8)])]
    ppermute x30 -> x24, waiting for transfers between devices: 113 us -> 79.3 us  [sum_line(): carried.append(lax.ppermute(block, 'dp', pairs))]
    ppermute x30 -> x24, starting transfers between devices: 73.4 us -> 51.2 us  [sum_line(): carried.append(lax.ppermute(block, 'dp', pairs))]
    concatenate x4 -> x1, local copies, waits for them, and re-layouts: 13.1 us -> 2.76 us  [gather_weight(): jnp.concatenate([values, exchange(values, 1), far, exchange(far, 1)], axi...]
    ppermute x6 -> x3, waiting for transfers between devices: 18.8 us -> 8.87 us  [sum_everywhere(): lax.ppermute(values, 'dp', [(i, i ^ flip) for i in range(8)])]
    squeeze x9 -> x4, local copies, waits for them, and re-layouts: 9.43 us -> 0.49 us  [sum_line(): blocks.append(lax.dynamic_index_in_dim(kept, target, axis, keepdims=False))]
    unnamed x216 -> x240, local copies, waits for them, and re-layouts: 29 us -> 20.6 us
    ppermute x55 -> x53, starting transfers between devices: 24.2 us -> 26.5 us  [exchange(): return lax.ppermute(values, 'tensor', [(i, i ^ flip) for i in range(4)])]
  transfers between devices with their start and end apart: 96 -> 86, of which waited for: 31 -> 28; matrix products, arithmetic and copies ran while one was open for 34% -> 31% of each run, Pallas kernels for 6% -> 7%
where the time goes in v3:
time: 650 us; the launch traced here: 641 us
  waiting for transfers between devices  284 us (44%)
  matrix products  129 us (20%)
  starting transfers between devices  89.5 us (14%)
  other arithmetic  49.2 us (8%)
  local copies, waits for them, and re-layouts  43.2 us (7%)
  Pallas kernels  42.4 us (7%)
    ppermute x53, waiting for transfers between devices, exchange(): return lax.ppermute(values, 'tensor', [(i, i ^ flip) for i in range(4)])  114 us
    ppermute x6, waiting for transfers between devices, swap_y(): return lax.ppermute(values, 'dp', [(i, i ^ 1) for i in range(8)])  82.1 us
    ppermute x24, waiting for transfers between devices, sum_line(): carried.append(lax.ppermute(block, 'dp', pairs))  79.3 us
    ppermute x24, starting transfers between devices, sum_line(): carried.append(lax.ppermute(block, 'dp', pairs))  51.2 us
    dot_general x10, matrix products, contract_rows(): lax.dot_general(left_mat, right_mat, (((0,), (0,)), ((), ())), preferred_...  43.1 us
    dot_general x11, matrix products, product(): return jnp.dot(left_mat, right_mat, preferred_element_type=jnp.float32)  41.5 us
    dot_general x11, matrix products, contract_cols(): lax.dot_general(left_mat, right_mat, (((1,), (1,)), ((), ())), preferred_...  37.3 us
    pallas_call x1, Pallas kernels, self_backward(): pl.pallas_call(partial(backward_kernel, rows), out_shape=[jax.ShapeDtypeS...  27.1 us
  transfers between devices with their start and end apart: 86, of which 28 were waited for; matrix products, arithmetic and copies ran while one was open for 31% of the time, Pallas kernels for 7%

profile of v3, /device:TPU:8, one launch (start us, length us, event | category | flops | bytes accessed | tf_op | source)
XLA Modules:
  0.0 640.8 jit_solution(8960117179482065326)
XLA Ops:
  3.7 2.4 fusion.47
  11.8 13.9 %collective-permute-done.1 = bf16[256,1536]{1,0:T(8,128)(2,1)} collective-permute-done((bf16[256,1536]{1,0:T(8,128)(2,1)}, bf16[256,1536]{1,0:T(8,128)(2,1)}, u32[]{:S(2)}, u32[]{:S(2)}) %collective-permute-start.1) | collective-permute-done | bytes 786464 | tf_op jit(solution)/shard_map/ppermute | solution.py:41
  29.7 2.4 constant_dynamic-update-slice_fusion.11
  38.6 7.0 %collective-permute-done.10 = bf16[768,384]{1,0:T(8,128)(2,1)} collective-permute-done((bf16[768,384]{1,0:T(8,128)(2,1)}, bf16[768,384]{1,0:T(8,128)(2,1)}, u32[]{:S(2)}, u32[]{:S(2)}) %collective-permute-start.10) | collective-permute-done | bytes 589856 | tf_op jit(solution)/shard_map/ppermute | solution.py:41
  47.2 10.4 %collective-permute-done.14 = bf16[192,1536]{1,0:T(8,128)(2,1)} collective-permute-done((bf16[192,1536]{1,0:T(8,128)(2,1)S(1)}, bf16[192,1536]{1,0:T(8,128)(2,1)}, u32[]{:S(2)}, u32[]{:S(2)}) %collective-permute-start.14) | collective-permute-done | bytes 589856 | tf_op jit(solution)/shard_map/ppermute | solution.py:41
  59.1 8.6 %convolution_convert_fusion.1.q_ref.k_ref.v_ref = bf16[1024,1152]{1,0:T(8,128)(2,1)} fusion(bf16[1536,1152]{1,0:T(8,128)(2,1)} %copy-done.56, bf16[256,1536]{1,0:T(8,128)(2,1)} %collective-permute-done.2, bf16[256,1536]{1,0:T(8,128)(2,1)} %collective-permute-done.1, bf16[256,1536]{1,0:T(8,128)(2,1)} %collective-permute-done, bf16[256,1536]{1,0:T(8,128)(2,1)} %fusion.47), kind=kOutput, calls=%fused_computation.7 | convolution fusion | flops 3637641216 | bytes 9043968 | tf_op jit(solution)/shard_map/dot_general | solution.py:25
  67.6 15.3 %self_forward.1 = bf16[1024,384]{1,0:T(8,128)(2,1)} custom-call(s32[1]{0:T(128)} %bitcast.id_ref, bf16[1024,1152]{1,0:T(8,128)(2,1)} %convolution_convert_fusion.1.q_ref.k_ref.v_ref, bf16[1024,1152]{1,0:T(8,128)(2,1)} %convolution_convert_fusion.1.q_ref.k_ref.v_ref, bf16[1024,1152]{1,0:T(8,128)(2,1)} %convolution_convert_fusion.1.q_ref.k_ref.v_ref), custom_call_target="tpu_custom_call" | custom-call | flops 1006632960 | bytes 3145728 | tf_op jit(solution)/shard_map/self_forward/pallas_call | solution.py:235
  88.4 2.6 constant_dynamic-update-slice_fusion.10
  96.8 16.1 %collective-permute-done.5 = bf16[256,1536]{1,0:T(8,128)(2,1)S(1)} collective-permute-done((bf16[256,1536]{1,0:T(8,128)(2,1)S(1)}, bf16[256,1536]{1,0:T(8,128)(2,1)S(1)}, u32[]{:S(2)}, u32[]{:S(2)}) %collective-permute-start.5) | collective-permute-done | bytes 786464 | tf_op jit(solution)/shard_map/ppermute | solution.py:41
  117.7 3.3 convolution_convert_fusion.10
  125.0 2.8 constant_dynamic-update-slice_fusion.7
  127.8 4.6 fusion.135
  137.2 11.2 %multiply_convert_fusion.1 = (bf16[512,1536]{1,0:T(8,128)(2,1)S(1)}, f32[512,1536]{1,0:T(8,128)S(1)}, f32[512,1536]{1,0:T(8,128)S(1)}) fusion(bf16[1536,1536]{1,0:T(8,128)(2,1)} %param.35, bf16[256,1536]{1,0:T(8,128)(2,1)} %collective-permute-done.17, bf16[256,1536]{1,0:T(8,128)(2,1)} %add_convert_fusion.6), kind=kOutput, calls=%fused_computation.43 | convolution fusion | flops 2470182912 | bytes 14155776 | tf_op jit(solution)/shard_map/dot_general | solution.py:25
  148.5 3.4 add_convert_fusion.3
  151.8 4.5 fusion.145
  156.7 2.6 fusion.143
  160.4 10.9 %collective-permute-done.19 = bf16[256,1536]{1,0:T(8,128)(2,1)S(1)} collective-permute-done((bf16[256,1536]{1,0:T(8,128)(2,1)}, bf16[256,1536]{1,0:T(8,128)(2,1)S(1)}, u32[]{:S(2)}, u32[]{:S(2)}) %collective-permute-start.19) | collective-permute-done | bytes 786464 | tf_op jit(solution)/shard_map/ppermute | solution.py:41
  172.6 6.6 %fusion.64 = f32[1536,1536]{1,0:T(8,128)} fusion(bf16[512,1536]{1,0:T(8,128)(2,1)S(1)} %add_convert_fusion.3, bf16[256,1536]{1,0:T(8,128)(2,1)} %collective-permute-done.17, bf16[256,1536]{1,0:T(8,128)(2,1)} %add_convert_fusion.6), kind=kOutput, calls=%fused_computation.156 | convolution fusion | flops 2419064832 | bytes 12582912 | tf_op jit(solution)/shard_map/dot_general | solution.py:29
  180.1 5.5 fusion.146
  185.7 2.6 fusion.144
  188.4 9.8 %add_convert_fusion.2 = (bf16[512,1536]{1,0:T(8,128)(2,1)S(1)}, f32[512,1536]{1,0:T(8,128)S(1)}) fusion(f32[512,1536]{1,0:T(8,128)S(1)} %fusion.144, bf16[512,1536]{1,0:T(8,128)(2,1)S(1)} %constant_dynamic-update-slice_fusion.16, bf16[1536,1536]{1,0:T(8,128)(2,1)S(1)} %bitcast.251), kind=kOutput, calls=%fused_computation.28 | convolution fusion | flops 2472542208 | bytes 14155776 | tf_op jit(solution)/shard_map/dot_general | solution.py:35
  199.0 2.6 convolution_convert_fusion.4
  201.8 5.3 add_convert_fusion.1
  209.7 5.4 add_convert_fusion
  218.7 19.1 %collective-permute-done.72 = bf16[2,192,1536]{2,1,0:T(8,128)(2,1)S(1)} collective-permute-done((bf16[2,192,1536]{2,1,0:T(8,128)(2,1)S(1)}, bf16[2,192,1536]{2,1,0:T(8,128)(2,1)S(1)}, u32[]{:S(2)}, u32[]{:S(2)}) %collective-permute-start.72) | collective-permute-done | bytes 1179680 | tf_op jit(solution)/shard_map/ppermute | solution.py:102
  244.2 3.4 convolution_convert_fusion.9
  247.7 2.3 copy.54
  250.0 2.2 multiply_reduce_fusion.6
  256.5 3.5 multiply_reduce_fusion.3
  264.8 3.7 collective-permute-start.74
  269.8 2.9 collective-permute-done.63
  274.3 4.8 fusion.29
  287.6 2.4 copy.57
  290.0 2.4 copy.58
  296.7 2.4 collective-permute-done.75
  299.2 2.8 bitcast_add_fusion
  304.7 15.9 %collective-permute-done.27 = bf16[256,1536]{1,0:T(8,128)(2,1)S(1)} collective-permute-done((bf16[256,1536]{1,0:T(8,128)(2,1)}, bf16[256,1536]{1,0:T(8,128)(2,1)S(1)}, u32[]{:S(2)}, u32[]{:S(2)}) %collective-permute-start.27) | collective-permute-done | bytes 786464 | tf_op jit(solution)/shard_map/ppermute | solution.py:41
  320.8 3.4 bitcast_add_fusion.3
  326.3 3.8 convolution_convert_fusion.3
  330.6 14.0 %collective-permute-done.54 = bf16[256,1536]{1,0:T(8,128)(2,1)} collective-permute-done((bf16[256,1536]{1,0:T(8,128)(2,1)}, bf16[256,1536]{1,0:T(8,128)(2,1)}, u32[]{:S(2)}, u32[]{:S(2)}) %collective-permute-start.54) | collective-permute-done | bytes 786464 | tf_op jit(solution)/shard_map/ppermute | solution.py:41
  344.6 4.5 convolution_convert_fusion.11.grad_ref
  349.1 27.1 %self_backward.1 = (bf16[1024,384]{1,0:T(8,128)(2,1)}, bf16[1024,384]{1,0:T(8,128)(2,1)}, bf16[1024,384]{1,0:T(8,128)(2,1)}) custom-call(s32[1]{0:T(128)} %bitcast.id_ref, bf16[1024,1152]{1,0:T(8,128)(2,1)} %convolution_convert_fusion.1.q_ref.k_ref.v_ref, bf16[1024,1152]{1,0:T(8,128)(2,1)} %convolution_convert_fusion.1.q_ref.k_ref.v_ref, ...), custom_call_target="tpu_custom_call" | custom-call | flops 2516582400 | bytes 5505024 | tf_op jit(solution)/shard_map/self_backward/pallas_call | solution.py:255
  385.8 3.9 collective-permute-start.76
  389.7 3.8 collective-permute-start.82
  394.9 3.8 fusion.32
  399.8 6.3 convolution_convert_fusion
  406.2 2.3 convolution_convert_fusion.8
  419.0 9.6 %collective-permute-done.82 = bf16[1,192,1536]{2,1,0:T(8,128)(2,1)S(1)} collective-permute-done((bf16[1,192,1536]{2,1,0:T(8,128)(2,1)S(1)}, bf16[1,192,1536]{2,1,0:T(8,128)(2,1)S(1)}, u32[]{:S(2)}, u32[]{:S(2)}) %collective-permute-start.82) | collective-permute-done | bytes 589856 | tf_op jit(solution)/shard_map/ppermute | solution.py:102
  432.5 2.6 collective-permute-done.34
  438.1 14.8 %collective-permute-done.30 = bf16[256,1536]{1,0:T(8,128)(2,1)S(1)} collective-permute-done((bf16[256,1536]{1,0:T(8,128)(2,1)S(1)}, bf16[256,1536]{1,0:T(8,128)(2,1)S(1)}, u32[]{:S(2)}, u32[]{:S(2)}) %collective-permute-start.30) | collective-permute-done | bytes 786464 | tf_op jit(solution)/shard_map/ppermute | solution.py:41
  454.8 2.6 constant_dynamic-update-slice_fusion.22
  459.5 3.9 collective-permute-start.84
  463.4 82.1 %collective-permute-done.78 = bf16[1,1,192,1536]{3,2,1,0:T(8,128)(2,1)S(1)} collective-permute-done((bf16[1,1,192,1536]{3,2,1,0:T(8,128)(2,1)S(1)}, bf16[1,1,192,1536]{3,2,1,0:T(8,128)(2,1)S(1)}, u32[]{:S(2)}, u32[]{:S(2)}) %collective-permute-start.78) | collective-permute-done | bytes 589856 | tf_op jit(solution)/shard_map/ppermute | solution.py:82
  554.0 3.1 collective-permute-start.44
  557.2 8.0 %collective-permute-done.44 = f32[9344]{0:T(1024)S(1)} collective-permute-done((f32[9344]{0:T(1024)S(1)}, f32[9344]{0:T(1024)S(1)}, u32[]{:S(2)}, u32[]{:S(2)}) %collective-permute-start.44) | collective-permute-done | bytes 37408 | tf_op jit(solution)/shard_map/ppermute | solution.py:140
  575.6 6.0 collective-permute-done.49
  581.7 11.9 %collective-permute-done.66 = bf16[5,192,384]{2,1,0:T(8,128)(2,1)S(1)} collective-permute-done((bf16[5,192,384]{2,1,0:T(8,128)(2,1)S(1)}, bf16[5,192,384]{2,1,0:T(8,128)(2,1)S(1)}, u32[]{:S(2)}, u32[]{:S(2)}) %collective-permute-start.66) | collective-permute-done | bytes 737312 | tf_op jit(solution)/shard_map/ppermute | solution.py:102
  593.7 3.5 collective-permute-start.68
  600.6 4.6 collective-permute-start.51
  605.7 9.3 %collective-permute-done.68 = bf16[5,192,384]{2,1,0:T(8,128)(2,1)S(1)} collective-permute-done((bf16[5,192,384]{2,1,0:T(8,128)(2,1)S(1)}, bf16[5,192,384]{2,1,0:T(8,128)(2,1)S(1)}, u32[]{:S(2)}, u32[]{:S(2)}) %collective-permute-start.68) | collective-permute-done | bytes 737312 | tf_op jit(solution)/shard_map/ppermute | solution.py:102
  615.0 3.6 collective-permute-done.69
  620.6 3.9 collective-permute-start.70
  624.6 3.5 collective-permute-done.52
  629.1 10.1 %collective-permute-done.71 = bf16[5,192,384]{2,1,0:T(8,128)(2,1)S(1)} collective-permute-done((bf16[5,192,384]{2,1,0:T(8,128)(2,1)S(1)}, bf16[5,192,384]{2,1,0:T(8,128)(2,1)S(1)}, u32[]{:S(2)}, u32[]{:S(2)}) %collective-permute-start.71) | collective-permute-done | bytes 737312 | tf_op jit(solution)/shard_map/ppermute | solution.py:102
  (502 shorter events, 153.8 us)
Async XLA Ops:
  6.1 19.6 %collective-permute-start.1 = (bf16[256,1536]{1,0:T(8,128)(2,1)}, bf16[256,1536]{1,0:T(8,128)(2,1)}, u32[]{:S(2)}, u32[]{:S(2)}) collective-permute-start(bf16[256,1536]{1,0:T(8,128)(2,1)} %fusion.47), channel_id=1, source_target_pairs={{0,2},{1,3},{2,0},{3,1},{4,6},{5,7},{6,4},{7,5},{8,10},{9,11},{10,... | collective-permute-start | bytes 2359304 | tf_op jit(solution)/shard_map/ppermute | solution.py:41
  7.6 30.6 %collective-permute-start = (bf16[256,1536]{1,0:T(8,128)(2,1)}, bf16[256,1536]{1,0:T(8,128)(2,1)}, u32[]{:S(2)}, u32[]{:S(2)}) collective-permute-start(bf16[256,1536]{1,0:T(8,128)(2,1)} %fusion.47), channel_id=1, source_target_pairs={{0,1},{1,0},{2,3},{3,2},{4,5},{5,4},{6,7},{7,6},{8,9},{9,8},{10,11... | collective-permute-start | bytes 2359304 | tf_op jit(solution)/shard_map/ppermute | solution.py:41
  29.1 16.5 %collective-permute-start.10 = (bf16[768,384]{1,0:T(8,128)(2,1)}, bf16[768,384]{1,0:T(8,128)(2,1)}, u32[]{:S(2)}, u32[]{:S(2)}) collective-permute-start(bf16[768,384]{1,0:T(8,128)(2,1)} %constant_dynamic-slice_fusion.3), channel_id=1, source_target_pairs={{0,2},{1,3},{2,0},{3,1},{4,6},{5,7},{6,4},{7,5},{8,10},{9,11},{10,... | collective-permute-start | bytes 1769480 | tf_op jit(solution)/shard_map/ppermute | solution.py:41
  33.2 24.4 %collective-permute-start.14 = (bf16[192,1536]{1,0:T(8,128)(2,1)S(1)}, bf16[192,1536]{1,0:T(8,128)(2,1)}, u32[]{:S(2)}, u32[]{:S(2)}) collective-permute-start(bf16[192,1536]{1,0:T(8,128)(2,1)S(1)} %constant_dynamic-slice_fusion.2), channel_id=1, source_target_pairs={{0,2},{1,3},{2,0},{3,1},{4,6},{5,7},{6,4},{7,5},{8,10},{9,11},{10,... | collective-permute-start | bytes 1769480 | tf_op jit(solution)/shard_map/ppermute | solution.py:41
  34.8 24.3 %collective-permute-start.2 = (bf16[256,1536]{1,0:T(8,128)(2,1)}, bf16[256,1536]{1,0:T(8,128)(2,1)}, u32[]{:S(2)}, u32[]{:S(2)}) collective-permute-start(bf16[256,1536]{1,0:T(8,128)(2,1)} %collective-permute-done.1), channel_id=1, source_target_pairs={{0,1},{1,0},{2,3},{3,2},{4,5},{5,4},{6,7},{7,6},{8,9},{9,8},{10,11... | collective-permute-start | bytes 2359304 | tf_op jit(solution)/shard_map/ppermute | solution.py:41
  37.5 79.2 %collective-permute-start.9 = (bf16[1536,384]{1,0:T(8,128)(2,1)}, bf16[1536,384]{1,0:T(8,128)(2,1)}, u32[]{:S(2)}, u32[]{:S(2)}) collective-permute-start(bf16[1536,384]{1,0:T(8,128)(2,1)} %param.29), channel_id=1, source_target_pairs={{0,1},{1,0},{2,3},{3,2},{4,5},{5,4},{6,7},{7,6},{8,9},{9,8},{10,11... | collective-permute-start | bytes 3538952 | tf_op jit(solution)/shard_map/ppermute | solution.py:41
  38.2 50.1 %collective-permute-start.13 = (bf16[384,1536]{1,0:T(8,128)(2,1)}, bf16[384,1536]{1,0:T(8,128)(2,1)}, u32[]{:S(2)}, u32[]{:S(2)}) collective-permute-start(bf16[384,1536]{1,0:T(8,128)(2,1)} %param.32), channel_id=1, source_target_pairs={{0,1},{1,0},{2,3},{3,2},{4,5},{5,4},{6,7},{7,6},{8,9},{9,8},{10,11... | collective-permute-start | bytes 3538952 | tf_op jit(solution)/shard_map/ppermute | solution.py:41
  45.6 40.6 %collective-permute-start.11 = (bf16[768,384]{1,0:T(8,128)(2,1)}, bf16[768,384]{1,0:T(8,128)(2,1)}, u32[]{:S(2)}, u32[]{:S(2)}) collective-permute-start(bf16[768,384]{1,0:T(8,128)(2,1)} %collective-permute-done.10), channel_id=1, source_target_pairs={{0,4},{4,0},{8,12},{12,8},{16,20},{20,16},{24,28},{28,24},{1,5},{5... | collective-permute-start | bytes 1769480 | tf_op jit(solution)/shard_map/ppermute | solution.py:82
  57.5 33.4 %collective-permute-start.15 = (bf16[192,1536]{1,0:T(8,128)(2,1)}, bf16[192,1536]{1,0:T(8,128)(2,1)}, u32[]{:S(2)}, u32[]{:S(2)}) collective-permute-start(bf16[192,1536]{1,0:T(8,128)(2,1)} %collective-permute-done.14), channel_id=1, source_target_pairs={{0,4},{4,0},{8,12},{12,8},{16,20},{20,16},{24,28},{28,24},{1,5},{5... | collective-permute-start | bytes 1769480 | tf_op jit(solution)/shard_map/ppermute | solution.py:82
  88.3 28.3 %collective-permute-start.12 = (bf16[1536,384]{1,0:T(8,128)(2,1)S(1)}, bf16[1536,384]{1,0:T(8,128)(2,1)S(1)}, u32[]{:S(2)}, u32[]{:S(2)}) collective-permute-start(bf16[1536,384]{1,0:T(8,128)(2,1)S(1)} %pad_maximum_fusion.4), channel_id=1, source_target_pairs={{0,1},{1,0},{2,3},{3,2},{4,5},{5,4},{6,7},{7,6},{8,9},{9,8},{10,11... | collective-permute-start | bytes 3538952 | tf_op jit(solution)/shard_map/ppermute | solution.py:41
  93.1 19.8 %collective-permute-start.5 = (bf16[256,1536]{1,0:T(8,128)(2,1)S(1)}, bf16[256,1536]{1,0:T(8,128)(2,1)S(1)}, u32[]{:S(2)}, u32[]{:S(2)}) collective-permute-start(bf16[256,1536]{1,0:T(8,128)(2,1)S(1)} %slice_add_fusion.7), channel_id=1, source_target_pairs={{0,2},{1,3},{2,0},{3,1},{4,6},{5,7},{6,4},{7,5},{8,10},{9,11},{10,... | collective-permute-start | bytes 2359304 | tf_op jit(solution)/shard_map/ppermute | solution.py:41
  96.8 28.2 %collective-permute-start.16 = (bf16[384,1536]{1,0:T(8,128)(2,1)}, bf16[384,1536]{1,0:T(8,128)(2,1)}, u32[]{:S(2)}, u32[]{:S(2)}) collective-permute-start(bf16[384,1536]{1,0:T(8,128)(2,1)} %pad_maximum_fusion.5), channel_id=1, source_target_pairs={{0,1},{1,0},{2,3},{3,2},{4,5},{5,4},{6,7},{7,6},{8,9},{9,8},{10,11... | collective-permute-start | bytes 3538952 | tf_op jit(solution)/shard_map/ppermute | solution.py:41
  134.5 37.4 %collective-permute-start.23 = (bf16[256,1536]{1,0:T(8,128)(2,1)S(1)}, bf16[256,1536]{1,0:T(8,128)(2,1)S(1)}, u32[]{:S(2)}, u32[]{:S(2)}) collective-permute-start(bf16[256,1536]{1,0:T(8,128)(2,1)S(1)} %copy-done.14), channel_id=1, source_target_pairs={{0,2},{1,3},{2,0},{3,1},{4,6},{5,7},{6,4},{7,5},{8,10},{9,11},{10,... | collective-permute-start | bytes 2359304 | tf_op jit(solution)/shard_map/ppermute | solution.py:41
  135.1 13.3 %collective-permute-start.21 = (bf16[256,1536]{1,0:T(8,128)(2,1)S(1)}, bf16[256,1536]{1,0:T(8,128)(2,1)S(1)}, u32[]{:S(2)}, u32[]{:S(2)}) collective-permute-start(bf16[256,1536]{1,0:T(8,128)(2,1)S(1)} %copy-done.14), channel_id=1, source_target_pairs={{0,1},{1,0},{2,3},{3,2},{4,5},{5,4},{6,7},{7,6},{8,9},{9,8},{10,11... | collective-permute-start | bytes 2359304 | tf_op jit(solution)/shard_map/ppermute | solution.py:41
  135.3 36.0 %collective-permute-start.19 = (bf16[256,1536]{1,0:T(8,128)(2,1)}, bf16[256,1536]{1,0:T(8,128)(2,1)S(1)}, u32[]{:S(2)}, u32[]{:S(2)}) collective-permute-start(bf16[256,1536]{1,0:T(8,128)(2,1)} %add_convert_fusion.6), channel_id=1, source_target_pairs={{0,2},{1,3},{2,0},{3,1},{4,6},{5,7},{6,4},{7,5},{8,10},{9,11},{10,... | collective-permute-start | bytes 2359304 | tf_op jit(solution)/shard_map/ppermute | solution.py:41
  156.5 83.4 %collective-permute-start.22 = (bf16[256,1536]{1,0:T(8,128)(2,1)S(1)}, bf16[256,1536]{1,0:T(8,128)(2,1)S(1)}, u32[]{:S(2)}, u32[]{:S(2)}) collective-permute-start(bf16[256,1536]{1,0:T(8,128)(2,1)S(1)} %slice.287), channel_id=1, source_target_pairs={{0,1},{1,0},{2,3},{3,2},{4,5},{5,4},{6,7},{7,6},{8,9},{9,8},{10,11... | collective-permute-start | bytes 2359304 | tf_op jit(solution)/shard_map/ppermute | solution.py:41
  171.3 47.1 %collective-permute-start.60 = (bf16[256,1536]{1,0:T(8,128)(2,1)}, bf16[256,1536]{1,0:T(8,128)(2,1)}, u32[]{:S(2)}, u32[]{:S(2)}) collective-permute-start(bf16[256,1536]{1,0:T(8,128)(2,1)} %add_convert_fusion.7), channel_id=1, source_target_pairs={{0,2},{1,3},{2,0},{3,1},{4,6},{5,7},{6,4},{7,5},{8,10},{9,11},{10,... | collective-permute-start | bytes 2359304 | tf_op jit(solution)/shard_map/ppermute | solution.py:41
  171.8 13.8 %collective-permute-start.20 = (bf16[256,1536]{1,0:T(8,128)(2,1)S(1)}, bf16[256,1536]{1,0:T(8,128)(2,1)S(1)}, u32[]{:S(2)}, u32[]{:S(2)}) collective-permute-start(bf16[256,1536]{1,0:T(8,128)(2,1)S(1)} %collective-permute-done.19), channel_id=1, source_target_pairs={{0,1},{1,0},{2,3},{3,2},{4,5},{5,4},{6,7},{7,6},{8,9},{9,8},{10,11... | collective-permute-start | bytes 2359304 | tf_op jit(solution)/shard_map/ppermute | solution.py:41
  172.0 16.3 %collective-permute-start.24 = (bf16[256,1536]{1,0:T(8,128)(2,1)S(1)}, bf16[256,1536]{1,0:T(8,128)(2,1)S(1)}, u32[]{:S(2)}, u32[]{:S(2)}) collective-permute-start(bf16[256,1536]{1,0:T(8,128)(2,1)S(1)} %collective-permute-done.23), channel_id=1, source_target_pairs={{0,1},{1,0},{2,3},{3,2},{4,5},{5,4},{6,7},{7,6},{8,9},{9,8},{10,11... | collective-permute-start | bytes 2359304 | tf_op jit(solution)/shard_map/ppermute | solution.py:41
  201.7 13.4 %collective-permute-start.25 = (bf16[256,1536]{1,0:T(8,128)(2,1)S(1)}, bf16[256,1536]{1,0:T(8,128)(2,1)S(1)}, u32[]{:S(2)}, u32[]{:S(2)}) collective-permute-start(bf16[256,1536]{1,0:T(8,128)(2,1)S(1)} %slice.189), channel_id=1, source_target_pairs={{0,1},{1,0},{2,3},{3,2},{4,5},{5,4},{6,7},{7,6},{8,9},{9,8},{10,11... | collective-permute-start | bytes 2359304 | tf_op jit(solution)/shard_map/ppermute | solution.py:41
  207.3 30.5 %collective-permute-start.72 = (bf16[2,192,1536]{2,1,0:T(8,128)(2,1)S(1)}, bf16[2,192,1536]{2,1,0:T(8,128)(2,1)S(1)}, u32[]{:S(2)}, u32[]{:S(2)}) collective-permute-start(bf16[2,192,1536]{2,1,0:T(8,128)(2,1)S(1)} %get-tuple-element.100), channel_id=1, source_target_pairs={{0,8},{4,12},{1,9},{5,13},{2,10},{6,14},{3,11},{7,15}} | collective-permute-start | bytes 3538952 | tf_op jit(solution)/shard_map/ppermute | solution.py:102
  208.8 29.4 %collective-permute-start.73 = (bf16[2,192,1536]{2,1,0:T(8,128)(2,1)S(1)}, bf16[2,192,1536]{2,1,0:T(8,128)(2,1)S(1)}, u32[]{:S(2)}, u32[]{:S(2)}) collective-permute-start(bf16[2,192,1536]{2,1,0:T(8,128)(2,1)S(1)} %get-tuple-element.101), channel_id=1, source_target_pairs={{24,16},{28,20},{25,17},{29,21},{26,18},{30,22},{27,19},{31,23}} | collective-permute-start | bytes 3538952 | tf_op jit(solution)/shard_map/ppermute | solution.py:102
  215.2 24.7 %collective-permute-start.26 = (bf16[256,1536]{1,0:T(8,128)(2,1)S(1)}, bf16[256,1536]{1,0:T(8,128)(2,1)S(1)}, u32[]{:S(2)}, u32[]{:S(2)}) collective-permute-start(bf16[256,1536]{1,0:T(8,128)(2,1)S(1)} %slice_add_fusion.6), channel_id=1, source_target_pairs={{0,2},{1,3},{2,0},{3,1},{4,6},{5,7},{6,4},{7,5},{8,10},{9,11},{10,... | collective-permute-start | bytes 2359304 | tf_op jit(solution)/shard_map/ppermute | solution.py:41
  218.4 45.5 %collective-permute-start.59 = (bf16[256,1536]{1,0:T(8,128)(2,1)}, bf16[256,1536]{1,0:T(8,128)(2,1)}, u32[]{:S(2)}, u32[]{:S(2)}) collective-permute-start(bf16[256,1536]{1,0:T(8,128)(2,1)} %add_convert_fusion.7), channel_id=1, source_target_pairs={{0,1},{1,0},{2,3},{3,2},{4,5},{5,4},{6,7},{7,6},{8,9},{9,8},{10,11... | collective-permute-start | bytes 2359304 | tf_op jit(solution)/shard_map/ppermute | solution.py:41
  237.8 61.4 %collective-permute-start.79 = (bf16[1,4,192,1536]{3,2,1,0:T(8,128)(2,1)}, bf16[1,4,192,1536]{3,2,1,0:T(8,128)(2,1)}, u32[]{:S(2)}, u32[]{:S(2)}) collective-permute-start(bf16[1,4,192,1536]{3,2,1,0:T(8,128)(2,1)} %dynamic-slice_bitcast_fusion), channel_id=1, source_target_pairs={{0,4},{4,0},{8,12},{12,8},{16,20},{20,16},{24,28},{28,24},{1,5},{5... | collective-permute-start | bytes 7077896 | tf_op jit(solution)/shard_map/ppermute | solution.py:82
  238.3 26.5 %collective-permute-start.61 = (bf16[256,1536]{1,0:T(8,128)(2,1)}, bf16[256,1536]{1,0:T(8,128)(2,1)}, u32[]{:S(2)}, u32[]{:S(2)}) collective-permute-start(bf16[256,1536]{1,0:T(8,128)(2,1)} %collective-permute-done.60), channel_id=1, source_target_pairs={{0,1},{1,0},{2,3},{3,2},{4,5},{5,4},{6,7},{7,6},{8,9},{9,8},{10,11... | collective-permute-start | bytes 2359304 | tf_op jit(solution)/shard_map/ppermute | solution.py:41
  264.8 30.4 %collective-permute-start.74 = (bf16[2,192,1536]{2,1,0:T(8,128)(2,1)}, bf16[2,192,1536]{2,1,0:T(8,128)(2,1)}, u32[]{:S(2)}, u32[]{:S(2)}) collective-permute-start(bf16[2,192,1536]{2,1,0:T(8,128)(2,1)} %get-tuple-element.104), channel_id=1, source_target_pairs={{0,8},{4,12},{8,16},{12,20},{1,9},{5,13},{9,17},{13,21},{2,10},{6,... | collective-permute-start | bytes 3538952 | tf_op jit(solution)/shard_map/ppermute | solution.py:102
  268.5 30.6 %collective-permute-start.75 = (bf16[2,192,1536]{2,1,0:T(8,128)(2,1)}, bf16[2,192,1536]{2,1,0:T(8,128)(2,1)}, u32[]{:S(2)}, u32[]{:S(2)}) collective-permute-start(bf16[2,192,1536]{2,1,0:T(8,128)(2,1)} %get-tuple-element.105), channel_id=1, source_target_pairs={{24,16},{28,20},{16,8},{20,12},{25,17},{29,21},{17,9},{21,13},{26,... | collective-permute-start | bytes 3538952 | tf_op jit(solution)/shard_map/ppermute | solution.py:102
  292.4 91.4 %collective-permute-start.58 = (bf16[256,384]{0,1:T(8,128)(2,1)}, bf16[256,384]{0,1:T(8,128)(2,1)}, u32[]{:S(2)}, u32[]{:S(2)}) collective-permute-start(bf16[256,384]{0,1:T(8,128)(2,1)} %get-tuple-element.205), channel_id=1, source_target_pairs={{0,3},{1,2},{2,1},{3,0},{4,7},{5,6},{6,5},{7,4},{8,11},{9,10},{10,... | collective-permute-start | bytes 589832 | tf_op jit(solution)/shard_map/ppermute | solution.py:41
  292.4 93.4 %collective-permute-start.57 = (bf16[256,384]{0,1:T(8,128)(2,1)}, bf16[256,384]{0,1:T(8,128)(2,1)}, u32[]{:S(2)}, u32[]{:S(2)}) collective-permute-start(bf16[256,384]{0,1:T(8,128)(2,1)} %get-tuple-element.206), channel_id=1, source_target_pairs={{0,2},{1,3},{2,0},{3,1},{4,6},{5,7},{6,4},{7,5},{8,10},{9,11},{10,... | collective-permute-start | bytes 589832 | tf_op jit(solution)/shard_map/ppermute | solution.py:41
  295.2 25.4 %collective-permute-start.27 = (bf16[256,1536]{1,0:T(8,128)(2,1)}, bf16[256,1536]{1,0:T(8,128)(2,1)S(1)}, u32[]{:S(2)}, u32[]{:S(2)}) collective-permute-start(bf16[256,1536]{1,0:T(8,128)(2,1)} %fusion.126), channel_id=1, source_target_pairs={{0,2},{1,3},{2,0},{3,1},{4,6},{5,7},{6,4},{7,5},{8,10},{9,11},{10,... | collective-permute-start | bytes 2359304 | tf_op jit(solution)/shard_map/ppermute | solution.py:41
  302.1 22.2 %collective-permute-start.80 = (bf16[1,192,1536]{2,1,0:T(8,128)(2,1)S(1)}, bf16[1,192,1536]{2,1,0:T(8,128)(2,1)S(1)}, u32[]{:S(2)}, u32[]{:S(2)}) collective-permute-start(bf16[1,192,1536]{2,1,0:T(8,128)(2,1)S(1)} %get-tuple-element.110), channel_id=1, source_target_pairs={{0,8},{4,12},{1,9},{5,13},{2,10},{6,14},{3,11},{7,15}} | collective-permute-start | bytes 1769480 | tf_op jit(solution)/shard_map/ppermute | solution.py:102
  303.6 20.9 %collective-permute-start.81 = (bf16[1,192,1536]{2,1,0:T(8,128)(2,1)S(1)}, bf16[1,192,1536]{2,1,0:T(8,128)(2,1)S(1)}, u32[]{:S(2)}, u32[]{:S(2)}) collective-permute-start(bf16[1,192,1536]{2,1,0:T(8,128)(2,1)S(1)} %get-tuple-element.111), channel_id=1, source_target_pairs={{24,16},{28,20},{25,17},{29,21},{26,18},{30,22},{27,19},{31,23}} | collective-permute-start | bytes 1769480 | tf_op jit(solution)/shard_map/ppermute | solution.py:102
  324.5 20.0 %collective-permute-start.54 = (bf16[256,1536]{1,0:T(8,128)(2,1)}, bf16[256,1536]{1,0:T(8,128)(2,1)}, u32[]{:S(2)}, u32[]{:S(2)}) collective-permute-start(bf16[256,1536]{1,0:T(8,128)(2,1)} %fusion.66), channel_id=1, source_target_pairs={{0,2},{1,3},{2,0},{3,1},{4,6},{5,7},{6,4},{7,5},{8,10},{9,11},{10,... | collective-permute-start | bytes 2359304 | tf_op jit(solution)/shard_map/ppermute | solution.py:41
  326.2 63.5 %collective-permute-start.56 = (bf16[256,384]{0,1:T(8,128)(2,1)S(1)}, bf16[256,384]{0,1:T(8,128)(2,1)}, u32[]{:S(2)}, u32[]{:S(2)}) collective-permute-start(bf16[256,384]{0,1:T(8,128)(2,1)S(1)} %copy-done.59), channel_id=1, source_target_pairs={{0,1},{1,0},{2,3},{3,2},{4,5},{5,4},{6,7},{7,6},{8,9},{9,8},{10,11... | collective-permute-start | bytes 589832 | tf_op jit(solution)/shard_map/ppermute | solution.py:41
  330.1 63.5 %collective-permute-start.53 = (bf16[256,1536]{1,0:T(8,128)(2,1)}, bf16[256,1536]{1,0:T(8,128)(2,1)}, u32[]{:S(2)}, u32[]{:S(2)}) collective-permute-start(bf16[256,1536]{1,0:T(8,128)(2,1)} %fusion.66), channel_id=1, source_target_pairs={{0,1},{1,0},{2,3},{3,2},{4,5},{5,4},{6,7},{7,6},{8,9},{9,8},{10,11... | collective-permute-start | bytes 2359304 | tf_op jit(solution)/shard_map/ppermute | solution.py:41
  344.6 50.3 %collective-permute-start.55 = (bf16[256,1536]{1,0:T(8,128)(2,1)}, bf16[256,1536]{1,0:T(8,128)(2,1)}, u32[]{:S(2)}, u32[]{:S(2)}) collective-permute-start(bf16[256,1536]{1,0:T(8,128)(2,1)} %collective-permute-done.54), channel_id=1, source_target_pairs={{0,1},{1,0},{2,3},{3,2},{4,5},{5,4},{6,7},{7,6},{8,9},{9,8},{10,11... | collective-permute-start | bytes 2359304 | tf_op jit(solution)/shard_map/ppermute | solution.py:41
  383.8 30.7 %collective-permute-start.77 = (bf16[2,192,1536]{2,1,0:T(8,128)(2,1)S(1)}, bf16[2,192,1536]{2,1,0:T(8,128)(2,1)S(1)}, u32[]{:S(2)}, u32[]{:S(2)}) collective-permute-start(bf16[2,192,1536]{2,1,0:T(8,128)(2,1)S(1)} %copy-done.44), channel_id=1, source_target_pairs={{24,16},{28,20},{16,8},{20,12},{8,0},{12,4},{25,17},{29,21},{17,9}... | collective-permute-start | bytes 3538952 | tf_op jit(solution)/shard_map/ppermute | solution.py:102
  385.8 30.7 %collective-permute-start.76 = (bf16[2,192,1536]{2,1,0:T(8,128)(2,1)S(1)}, bf16[2,192,1536]{2,1,0:T(8,128)(2,1)S(1)}, u32[]{:S(2)}, u32[]{:S(2)}) collective-permute-start(bf16[2,192,1536]{2,1,0:T(8,128)(2,1)S(1)} %copy-done.43), channel_id=1, source_target_pairs={{0,8},{4,12},{8,16},{12,20},{16,24},{20,28},{1,9},{5,13},{9,17},{1... | collective-permute-start | bytes 3538952 | tf_op jit(solution)/shard_map/ppermute | solution.py:102
  389.7 38.9 %collective-permute-start.82 = (bf16[1,192,1536]{2,1,0:T(8,128)(2,1)S(1)}, bf16[1,192,1536]{2,1,0:T(8,128)(2,1)S(1)}, u32[]{:S(2)}, u32[]{:S(2)}) collective-permute-start(bf16[1,192,1536]{2,1,0:T(8,128)(2,1)S(1)} %copy-done.52), channel_id=1, source_target_pairs={{0,8},{4,12},{8,16},{12,20},{1,9},{5,13},{9,17},{13,21},{2,10},{6,... | collective-permute-start | bytes 1769480 | tf_op jit(solution)/shard_map/ppermute | solution.py:102
  393.5 35.1 %collective-permute-start.83 = (bf16[1,192,1536]{2,1,0:T(8,128)(2,1)S(1)}, bf16[1,192,1536]{2,1,0:T(8,128)(2,1)S(1)}, u32[]{:S(2)}, u32[]{:S(2)}) collective-permute-start(bf16[1,192,1536]{2,1,0:T(8,128)(2,1)S(1)} %get-tuple-element.115), channel_id=1, source_target_pairs={{24,16},{28,20},{16,8},{20,12},{25,17},{29,21},{17,9},{21,13},{26,... | collective-permute-start | bytes 1769480 | tf_op jit(solution)/shard_map/ppermute | solution.py:102
  394.9 17.2 %collective-permute-start.33 = (bf16[256,1536]{1,0:T(8,128)(2,1)S(1)}, bf16[256,1536]{1,0:T(8,128)(2,1)S(1)}, u32[]{:S(2)}, u32[]{:S(2)}) collective-permute-start(bf16[256,1536]{1,0:T(8,128)(2,1)S(1)} %slice.197), channel_id=1, source_target_pairs={{0,1},{1,0},{2,3},{3,2},{4,5},{5,4},{6,7},{7,6},{8,9},{9,8},{10,11... | collective-permute-start | bytes 2359304 | tf_op jit(solution)/shard_map/ppermute | solution.py:41
  412.1 18.2 %collective-permute-start.29 = (bf16[256,1536]{1,0:T(8,128)(2,1)S(1)}, bf16[256,1536]{1,0:T(8,128)(2,1)S(1)}, u32[]{:S(2)}, u32[]{:S(2)}) collective-permute-start(bf16[256,1536]{1,0:T(8,128)(2,1)S(1)} %slice.191), channel_id=1, source_target_pairs={{0,1},{1,0},{2,3},{3,2},{4,5},{5,4},{6,7},{7,6},{8,9},{9,8},{10,11... | collective-permute-start | bytes 2359304 | tf_op jit(solution)/shard_map/ppermute | solution.py:41
  414.6 16.3 %collective-permute-start.32 = (bf16[256,1536]{1,0:T(8,128)(2,1)S(1)}, bf16[256,1536]{1,0:T(8,128)(2,1)S(1)}, u32[]{:S(2)}, u32[]{:S(2)}) collective-permute-start(bf16[256,1536]{1,0:T(8,128)(2,1)S(1)} %slice.286), channel_id=1, source_target_pairs={{0,1},{1,0},{2,3},{3,2},{4,5},{5,4},{6,7},{7,6},{8,9},{9,8},{10,11... | collective-permute-start | bytes 2359304 | tf_op jit(solution)/shard_map/ppermute | solution.py:41
  416.5 18.6 %collective-permute-start.34 = (bf16[256,1536]{1,0:T(8,128)(2,1)S(1)}, bf16[256,1536]{1,0:T(8,128)(2,1)S(1)}, u32[]{:S(2)}, u32[]{:S(2)}) collective-permute-start(bf16[256,1536]{1,0:T(8,128)(2,1)S(1)} %slice_add_fusion.4), channel_id=1, source_target_pairs={{0,2},{1,3},{2,0},{3,1},{4,6},{5,7},{6,4},{7,5},{8,10},{9,11},{10,... | collective-permute-start | bytes 2359304 | tf_op jit(solution)/shard_map/ppermute | solution.py:41
  428.7 120.9 %collective-permute-start.46 = (bf16[1,4,192,1152]{3,2,1,0:T(8,128)(2,1)S(1)}, bf16[1,4,192,1152]{3,2,1,0:T(8,128)(2,1)S(1)}, u32[]{:S(2)}, u32[]{:S(2)}) collective-permute-start(bf16[1,4,192,1152]{3,2,1,0:T(8,128)(2,1)S(1)} %dynamic-slice_bitcast_fusion.1), channel_id=1, source_target_pairs={{0,4},{4,0},{8,12},{12,8},{16,20},{20,16},{24,28},{28,24},{1,5},{5... | collective-permute-start | bytes 5308424 | tf_op jit(solution)/shard_map/ppermute | solution.py:82
  430.3 139.7 %collective-permute-start.65 = (bf16[5,4,192,384]{3,2,0,1:T(8,128)(2,1)S(1)}, bf16[5,4,192,384]{3,2,0,1:T(8,128)(2,1)S(1)}, u32[]{:S(2)}, u32[]{:S(2)}) collective-permute-start(bf16[5,4,192,384]{3,2,0,1:T(8,128)(2,1)S(1)} %get-tuple-element.185), channel_id=1, source_target_pairs={{0,4},{4,0},{8,12},{12,8},{16,20},{20,16},{24,28},{28,24},{1,5},{5... | collective-permute-start | bytes 8847368 | tf_op jit(solution)/shard_map/ppermute | solution.py:82
  430.9 114.6 %collective-permute-start.78 = (bf16[1,1,192,1536]{3,2,1,0:T(8,128)(2,1)S(1)}, bf16[1,1,192,1536]{3,2,1,0:T(8,128)(2,1)S(1)}, u32[]{:S(2)}, u32[]{:S(2)}) collective-permute-start(bf16[1,1,192,1536]{3,2,1,0:T(8,128)(2,1)S(1)} %fusion.83), channel_id=1, source_target_pairs={{0,4},{4,0},{8,12},{12,8},{16,20},{20,16},{24,28},{28,24},{1,5},{5... | collective-permute-start | bytes 1769480 | tf_op jit(solution)/shard_map/ppermute | solution.py:82
  435.1 17.8 %collective-permute-start.30 = (bf16[256,1536]{1,0:T(8,128)(2,1)S(1)}, bf16[256,1536]{1,0:T(8,128)(2,1)S(1)}, u32[]{:S(2)}, u32[]{:S(2)}) collective-permute-start(bf16[256,1536]{1,0:T(8,128)(2,1)S(1)} %slice_add_fusion.5), channel_id=1, source_target_pairs={{0,2},{1,3},{2,0},{3,1},{4,6},{5,7},{6,4},{7,5},{8,10},{9,11},{10,... | collective-permute-start | bytes 2359304 | tf_op jit(solution)/shard_map/ppermute | solution.py:41
  457.5 93.6 %collective-permute-start.85 = (bf16[1,192,1536]{2,1,0:T(8,128)(2,1)S(1)}, bf16[1,192,1536]{2,1,0:T(8,128)(2,1)S(1)}, u32[]{:S(2)}, u32[]{:S(2)}) collective-permute-start(bf16[1,192,1536]{2,1,0:T(8,128)(2,1)S(1)} %get-tuple-element.119), channel_id=1, source_target_pairs={{24,16},{28,20},{16,8},{20,12},{8,0},{12,4},{25,17},{29,21},{17,9}... | collective-permute-start | bytes 1769480 | tf_op jit(solution)/shard_map/ppermute | solution.py:102
  459.5 92.4 %collective-permute-start.84 = (bf16[1,192,1536]{2,1,0:T(8,128)(2,1)S(1)}, bf16[1,192,1536]{2,1,0:T(8,128)(2,1)S(1)}, u32[]{:S(2)}, u32[]{:S(2)}) collective-permute-start(bf16[1,192,1536]{2,1,0:T(8,128)(2,1)S(1)} %get-tuple-element.118), channel_id=1, source_target_pairs={{0,8},{4,12},{8,16},{12,20},{16,24},{20,28},{1,9},{5,13},{9,17},{1... | collective-permute-start | bytes 1769480 | tf_op jit(solution)/shard_map/ppermute | solution.py:102
  549.9 16.7 %collective-permute-start.47 = (bf16[1,192,1152]{2,1,0:T(8,128)(2,1)S(1)}, bf16[1,192,1152]{2,1,0:T(8,128)(2,1)S(1)}, u32[]{:S(2)}, u32[]{:S(2)}) collective-permute-start(bf16[1,192,1152]{2,1,0:T(8,128)(2,1)S(1)} %get-tuple-element.78), channel_id=1, source_target_pairs={{0,8},{4,12},{1,9},{5,13},{2,10},{6,14},{3,11},{7,15}} | collective-permute-start | bytes 1327112 | tf_op jit(solution)/shard_map/ppermute | solution.py:102
  551.2 15.4 %collective-permute-start.48 = (bf16[1,192,1152]{2,1,0:T(8,128)(2,1)S(1)}, bf16[1,192,1152]{2,1,0:T(8,128)(2,1)S(1)}, u32[]{:S(2)}, u32[]{:S(2)}) collective-permute-start(bf16[1,192,1152]{2,1,0:T(8,128)(2,1)S(1)} %get-tuple-element.79), channel_id=1, source_target_pairs={{24,16},{28,20},{25,17},{29,21},{26,18},{30,22},{27,19},{31,23}} | collective-permute-start | bytes 1327112 | tf_op jit(solution)/shard_map/ppermute | solution.py:102
  554.0 11.2 %collective-permute-start.44 = (f32[9344]{0:T(1024)S(1)}, f32[9344]{0:T(1024)S(1)}, u32[]{:S(2)}, u32[]{:S(2)}) collective-permute-start(f32[9344]{0:T(1024)S(1)} %add.405), channel_id=1, source_target_pairs={{0,16},{4,20},{8,24},{12,28},{16,0},{20,4},{24,8},{28,12},{1,17},{... | collective-permute-start | bytes 112136 | tf_op jit(solution)/shard_map/ppermute | solution.py:140
  566.7 14.9 %collective-permute-start.49 = (bf16[1,192,1152]{2,1,0:T(8,128)(2,1)S(1)}, bf16[1,192,1152]{2,1,0:T(8,128)(2,1)S(1)}, u32[]{:S(2)}, u32[]{:S(2)}) collective-permute-start(bf16[1,192,1152]{2,1,0:T(8,128)(2,1)S(1)} %get-tuple-element.82), channel_id=1, source_target_pairs={{0,8},{4,12},{8,16},{12,20},{1,9},{5,13},{9,17},{13,21},{2,10},{6,... | collective-permute-start | bytes 1327112 | tf_op jit(solution)/shard_map/ppermute | solution.py:102
  568.7 13.0 %collective-permute-start.50 = (bf16[1,192,1152]{2,1,0:T(8,128)(2,1)S(1)}, bf16[1,192,1152]{2,1,0:T(8,128)(2,1)S(1)}, u32[]{:S(2)}, u32[]{:S(2)}) collective-permute-start(bf16[1,192,1152]{2,1,0:T(8,128)(2,1)S(1)} %get-tuple-element.83), channel_id=1, source_target_pairs={{24,16},{28,20},{16,8},{20,12},{25,17},{29,21},{17,9},{21,13},{26,... | collective-permute-start | bytes 1327112 | tf_op jit(solution)/shard_map/ppermute | solution.py:102
  571.1 22.5 %collective-permute-start.66 = (bf16[5,192,384]{2,1,0:T(8,128)(2,1)S(1)}, bf16[5,192,384]{2,1,0:T(8,128)(2,1)S(1)}, u32[]{:S(2)}, u32[]{:S(2)}) collective-permute-start(bf16[5,192,384]{2,1,0:T(8,128)(2,1)S(1)} %get-tuple-element.90), channel_id=1, source_target_pairs={{0,8},{4,12},{1,9},{5,13},{2,10},{6,14},{3,11},{7,15}} | collective-permute-start | bytes 2211848 | tf_op jit(solution)/shard_map/ppermute | solution.py:102
  572.5 21.0 %collective-permute-start.67 = (bf16[5,192,384]{2,1,0:T(8,128)(2,1)S(1)}, bf16[5,192,384]{2,1,0:T(8,128)(2,1)S(1)}, u32[]{:S(2)}, u32[]{:S(2)}) collective-permute-start(bf16[5,192,384]{2,1,0:T(8,128)(2,1)S(1)} %get-tuple-element.91), channel_id=1, source_target_pairs={{24,16},{28,20},{25,17},{29,21},{26,18},{30,22},{27,19},{31,23}} | collective-permute-start | bytes 2211848 | tf_op jit(solution)/shard_map/ppermute | solution.py:102
  593.7 21.2 %collective-permute-start.68 = (bf16[5,192,384]{2,1,0:T(8,128)(2,1)S(1)}, bf16[5,192,384]{2,1,0:T(8,128)(2,1)S(1)}, u32[]{:S(2)}, u32[]{:S(2)}) collective-permute-start(bf16[5,192,384]{2,1,0:T(8,128)(2,1)S(1)} %get-tuple-element.94), channel_id=1, source_target_pairs={{0,8},{4,12},{8,16},{12,20},{1,9},{5,13},{9,17},{13,21},{2,10},{6,... | collective-permute-start | bytes 2211848 | tf_op jit(solution)/shard_map/ppermute | solution.py:102
  597.3 21.3 %collective-permute-start.69 = (bf16[5,192,384]{2,1,0:T(8,128)(2,1)S(1)}, bf16[5,192,384]{2,1,0:T(8,128)(2,1)S(1)}, u32[]{:S(2)}, u32[]{:S(2)}) collective-permute-start(bf16[5,192,384]{2,1,0:T(8,128)(2,1)S(1)} %get-tuple-element.95), channel_id=1, source_target_pairs={{24,16},{28,20},{16,8},{20,12},{25,17},{29,21},{17,9},{21,13},{26,... | collective-permute-start | bytes 2211848 | tf_op jit(solution)/shard_map/ppermute | solution.py:102
  598.7 29.3 %collective-permute-start.52 = (bf16[1,192,1152]{2,1,0:T(8,128)(2,1)S(1)}, bf16[1,192,1152]{2,1,0:T(8,128)(2,1)S(1)}, u32[]{:S(2)}, u32[]{:S(2)}) collective-permute-start(bf16[1,192,1152]{2,1,0:T(8,128)(2,1)S(1)} %get-tuple-element.87), channel_id=1, source_target_pairs={{24,16},{28,20},{16,8},{20,12},{8,0},{12,4},{25,17},{29,21},{17,9}... | collective-permute-start | bytes 1327112 | tf_op jit(solution)/shard_map/ppermute | solution.py:102
  600.6 27.4 %collective-permute-start.51 = (bf16[1,192,1152]{2,1,0:T(8,128)(2,1)S(1)}, bf16[1,192,1152]{2,1,0:T(8,128)(2,1)S(1)}, u32[]{:S(2)}, u32[]{:S(2)}) collective-permute-start(bf16[1,192,1152]{2,1,0:T(8,128)(2,1)S(1)} %get-tuple-element.86), channel_id=1, source_target_pairs={{0,8},{4,12},{8,16},{12,20},{16,24},{20,28},{1,9},{5,13},{9,17},{1... | collective-permute-start | bytes 1327112 | tf_op jit(solution)/shard_map/ppermute | solution.py:102
  618.7 20.5 %collective-permute-start.71 = (bf16[5,192,384]{2,1,0:T(8,128)(2,1)S(1)}, bf16[5,192,384]{2,1,0:T(8,128)(2,1)S(1)}, u32[]{:S(2)}, u32[]{:S(2)}) collective-permute-start(bf16[5,192,384]{2,1,0:T(8,128)(2,1)S(1)} %get-tuple-element.99), channel_id=1, source_target_pairs={{24,16},{28,20},{16,8},{20,12},{8,0},{12,4},{25,17},{29,21},{17,9}... | collective-permute-start | bytes 2211848 | tf_op jit(solution)/shard_map/ppermute | solution.py:102
  620.6 18.6 %collective-permute-start.70 = (bf16[5,192,384]{2,1,0:T(8,128)(2,1)S(1)}, bf16[5,192,384]{2,1,0:T(8,128)(2,1)S(1)}, u32[]{:S(2)}, u32[]{:S(2)}) collective-permute-start(bf16[5,192,384]{2,1,0:T(8,128)(2,1)S(1)} %get-tuple-element.98), channel_id=1, source_target_pairs={{0,8},{4,12},{8,16},{12,20},{16,24},{20,28},{1,9},{5,13},{9,17},{1... | collective-permute-start | bytes 2211848 | tf_op jit(solution)/shard_map/ppermute | solution.py:102
  (131 other events, 1218.8 us)

commit v4 on v3

--- a/solution.py
+++ b/solution.py
@@ -68,14 +68,17 @@
     return [blocks[0]] + [exchange(blocks[flip], flip) for flip in (1, 2, 3)]
 
 
-def scatter_product(far_pair, near_pair, own_rows):
+def scatter_product(far_pair, near_pair, own_rows, held_by=None):
     far_part = far_pair().astype(jnp.bfloat16)
     mine, other = far_part[:own_rows], far_part[own_rows:]
     both_mine = mine + exchange(other, 1)
     over_link = exchange(both_mine, 2)
     near_part = near_pair()
     near_other = exchange(near_part[own_rows:].astype(jnp.bfloat16), 1)
-    return near_part[:own_rows] + near_other + over_link
+    total = near_part[:own_rows] + near_other + over_link
+    if held_by is None:
+        return total
+    return total + jnp.minimum(jnp.abs(held_by.astype(jnp.float32)), 0.0)
 
 
 def swap_y(values):
@@ -415,14 +418,14 @@
 
     one_grads = gather_relative(grad_one.astype(low))
     grad_one_rows = jnp.concatenate(one_grads)
-    arrived = one_grads[3]
+    grad_mixed_one = contract_cols(grad_one_rows, w_o).astype(low)
+    qkv_grads = self_backward(qkv, grad_mixed_one, own_id, own_rows)
     branch_three = scatter_product(
-        lambda: product(after(act_parts[1], arrived), w_out),
+        lambda: product(act_parts[1], w_out),
         lambda: product(act_parts[0], w_out),
         own_rows,
-    )
-    grad_mixed_one = contract_cols(grad_one_rows, w_o).astype(low)
-    qkv_grads = self_backward(qkv, grad_mixed_one, own_id, own_rows)
+        qkv_grads[0][0, 0],
+    )
     grad_qkv = jnp.concatenate(qkv_grads, axis=1)
     grad_normed_one = scatter_product(
         lambda: contract_cols(grad_qkv[2 * own_rows :], w_qkv),
@@ -450,9 +453,9 @@
     ).astype(jnp.float32)
     grad_text = scatter_relative(*columns(grad_text)).astype(low)
     grad_tk, grad_tv = grad_text[:text_len], grad_text[text_len:]
-    c_o_grad, w_o_grad, c_q_grad, c_k_grad, c_v_grad = sum_clips(
+    c_o_grad = sum_clips([contract_rows(grad_two_rows, crossed_rows)])[0]
+    w_o_grad, c_q_grad, c_k_grad, c_v_grad = sum_clips(
         [
-            contract_rows(grad_two_rows, crossed_rows),
             contract_rows(grad_one_rows, attended),
             contract_rows(rows_two, grad_cq_rows),
             contract_rows(text_rows, grad_tk),

time: 650 us -> 672 us (1.034)
  starting transfers between devices: 89.5 us -> 106 us
  waiting for transfers between devices: 284 us -> 270 us
  matrix products: 129 us -> 141 us
    ppermute x53, waiting for transfers between devices: 114 us -> 91.8 us  [exchange(): return lax.ppermute(values, 'tensor', [(i, i ^ flip) for i in range(4)])]
    ppermute x6 -> x7, waiting for transfers between devices: 82.1 us -> 103 us  [swap_y(): return lax.ppermute(values, 'dp', [(i, i ^ 1) for i in range(8)])]
    ppermute x24 -> x30, starting transfers between devices: 51.2 us -> 66.9 us  [sum_line(): carried.append(lax.ppermute(block, 'dp', pairs))]
    ppermute x24 -> x30, waiting for transfers between devices: 79.3 us -> 66.3 us  [sum_line(): carried.append(lax.ppermute(block, 'dp', pairs))]
    dot_general x11, matrix products: 41.5 us -> 53.6 us  [product(): return jnp.dot(left_mat, right_mat, preferred_element_type=jnp.float32)]
    unnamed x240 -> x230, local copies, waits for them, and re-layouts: 20.6 us -> 19.7 us
  transfers between devices with their start and end apart: 86 -> 93, of which waited for: 28 -> 30; matrix products, arithmetic and copies ran while one was open for 31% -> 32% of each run, Pallas kernels for 7% -> 6%
where the time goes in v4:
time: 672 us; the launch traced here: 663 us
  waiting for transfers between devices  270 us (40%)
  matrix products  141 us (21%)
  starting transfers between devices  106 us (16%)
  other arithmetic  52.4 us (8%)
  local copies, waits for them, and re-layouts  47.5 us (7%)
  Pallas kernels  42.2 us (6%)
    ppermute x7, waiting for transfers between devices, swap_y(): return lax.ppermute(values, 'dp', [(i, i ^ 1) for i in range(8)])  103 us
    ppermute x53, waiting for transfers between devices, exchange(): return lax.ppermute(values, 'tensor', [(i, i ^ flip) for i in range(4)])  91.8 us
    ppermute x30, starting transfers between devices, sum_line(): carried.append(lax.ppermute(block, 'dp', pairs))  66.9 us
    ppermute x30, waiting for transfers between devices, sum_line(): carried.append(lax.ppermute(block, 'dp', pairs))  66.3 us
    dot_general x11, matrix products, product(): return jnp.dot(left_mat, right_mat, preferred_element_type=jnp.float32)  53.6 us
    dot_general x10, matrix products, contract_rows(): lax.dot_general(left_mat, right_mat, (((0,), (0,)), ((), ())), preferred_...  44.7 us
    dot_general x11, matrix products, contract_cols(): lax.dot_general(left_mat, right_mat, (((1,), (1,)), ((), ())), preferred_...  35 us
    ppermute x53, starting transfers between devices, exchange(): return lax.ppermute(values, 'tensor', [(i, i ^ flip) for i in range(4)])  29.3 us
  transfers between devices with their start and end apart: 93, of which 30 were waited for; matrix products, arithmetic and copies ran while one was open for 32% of the time, Pallas kernels for 6%

profile of v4, /device:TPU:8, one launch (start us, length us, event | category | flops | bytes accessed | tf_op | source)
XLA Modules:
  0.0 663.1 jit_solution(12578287869254188630)
XLA Ops:
  4.3 2.4 fusion.47
  15.1 11.2 %collective-permute-done.1 = bf16[256,1536]{1,0:T(8,128)(2,1)} collective-permute-done((bf16[256,1536]{1,0:T(8,128)(2,1)}, bf16[256,1536]{1,0:T(8,128)(2,1)}, u32[]{:S(2)}, u32[]{:S(2)}) %collective-permute-start.1) | collective-permute-done | bytes 786464 | tf_op jit(solution)/shard_map/ppermute | solution.py:41
  29.5 2.4 constant_dynamic-update-slice_fusion.11
  39.8 5.5 collective-permute-done.10
  46.8 10.4 %collective-permute-done.14 = bf16[192,1536]{1,0:T(8,128)(2,1)} collective-permute-done((bf16[192,1536]{1,0:T(8,128)(2,1)S(1)}, bf16[192,1536]{1,0:T(8,128)(2,1)}, u32[]{:S(2)}, u32[]{:S(2)}) %collective-permute-start.14) | collective-permute-done | bytes 589856 | tf_op jit(solution)/shard_map/ppermute | solution.py:41
  58.7 8.7 %convolution_convert_fusion.1.q_ref.k_ref.v_ref = bf16[1024,1152]{1,0:T(8,128)(2,1)} fusion(bf16[1536,1152]{1,0:T(8,128)(2,1)} %copy-done.57, bf16[256,1536]{1,0:T(8,128)(2,1)} %collective-permute-done.2, bf16[256,1536]{1,0:T(8,128)(2,1)} %collective-permute-done.1, bf16[256,1536]{1,0:T(8,128)(2,1)} %collective-permute-done, bf16[256,1536]{1,0:T(8,128)(2,1)} %fusion.47), kind=kOutput, calls=%fused_computation.7 | convolution fusion | flops 3637641216 | bytes 9043968 | tf_op jit(solution)/shard_map/dot_general | solution.py:25
  67.3 15.3 %self_forward.1 = bf16[1024,384]{1,0:T(8,128)(2,1)} custom-call(s32[1]{0:T(128)} %bitcast.id_ref, bf16[1024,1152]{1,0:T(8,128)(2,1)} %convolution_convert_fusion.1.q_ref.k_ref.v_ref, bf16[1024,1152]{1,0:T(8,128)(2,1)} %convolution_convert_fusion.1.q_ref.k_ref.v_ref, bf16[1024,1152]{1,0:T(8,128)(2,1)} %convolution_convert_fusion.1.q_ref.k_ref.v_ref), custom_call_target="tpu_custom_call" | custom-call | flops 1006632960 | bytes 3145728 | tf_op jit(solution)/shard_map/self_forward/pallas_call | solution.py:238
  88.1 2.6 constant_dynamic-update-slice_fusion.10
  97.2 15.4 %collective-permute-done.5 = bf16[256,1536]{1,0:T(8,128)(2,1)S(1)} collective-permute-done((bf16[256,1536]{1,0:T(8,128)(2,1)S(1)}, bf16[256,1536]{1,0:T(8,128)(2,1)S(1)}, u32[]{:S(2)}, u32[]{:S(2)}) %collective-permute-start.5) | collective-permute-done | bytes 786464 | tf_op jit(solution)/shard_map/ppermute | solution.py:41
  117.5 3.3 convolution_convert_fusion.10
  121.1 2.6 fusion.145
  125.4 2.8 constant_dynamic-update-slice_fusion.7
  128.1 4.6 fusion.138
  137.5 11.4 %multiply_convert_fusion.1 = (bf16[512,1536]{1,0:T(8,128)(2,1)S(1)}, f32[512,1536]{1,0:T(8,128)S(1)}, f32[512,1536]{1,0:T(8,128)S(1)}) fusion(bf16[1536,1536]{1,0:T(8,128)(2,1)} %param.35, bf16[256,1536]{1,0:T(8,128)(2,1)} %collective-permute-done.17, bf16[256,1536]{1,0:T(8,128)(2,1)} %add_convert_fusion.6), kind=kOutput, calls=%fused_computation.43 | convolution fusion | flops 2470182912 | bytes 14155776 | tf_op jit(solution)/shard_map/dot_general | solution.py:25
  149.0 3.4 add_convert_fusion.3
  152.4 4.5 fusion.147
  157.3 2.6 fusion.146
  161.0 10.7 %collective-permute-done.19 = bf16[256,1536]{1,0:T(8,128)(2,1)S(1)} collective-permute-done((bf16[256,1536]{1,0:T(8,128)(2,1)}, bf16[256,1536]{1,0:T(8,128)(2,1)S(1)}, u32[]{:S(2)}, u32[]{:S(2)}) %collective-permute-start.19) | collective-permute-done | bytes 786464 | tf_op jit(solution)/shard_map/ppermute | solution.py:41
  172.4 6.8 %fusion.65 = f32[1536,1536]{1,0:T(8,128)} fusion(bf16[512,1536]{1,0:T(8,128)(2,1)S(1)} %add_convert_fusion.3, bf16[256,1536]{1,0:T(8,128)(2,1)} %collective-permute-done.17, bf16[256,1536]{1,0:T(8,128)(2,1)} %add_convert_fusion.6), kind=kOutput, calls=%fused_computation.159 | convolution fusion | flops 2419064832 | bytes 12582912 | tf_op jit(solution)/shard_map/dot_general | solution.py:29
  180.1 5.1 fusion.148
  185.3 11.3 %multiply_convert_fusion = (bf16[512,1536]{1,0:T(8,128)(2,1)S(1)}, f32[512,1536]{1,0:T(8,128)S(1)}, f32[512,1536]{1,0:T(8,128)}) fusion(bf16[512,1536]{1,0:T(8,128)(2,1)S(1)} %constant_dynamic-update-slice_fusion.12, bf16[1536,1536]{1,0:T(8,128)(2,1)S(1)} %bitcast.266), kind=kOutput, calls=%fused_computation.30 | convolution fusion | flops 2467037184 | bytes 14155776 | tf_op jit(solution)/shard_map/dot_general | solution.py:25
  196.6 7.5 %add_convert_fusion.2 = bf16[512,1536]{1,0:T(8,128)(2,1)S(1)} fusion(f32[512,1536]{1,0:T(8,128)S(1)} %get-tuple-element.155, f32[512,1536]{1,0:T(8,128)} %get-tuple-element.241, bf16[512,1536]{1,0:T(8,128)(2,1)S(1)} %constant_dynamic-update-slice_fusion.16, bf16[1536,1536]{1,0:T(8,128)(2,1)} %param.36), kind=kOutput, calls=%fused_computation.28 | convolution fusion | flops 2426929152 | bytes 14155776 | tf_op jit(solution)/shard_map/dot_general | solution.py:35
  204.2 2.6 convolution_convert_fusion.3
  207.0 5.0 convolution_convert_fusion.4
  212.5 5.3 add_convert_fusion.1
  220.4 7.3 %add_convert_fusion = bf16[1536,1536]{1,0:T(8,128)(2,1)S(1)} fusion(f32[1536,1536]{1,0:T(8,128)} %fusion.148, bf16[512,1536]{1,0:T(8,128)(2,1)} %copy-done.55, bf16[512,1536]{1,0:T(8,128)(2,1)} %copy-done.97), kind=kOutput, calls=%fused_computation.1 | convolution fusion | flops 2420637696 | bytes 17301504 | tf_op jit(solution)/shard_map/dot_general | solution.py:29
  233.7 17.6 %collective-permute-done.54 = bf16[256,1536]{1,0:T(8,128)(2,1)} collective-permute-done((bf16[256,1536]{1,0:T(8,128)(2,1)}, bf16[256,1536]{1,0:T(8,128)(2,1)}, u32[]{:S(2)}, u32[]{:S(2)}) %collective-permute-start.54) | collective-permute-done | bytes 786464 | tf_op jit(solution)/shard_map/ppermute | solution.py:41
  253.5 13.7 %collective-permute-done.28 = bf16[256,1536]{1,0:T(8,128)(2,1)S(1)} collective-permute-done((bf16[256,1536]{1,0:T(8,128)(2,1)S(1)}, bf16[256,1536]{1,0:T(8,128)(2,1)S(1)}, u32[]{:S(2)}, u32[]{:S(2)}) %collective-permute-start.28) | collective-permute-done | bytes 786464 | tf_op jit(solution)/shard_map/ppermute | solution.py:41
  271.5 3.4 convolution_convert_fusion.9
  283.8 3.5 multiply_reduce_fusion.3
  292.5 3.5 collective-permute-start.81
  300.9 4.9 fusion.32
  314.7 2.4 copy.57
  319.3 3.3 dynamic-slice_bitcast_fusion.13
  326.3 19.6 %collective-permute-done.86 = bf16[1,4,192,1536]{3,2,1,0:T(8,128)(2,1)} collective-permute-done((bf16[1,4,192,1536]{3,2,1,0:T(8,128)(2,1)}, bf16[1,4,192,1536]{3,2,1,0:T(8,128)(2,1)}, u32[]{:S(2)}, u32[]{:S(2)}) %collective-permute-start.86) | collective-permute-done | bytes 2359328 | tf_op jit(solution)/shard_map/ppermute | solution.py:85
  345.9 2.6 bitcast_add_fusion
  351.0 3.4 bitcast_add_fusion.3
  354.4 11.1 %collective-permute-done.87 = bf16[1,192,1536]{2,1,0:T(8,128)(2,1)S(1)} collective-permute-done((bf16[1,192,1536]{2,1,0:T(8,128)(2,1)S(1)}, bf16[1,192,1536]{2,1,0:T(8,128)(2,1)S(1)}, u32[]{:S(2)}, u32[]{:S(2)}) %collective-permute-start.87) | collective-permute-done | bytes 589856 | tf_op jit(solution)/shard_map/ppermute | solution.py:105
  369.5 4.5 convolution_convert_fusion.11.grad_ref
  374.0 26.9 %self_backward.1 = (bf16[1024,384]{1,0:T(8,128)(2,1)}, bf16[1024,384]{1,0:T(8,128)(2,1)}, bf16[1024,384]{1,0:T(8,128)(2,1)}) custom-call(s32[1]{0:T(128)} %bitcast.id_ref, bf16[1024,1152]{1,0:T(8,128)(2,1)} %convolution_convert_fusion.1.q_ref.k_ref.v_ref, bf16[1024,1152]{1,0:T(8,128)(2,1)} %convolution_convert_fusion.1.q_ref.k_ref.v_ref, ...), custom_call_target="tpu_custom_call" | custom-call | flops 2516582400 | bytes 5505024 | tf_op jit(solution)/shard_map/self_backward/pallas_call | solution.py:258
  406.4 6.3 convolution_convert_fusion
  420.9 3.9 collective-permute-start.83
  424.8 3.3 collective-permute-start.89
  428.2 3.8 fusion.29
  440.0 9.7 %collective-permute-done.84 = bf16[2,192,1536]{2,1,0:T(8,128)(2,1)S(1)} collective-permute-done((bf16[2,192,1536]{2,1,0:T(8,128)(2,1)S(1)}, bf16[2,192,1536]{2,1,0:T(8,128)(2,1)S(1)}, u32[]{:S(2)}, u32[]{:S(2)}) %collective-permute-start.84) | collective-permute-done | bytes 1179680 | tf_op jit(solution)/shard_map/ppermute | solution.py:105
  453.3 9.4 %collective-permute-done.72 = bf16[1,4,192,384]{3,2,1,0:T(8,128)(2,1)S(1)} collective-permute-done((bf16[1,4,192,384]{3,2,1,0:T(8,128)(2,1)S(1)}, bf16[1,4,192,384]{3,2,1,0:T(8,128)(2,1)S(1)}, u32[]{:S(2)}, u32[]{:S(2)}) %collective-permute-start.72) | collective-permute-done | bytes 589856 | tf_op jit(solution)/shard_map/ppermute | solution.py:85
  466.0 4.1 collective-permute-done.73
  471.7 4.5 collective-permute-start.75
  479.4 4.0 collective-permute-done.76
  485.7 4.9 collective-permute-start.91
  492.9 2.6 constant_dynamic-update-slice_fusion.22
  495.5 74.1 %collective-permute-done.85 = bf16[1,1,192,1536]{3,2,1,0:T(8,128)(2,1)S(1)} collective-permute-done((bf16[1,1,192,1536]{3,2,1,0:T(8,128)(2,1)S(1)}, bf16[1,1,192,1536]{3,2,1,0:T(8,128)(2,1)S(1)}, u32[]{:S(2)}, u32[]{:S(2)}) %collective-permute-start.85) | collective-permute-done | bytes 589856 | tf_op jit(solution)/shard_map/ppermute | solution.py:85
  570.8 4.5 collective-permute-start.78
  588.2 9.3 %collective-permute-done.44 = f32[9344]{0:T(1024)S(1)} collective-permute-done((f32[9344]{0:T(1024)S(1)}, f32[9344]{0:T(1024)S(1)}, u32[]{:S(2)}, u32[]{:S(2)}) %collective-permute-start.44) | collective-permute-done | bytes 37408 | tf_op jit(solution)/shard_map/ppermute | solution.py:143
  598.2 3.0 collective-permute-start.49
  607.7 5.4 collective-permute-done.49
  613.1 9.5 %collective-permute-done.60 = bf16[4,192,384]{2,1,0:T(8,128)(2,1)S(1)} collective-permute-done((bf16[4,192,384]{2,1,0:T(8,128)(2,1)S(1)}, bf16[4,192,384]{2,1,0:T(8,128)(2,1)S(1)}, u32[]{:S(2)}, u32[]{:S(2)}) %collective-permute-start.60) | collective-permute-done | bytes 589856 | tf_op jit(solution)/shard_map/ppermute | solution.py:105
  622.8 3.4 collective-permute-start.62
  629.6 4.6 collective-permute-start.51
  634.7 6.2 collective-permute-done.62
  640.9 3.4 collective-permute-done.63
  646.4 3.9 collective-permute-start.64
  650.4 3.4 collective-permute-done.52
  654.9 6.5 collective-permute-done.65
  (513 shorter events, 174.5 us)
Async XLA Ops:
  6.7 19.6 %collective-permute-start.1 = (bf16[256,1536]{1,0:T(8,128)(2,1)}, bf16[256,1536]{1,0:T(8,128)(2,1)}, u32[]{:S(2)}, u32[]{:S(2)}) collective-permute-start(bf16[256,1536]{1,0:T(8,128)(2,1)} %fusion.47), channel_id=1, source_target_pairs={{0,2},{1,3},{2,0},{3,1},{4,6},{5,7},{6,4},{7,5},{8,10},{9,11},{10,... | collective-permute-start | bytes 2359304 | tf_op jit(solution)/shard_map/ppermute | solution.py:41
  8.2 31.2 %collective-permute-start = (bf16[256,1536]{1,0:T(8,128)(2,1)}, bf16[256,1536]{1,0:T(8,128)(2,1)}, u32[]{:S(2)}, u32[]{:S(2)}) collective-permute-start(bf16[256,1536]{1,0:T(8,128)(2,1)} %fusion.47), channel_id=1, source_target_pairs={{0,1},{1,0},{2,3},{3,2},{4,5},{5,4},{6,7},{7,6},{8,9},{9,8},{10,11... | collective-permute-start | bytes 2359304 | tf_op jit(solution)/shard_map/ppermute | solution.py:41
  28.9 16.4 %collective-permute-start.10 = (bf16[768,384]{1,0:T(8,128)(2,1)S(1)}, bf16[768,384]{1,0:T(8,128)(2,1)}, u32[]{:S(2)}, u32[]{:S(2)}) collective-permute-start(bf16[768,384]{1,0:T(8,128)(2,1)S(1)} %constant_dynamic-slice_fusion.3), channel_id=1, source_target_pairs={{0,2},{1,3},{2,0},{3,1},{4,6},{5,7},{6,4},{7,5},{8,10},{9,11},{10,... | collective-permute-start | bytes 1769480 | tf_op jit(solution)/shard_map/ppermute | solution.py:41
  33.0 24.2 %collective-permute-start.14 = (bf16[192,1536]{1,0:T(8,128)(2,1)S(1)}, bf16[192,1536]{1,0:T(8,128)(2,1)}, u32[]{:S(2)}, u32[]{:S(2)}) collective-permute-start(bf16[192,1536]{1,0:T(8,128)(2,1)S(1)} %constant_dynamic-slice_fusion.2), channel_id=1, source_target_pairs={{0,2},{1,3},{2,0},{3,1},{4,6},{5,7},{6,4},{7,5},{8,10},{9,11},{10,... | collective-permute-start | bytes 1769480 | tf_op jit(solution)/shard_map/ppermute | solution.py:41
  34.6 24.1 %collective-permute-start.2 = (bf16[256,1536]{1,0:T(8,128)(2,1)}, bf16[256,1536]{1,0:T(8,128)(2,1)}, u32[]{:S(2)}, u32[]{:S(2)}) collective-permute-start(bf16[256,1536]{1,0:T(8,128)(2,1)} %collective-permute-done.1), channel_id=1, source_target_pairs={{0,1},{1,0},{2,3},{3,2},{4,5},{5,4},{6,7},{7,6},{8,9},{9,8},{10,11... | collective-permute-start | bytes 2359304 | tf_op jit(solution)/shard_map/ppermute | solution.py:41
  37.3 79.2 %collective-permute-start.9 = (bf16[1536,384]{1,0:T(8,128)(2,1)}, bf16[1536,384]{1,0:T(8,128)(2,1)}, u32[]{:S(2)}, u32[]{:S(2)}) collective-permute-start(bf16[1536,384]{1,0:T(8,128)(2,1)} %param.29), channel_id=1, source_target_pairs={{0,1},{1,0},{2,3},{3,2},{4,5},{5,4},{6,7},{7,6},{8,9},{9,8},{10,11... | collective-permute-start | bytes 3538952 | tf_op jit(solution)/shard_map/ppermute | solution.py:41
  39.4 48.6 %collective-permute-start.13 = (bf16[384,1536]{1,0:T(8,128)(2,1)}, bf16[384,1536]{1,0:T(8,128)(2,1)}, u32[]{:S(2)}, u32[]{:S(2)}) collective-permute-start(bf16[384,1536]{1,0:T(8,128)(2,1)} %param.32), channel_id=1, source_target_pairs={{0,1},{1,0},{2,3},{3,2},{4,5},{5,4},{6,7},{7,6},{8,9},{9,8},{10,11... | collective-permute-start | bytes 3538952 | tf_op jit(solution)/shard_map/ppermute | solution.py:41
  45.3 40.7 %collective-permute-start.11 = (bf16[768,384]{1,0:T(8,128)(2,1)}, bf16[768,384]{1,0:T(8,128)(2,1)}, u32[]{:S(2)}, u32[]{:S(2)}) collective-permute-start(bf16[768,384]{1,0:T(8,128)(2,1)} %collective-permute-done.10), channel_id=1, source_target_pairs={{0,4},{4,0},{8,12},{12,8},{16,20},{20,16},{24,28},{28,24},{1,5},{5... | collective-permute-start | bytes 1769480 | tf_op jit(solution)/shard_map/ppermute | solution.py:85
  57.2 33.5 %collective-permute-start.15 = (bf16[192,1536]{1,0:T(8,128)(2,1)}, bf16[192,1536]{1,0:T(8,128)(2,1)}, u32[]{:S(2)}, u32[]{:S(2)}) collective-permute-start(bf16[192,1536]{1,0:T(8,128)(2,1)} %collective-permute-done.14), channel_id=1, source_target_pairs={{0,4},{4,0},{8,12},{12,8},{16,20},{20,16},{24,28},{28,24},{1,5},{5... | collective-permute-start | bytes 1769480 | tf_op jit(solution)/shard_map/ppermute | solution.py:85
  88.0 28.4 %collective-permute-start.12 = (bf16[1536,384]{1,0:T(8,128)(2,1)S(1)}, bf16[1536,384]{1,0:T(8,128)(2,1)S(1)}, u32[]{:S(2)}, u32[]{:S(2)}) collective-permute-start(bf16[1536,384]{1,0:T(8,128)(2,1)S(1)} %pad_maximum_fusion.5), channel_id=1, source_target_pairs={{0,1},{1,0},{2,3},{3,2},{4,5},{5,4},{6,7},{7,6},{8,9},{9,8},{10,11... | collective-permute-start | bytes 3538952 | tf_op jit(solution)/shard_map/ppermute | solution.py:41
  92.8 19.8 %collective-permute-start.5 = (bf16[256,1536]{1,0:T(8,128)(2,1)S(1)}, bf16[256,1536]{1,0:T(8,128)(2,1)S(1)}, u32[]{:S(2)}, u32[]{:S(2)}) collective-permute-start(bf16[256,1536]{1,0:T(8,128)(2,1)S(1)} %slice_add_fusion.7), channel_id=1, source_target_pairs={{0,2},{1,3},{2,0},{3,1},{4,6},{5,7},{6,4},{7,5},{8,10},{9,11},{10,... | collective-permute-start | bytes 2359304 | tf_op jit(solution)/shard_map/ppermute | solution.py:41
  97.2 28.2 %collective-permute-start.16 = (bf16[384,1536]{1,0:T(8,128)(2,1)}, bf16[384,1536]{1,0:T(8,128)(2,1)}, u32[]{:S(2)}, u32[]{:S(2)}) collective-permute-start(bf16[384,1536]{1,0:T(8,128)(2,1)} %pad_maximum_fusion.6), channel_id=1, source_target_pairs={{0,1},{1,0},{2,3},{3,2},{4,5},{5,4},{6,7},{7,6},{8,9},{9,8},{10,11... | collective-permute-start | bytes 3538952 | tf_op jit(solution)/shard_map/ppermute | solution.py:41
  134.9 36.9 %collective-permute-start.25 = (bf16[256,1536]{1,0:T(8,128)(2,1)S(1)}, bf16[256,1536]{1,0:T(8,128)(2,1)S(1)}, u32[]{:S(2)}, u32[]{:S(2)}) collective-permute-start(bf16[256,1536]{1,0:T(8,128)(2,1)S(1)} %copy-done.14), channel_id=1, source_target_pairs={{0,2},{1,3},{2,0},{3,1},{4,6},{5,7},{6,4},{7,5},{8,10},{9,11},{10,... | collective-permute-start | bytes 2359304 | tf_op jit(solution)/shard_map/ppermute | solution.py:41
  136.4 35.3 %collective-permute-start.19 = (bf16[256,1536]{1,0:T(8,128)(2,1)}, bf16[256,1536]{1,0:T(8,128)(2,1)S(1)}, u32[]{:S(2)}, u32[]{:S(2)}) collective-permute-start(bf16[256,1536]{1,0:T(8,128)(2,1)} %add_convert_fusion.6), channel_id=1, source_target_pairs={{0,2},{1,3},{2,0},{3,1},{4,6},{5,7},{6,4},{7,5},{8,10},{9,11},{10,... | collective-permute-start | bytes 2359304 | tf_op jit(solution)/shard_map/ppermute | solution.py:41
  157.0 96.4 %collective-permute-start.24 = (bf16[256,1536]{1,0:T(8,128)(2,1)S(1)}, bf16[256,1536]{1,0:T(8,128)(2,1)S(1)}, u32[]{:S(2)}, u32[]{:S(2)}) collective-permute-start(bf16[256,1536]{1,0:T(8,128)(2,1)S(1)} %slice.293), channel_id=1, source_target_pairs={{0,1},{1,0},{2,3},{3,2},{4,5},{5,4},{6,7},{7,6},{8,9},{9,8},{10,11... | collective-permute-start | bytes 2359304 | tf_op jit(solution)/shard_map/ppermute | solution.py:41
  171.7 13.5 %collective-permute-start.20 = (bf16[256,1536]{1,0:T(8,128)(2,1)S(1)}, bf16[256,1536]{1,0:T(8,128)(2,1)S(1)}, u32[]{:S(2)}, u32[]{:S(2)}) collective-permute-start(bf16[256,1536]{1,0:T(8,128)(2,1)S(1)} %collective-permute-done.19), channel_id=1, source_target_pairs={{0,1},{1,0},{2,3},{3,2},{4,5},{5,4},{6,7},{7,6},{8,9},{9,8},{10,11... | collective-permute-start | bytes 2359304 | tf_op jit(solution)/shard_map/ppermute | solution.py:41
  171.8 24.7 %collective-permute-start.26 = (bf16[256,1536]{1,0:T(8,128)(2,1)S(1)}, bf16[256,1536]{1,0:T(8,128)(2,1)S(1)}, u32[]{:S(2)}, u32[]{:S(2)}) collective-permute-start(bf16[256,1536]{1,0:T(8,128)(2,1)S(1)} %collective-permute-done.25), channel_id=1, source_target_pairs={{0,1},{1,0},{2,3},{3,2},{4,5},{5,4},{6,7},{7,6},{8,9},{9,8},{10,11... | collective-permute-start | bytes 2359304 | tf_op jit(solution)/shard_map/ppermute | solution.py:41
  206.9 23.7 %collective-permute-start.27 = (bf16[256,1536]{1,0:T(8,128)(2,1)S(1)}, bf16[256,1536]{1,0:T(8,128)(2,1)S(1)}, u32[]{:S(2)}, u32[]{:S(2)}) collective-permute-start(bf16[256,1536]{1,0:T(8,128)(2,1)S(1)} %slice.195), channel_id=1, source_target_pairs={{0,1},{1,0},{2,3},{3,2},{4,5},{5,4},{6,7},{7,6},{8,9},{9,8},{10,11... | collective-permute-start | bytes 2359304 | tf_op jit(solution)/shard_map/ppermute | solution.py:41
  212.0 19.9 %collective-permute-start.21 = (bf16[256,1536]{1,0:T(8,128)(2,1)S(1)}, bf16[256,1536]{1,0:T(8,128)(2,1)S(1)}, u32[]{:S(2)}, u32[]{:S(2)}) collective-permute-start(bf16[256,1536]{1,0:T(8,128)(2,1)S(1)} %slice.191), channel_id=1, source_target_pairs={{0,1},{1,0},{2,3},{3,2},{4,5},{5,4},{6,7},{7,6},{8,9},{9,8},{10,11... | collective-permute-start | bytes 2359304 | tf_op jit(solution)/shard_map/ppermute | solution.py:41
  218.0 33.3 %collective-permute-start.79 = (bf16[2,192,1536]{2,1,0:T(8,128)(2,1)S(1)}, bf16[2,192,1536]{2,1,0:T(8,128)(2,1)S(1)}, u32[]{:S(2)}, u32[]{:S(2)}) collective-permute-start(bf16[2,192,1536]{2,1,0:T(8,128)(2,1)S(1)} %get-tuple-element.118), channel_id=1, source_target_pairs={{0,8},{4,12},{1,9},{5,13},{2,10},{6,14},{3,11},{7,15}} | collective-permute-start | bytes 3538952 | tf_op jit(solution)/shard_map/ppermute | solution.py:105
  219.3 32.5 %collective-permute-start.80 = (bf16[2,192,1536]{2,1,0:T(8,128)(2,1)S(1)}, bf16[2,192,1536]{2,1,0:T(8,128)(2,1)S(1)}, u32[]{:S(2)}, u32[]{:S(2)}) collective-permute-start(bf16[2,192,1536]{2,1,0:T(8,128)(2,1)S(1)} %get-tuple-element.119), channel_id=1, source_target_pairs={{24,16},{28,20},{25,17},{29,21},{26,18},{30,22},{27,19},{31,23}} | collective-permute-start | bytes 3538952 | tf_op jit(solution)/shard_map/ppermute | solution.py:105
  230.6 20.7 %collective-permute-start.54 = (bf16[256,1536]{1,0:T(8,128)(2,1)}, bf16[256,1536]{1,0:T(8,128)(2,1)}, u32[]{:S(2)}, u32[]{:S(2)}) collective-permute-start(bf16[256,1536]{1,0:T(8,128)(2,1)} %add_convert_fusion.7), channel_id=1, source_target_pairs={{0,2},{1,3},{2,0},{3,1},{4,6},{5,7},{6,4},{7,5},{8,10},{9,11},{10,... | collective-permute-start | bytes 2359304 | tf_op jit(solution)/shard_map/ppermute | solution.py:41
  231.9 35.3 %collective-permute-start.28 = (bf16[256,1536]{1,0:T(8,128)(2,1)S(1)}, bf16[256,1536]{1,0:T(8,128)(2,1)S(1)}, u32[]{:S(2)}, u32[]{:S(2)}) collective-permute-start(bf16[256,1536]{1,0:T(8,128)(2,1)S(1)} %slice_add_fusion.5), channel_id=1, source_target_pairs={{0,2},{1,3},{2,0},{3,1},{4,6},{5,7},{6,4},{7,5},{8,10},{9,11},{10,... | collective-permute-start | bytes 2359304 | tf_op jit(solution)/shard_map/ppermute | solution.py:41
  251.3 40.6 %collective-permute-start.53 = (bf16[256,1536]{1,0:T(8,128)(2,1)}, bf16[256,1536]{1,0:T(8,128)(2,1)}, u32[]{:S(2)}, u32[]{:S(2)}) collective-permute-start(bf16[256,1536]{1,0:T(8,128)(2,1)} %add_convert_fusion.7), channel_id=1, source_target_pairs={{0,1},{1,0},{2,3},{3,2},{4,5},{5,4},{6,7},{7,6},{8,9},{9,8},{10,11... | collective-permute-start | bytes 2359304 | tf_op jit(solution)/shard_map/ppermute | solution.py:41
  251.3 41.2 %collective-permute-start.55 = (bf16[256,1536]{1,0:T(8,128)(2,1)}, bf16[256,1536]{1,0:T(8,128)(2,1)}, u32[]{:S(2)}, u32[]{:S(2)}) collective-permute-start(bf16[256,1536]{1,0:T(8,128)(2,1)} %collective-permute-done.54), channel_id=1, source_target_pairs={{0,1},{1,0},{2,3},{3,2},{4,5},{5,4},{6,7},{7,6},{8,9},{9,8},{10,11... | collective-permute-start | bytes 2359304 | tf_op jit(solution)/shard_map/ppermute | solution.py:41
  291.9 54.0 %collective-permute-start.86 = (bf16[1,4,192,1536]{3,2,1,0:T(8,128)(2,1)}, bf16[1,4,192,1536]{3,2,1,0:T(8,128)(2,1)}, u32[]{:S(2)}, u32[]{:S(2)}) collective-permute-start(bf16[1,4,192,1536]{3,2,1,0:T(8,128)(2,1)} %dynamic-slice_bitcast_fusion), channel_id=1, source_target_pairs={{0,4},{4,0},{8,12},{12,8},{16,20},{20,16},{24,28},{28,24},{1,5},{5... | collective-permute-start | bytes 7077896 | tf_op jit(solution)/shard_map/ppermute | solution.py:85
  292.5 32.5 %collective-permute-start.81 = (bf16[2,192,1536]{2,1,0:T(8,128)(2,1)}, bf16[2,192,1536]{2,1,0:T(8,128)(2,1)}, u32[]{:S(2)}, u32[]{:S(2)}) collective-permute-start(bf16[2,192,1536]{2,1,0:T(8,128)(2,1)} %get-tuple-element.122), channel_id=1, source_target_pairs={{0,8},{4,12},{8,16},{12,20},{1,9},{5,13},{9,17},{13,21},{2,10},{6,... | collective-permute-start | bytes 3538952 | tf_op jit(solution)/shard_map/ppermute | solution.py:105
  296.0 30.3 %collective-permute-start.82 = (bf16[2,192,1536]{2,1,0:T(8,128)(2,1)}, bf16[2,192,1536]{2,1,0:T(8,128)(2,1)}, u32[]{:S(2)}, u32[]{:S(2)}) collective-permute-start(bf16[2,192,1536]{2,1,0:T(8,128)(2,1)} %get-tuple-element.123), channel_id=1, source_target_pairs={{24,16},{28,20},{16,8},{20,12},{25,17},{29,21},{17,9},{21,13},{26,... | collective-permute-start | bytes 3538952 | tf_op jit(solution)/shard_map/ppermute | solution.py:105
  322.6 28.3 %collective-permute-start.30 = (bf16[256,1536]{1,0:T(8,128)(2,1)S(1)}, bf16[256,1536]{1,0:T(8,128)(2,1)S(1)}, u32[]{:S(2)}, u32[]{:S(2)}) collective-permute-start(bf16[256,1536]{1,0:T(8,128)(2,1)S(1)} %copy-done.51), channel_id=1, source_target_pairs={{0,2},{1,3},{2,0},{3,1},{4,6},{5,7},{6,4},{7,5},{8,10},{9,11},{10,... | collective-permute-start | bytes 2359304 | tf_op jit(solution)/shard_map/ppermute | solution.py:41
  323.5 44.4 %collective-permute-start.29 = (bf16[256,1536]{1,0:T(8,128)(2,1)S(1)}, bf16[256,1536]{1,0:T(8,128)(2,1)S(1)}, u32[]{:S(2)}, u32[]{:S(2)}) collective-permute-start(bf16[256,1536]{1,0:T(8,128)(2,1)S(1)} %copy-done.51), channel_id=1, source_target_pairs={{0,1},{1,0},{2,3},{3,2},{4,5},{5,4},{6,7},{7,6},{8,9},{9,8},{10,11... | collective-permute-start | bytes 2359304 | tf_op jit(solution)/shard_map/ppermute | solution.py:41
  324.9 43.6 %collective-permute-start.67 = (bf16[256,1536]{1,0:T(8,128)(2,1)}, bf16[256,1536]{1,0:T(8,128)(2,1)}, u32[]{:S(2)}, u32[]{:S(2)}) collective-permute-start(bf16[256,1536]{1,0:T(8,128)(2,1)} %fusion.67), channel_id=1, source_target_pairs={{0,2},{1,3},{2,0},{3,1},{4,6},{5,7},{6,4},{7,5},{8,10},{9,11},{10,... | collective-permute-start | bytes 2359304 | tf_op jit(solution)/shard_map/ppermute | solution.py:41
  348.6 16.8 %collective-permute-start.87 = (bf16[1,192,1536]{2,1,0:T(8,128)(2,1)S(1)}, bf16[1,192,1536]{2,1,0:T(8,128)(2,1)S(1)}, u32[]{:S(2)}, u32[]{:S(2)}) collective-permute-start(bf16[1,192,1536]{2,1,0:T(8,128)(2,1)S(1)} %get-tuple-element.128), channel_id=1, source_target_pairs={{0,8},{4,12},{1,9},{5,13},{2,10},{6,14},{3,11},{7,15}} | collective-permute-start | bytes 1769480 | tf_op jit(solution)/shard_map/ppermute | solution.py:105
  349.9 15.5 %collective-permute-start.88 = (bf16[1,192,1536]{2,1,0:T(8,128)(2,1)S(1)}, bf16[1,192,1536]{2,1,0:T(8,128)(2,1)S(1)}, u32[]{:S(2)}, u32[]{:S(2)}) collective-permute-start(bf16[1,192,1536]{2,1,0:T(8,128)(2,1)S(1)} %get-tuple-element.129), channel_id=1, source_target_pairs={{24,16},{28,20},{25,17},{29,21},{26,18},{30,22},{27,19},{31,23}} | collective-permute-start | bytes 1769480 | tf_op jit(solution)/shard_map/ppermute | solution.py:105
  350.8 17.7 %collective-permute-start.31 = (bf16[256,1536]{1,0:T(8,128)(2,1)S(1)}, bf16[256,1536]{1,0:T(8,128)(2,1)S(1)}, u32[]{:S(2)}, u32[]{:S(2)}) collective-permute-start(bf16[256,1536]{1,0:T(8,128)(2,1)S(1)} %collective-permute-done.30), channel_id=1, source_target_pairs={{0,1},{1,0},{2,3},{3,2},{4,5},{5,4},{6,7},{7,6},{8,9},{9,8},{10,11... | collective-permute-start | bytes 2359304 | tf_op jit(solution)/shard_map/ppermute | solution.py:41
  365.5 51.8 %collective-permute-start.71 = (bf16[256,384]{0,1:T(8,128)(2,1)}, bf16[256,384]{0,1:T(8,128)(2,1)}, u32[]{:S(2)}, u32[]{:S(2)}) collective-permute-start(bf16[256,384]{0,1:T(8,128)(2,1)} %get-tuple-element.216), channel_id=1, source_target_pairs={{0,3},{1,2},{2,1},{3,0},{4,7},{5,6},{6,5},{7,4},{8,11},{9,10},{10,... | collective-permute-start | bytes 589832 | tf_op jit(solution)/shard_map/ppermute | solution.py:41
  365.5 52.3 %collective-permute-start.70 = (bf16[256,384]{0,1:T(8,128)(2,1)}, bf16[256,384]{0,1:T(8,128)(2,1)}, u32[]{:S(2)}, u32[]{:S(2)}) collective-permute-start(bf16[256,384]{0,1:T(8,128)(2,1)} %get-tuple-element.217), channel_id=1, source_target_pairs={{0,2},{1,3},{2,0},{3,1},{4,6},{5,7},{6,4},{7,5},{8,10},{9,11},{10,... | collective-permute-start | bytes 589832 | tf_op jit(solution)/shard_map/ppermute | solution.py:41
  367.8 51.1 %collective-permute-start.69 = (bf16[256,384]{0,1:T(8,128)(2,1)}, bf16[256,384]{0,1:T(8,128)(2,1)}, u32[]{:S(2)}, u32[]{:S(2)}) collective-permute-start(bf16[256,384]{0,1:T(8,128)(2,1)} %get-tuple-element.218), channel_id=1, source_target_pairs={{0,1},{1,0},{2,3},{3,2},{4,5},{5,4},{6,7},{7,6},{8,9},{9,8},{10,11... | collective-permute-start | bytes 589832 | tf_op jit(solution)/shard_map/ppermute | solution.py:41
  368.5 52.4 %collective-permute-start.66 = (bf16[256,1536]{1,0:T(8,128)(2,1)}, bf16[256,1536]{1,0:T(8,128)(2,1)}, u32[]{:S(2)}, u32[]{:S(2)}) collective-permute-start(bf16[256,1536]{1,0:T(8,128)(2,1)} %fusion.67), channel_id=1, source_target_pairs={{0,1},{1,0},{2,3},{3,2},{4,5},{5,4},{6,7},{7,6},{8,9},{9,8},{10,11... | collective-permute-start | bytes 2359304 | tf_op jit(solution)/shard_map/ppermute | solution.py:41
  368.6 56.2 %collective-permute-start.68 = (bf16[256,1536]{1,0:T(8,128)(2,1)}, bf16[256,1536]{1,0:T(8,128)(2,1)}, u32[]{:S(2)}, u32[]{:S(2)}) collective-permute-start(bf16[256,1536]{1,0:T(8,128)(2,1)} %collective-permute-done.67), channel_id=1, source_target_pairs={{0,1},{1,0},{2,3},{3,2},{4,5},{5,4},{6,7},{7,6},{8,9},{9,8},{10,11... | collective-permute-start | bytes 2359304 | tf_op jit(solution)/shard_map/ppermute | solution.py:41
  417.3 18.7 %collective-permute-start.18 = (bf16[256,1536]{1,0:T(8,128)(2,1)S(1)}, bf16[256,1536]{1,0:T(8,128)(2,1)S(1)}, u32[]{:S(2)}, u32[]{:S(2)}) collective-permute-start(bf16[256,1536]{1,0:T(8,128)(2,1)S(1)} %copy-done.44), channel_id=1, source_target_pairs={{0,1},{1,0},{2,3},{3,2},{4,5},{5,4},{6,7},{7,6},{8,9},{9,8},{10,11... | collective-permute-start | bytes 2359304 | tf_op jit(solution)/shard_map/ppermute | solution.py:41
  417.8 20.2 %collective-permute-start.22 = (bf16[256,1536]{1,0:T(8,128)(2,1)S(1)}, bf16[256,1536]{1,0:T(8,128)(2,1)S(1)}, u32[]{:S(2)}, u32[]{:S(2)}) collective-permute-start(bf16[256,1536]{1,0:T(8,128)(2,1)S(1)} %copy-done.50), channel_id=1, source_target_pairs={{0,2},{1,3},{2,0},{3,1},{4,6},{5,7},{6,4},{7,5},{8,10},{9,11},{10,... | collective-permute-start | bytes 2359304 | tf_op jit(solution)/shard_map/ppermute | solution.py:41
  419.0 30.7 %collective-permute-start.84 = (bf16[2,192,1536]{2,1,0:T(8,128)(2,1)S(1)}, bf16[2,192,1536]{2,1,0:T(8,128)(2,1)S(1)}, u32[]{:S(2)}, u32[]{:S(2)}) collective-permute-start(bf16[2,192,1536]{2,1,0:T(8,128)(2,1)S(1)} %copy-done.43), channel_id=1, source_target_pairs={{24,16},{28,20},{16,8},{20,12},{8,0},{12,4},{25,17},{29,21},{17,9}... | collective-permute-start | bytes 3538952 | tf_op jit(solution)/shard_map/ppermute | solution.py:105
  420.9 30.7 %collective-permute-start.83 = (bf16[2,192,1536]{2,1,0:T(8,128)(2,1)S(1)}, bf16[2,192,1536]{2,1,0:T(8,128)(2,1)S(1)}, u32[]{:S(2)}, u32[]{:S(2)}) collective-permute-start(bf16[2,192,1536]{2,1,0:T(8,128)(2,1)S(1)} %copy-done.42), channel_id=1, source_target_pairs={{0,8},{4,12},{8,16},{12,20},{16,24},{20,28},{1,9},{5,13},{9,17},{1... | collective-permute-start | bytes 3538952 | tf_op jit(solution)/shard_map/ppermute | solution.py:105
  424.8 40.5 %collective-permute-start.89 = (bf16[1,192,1536]{2,1,0:T(8,128)(2,1)S(1)}, bf16[1,192,1536]{2,1,0:T(8,128)(2,1)S(1)}, u32[]{:S(2)}, u32[]{:S(2)}) collective-permute-start(bf16[1,192,1536]{2,1,0:T(8,128)(2,1)S(1)} %copy-done.54), channel_id=1, source_target_pairs={{0,8},{4,12},{8,16},{12,20},{1,9},{5,13},{9,17},{13,21},{2,10},{6,... | collective-permute-start | bytes 1769480 | tf_op jit(solution)/shard_map/ppermute | solution.py:105
  436.5 28.9 %collective-permute-start.90 = (bf16[1,192,1536]{2,1,0:T(8,128)(2,1)S(1)}, bf16[1,192,1536]{2,1,0:T(8,128)(2,1)S(1)}, u32[]{:S(2)}, u32[]{:S(2)}) collective-permute-start(bf16[1,192,1536]{2,1,0:T(8,128)(2,1)S(1)} %copy-done.53), channel_id=1, source_target_pairs={{24,16},{28,20},{16,8},{20,12},{25,17},{29,21},{17,9},{21,13},{26,... | collective-permute-start | bytes 1769480 | tf_op jit(solution)/shard_map/ppermute | solution.py:105
  438.0 32.1 %collective-permute-start.33 = (bf16[256,1536]{1,0:T(8,128)(2,1)S(1)}, bf16[256,1536]{1,0:T(8,128)(2,1)S(1)}, u32[]{:S(2)}, u32[]{:S(2)}) collective-permute-start(bf16[256,1536]{1,0:T(8,128)(2,1)S(1)} %slice.201), channel_id=1, source_target_pairs={{0,1},{1,0},{2,3},{3,2},{4,5},{5,4},{6,7},{7,6},{8,9},{9,8},{10,11... | collective-permute-start | bytes 2359304 | tf_op jit(solution)/shard_map/ppermute | solution.py:41
  465.3 18.5 %collective-permute-start.32 = (bf16[256,1536]{1,0:T(8,128)(2,1)S(1)}, bf16[256,1536]{1,0:T(8,128)(2,1)S(1)}, u32[]{:S(2)}, u32[]{:S(2)}) collective-permute-start(bf16[256,1536]{1,0:T(8,128)(2,1)S(1)} %slice.292), channel_id=1, source_target_pairs={{0,1},{1,0},{2,3},{3,2},{4,5},{5,4},{6,7},{7,6},{8,9},{9,8},{10,11... | collective-permute-start | bytes 2359304 | tf_op jit(solution)/shard_map/ppermute | solution.py:41
  465.4 118.0 %collective-permute-start.46 = (bf16[1,4,192,1152]{3,2,1,0:T(8,128)(2,1)S(1)}, bf16[1,4,192,1152]{3,2,1,0:T(8,128)(2,1)S(1)}, u32[]{:S(2)}, u32[]{:S(2)}) collective-permute-start(bf16[1,4,192,1152]{3,2,1,0:T(8,128)(2,1)S(1)} %dynamic-slice_bitcast_fusion.1), channel_id=1, source_target_pairs={{0,4},{4,0},{8,12},{12,8},{16,20},{20,16},{24,28},{28,24},{1,5},{5... | collective-permute-start | bytes 5308424 | tf_op jit(solution)/shard_map/ppermute | solution.py:85
  470.1 15.6 %collective-permute-start.34 = (bf16[256,1536]{1,0:T(8,128)(2,1)S(1)}, bf16[256,1536]{1,0:T(8,128)(2,1)S(1)}, u32[]{:S(2)}, u32[]{:S(2)}) collective-permute-start(bf16[256,1536]{1,0:T(8,128)(2,1)S(1)} %slice_add_fusion.4), channel_id=1, source_target_pairs={{0,2},{1,3},{2,0},{3,1},{4,6},{5,7},{6,4},{7,5},{8,10},{9,11},{10,... | collective-permute-start | bytes 2359304 | tf_op jit(solution)/shard_map/ppermute | solution.py:41
  478.9 123.6 %collective-permute-start.59 = (bf16[4,4,192,384]{3,2,0,1:T(8,128)(2,1)S(1)}, bf16[4,4,192,384]{3,2,0,1:T(8,128)(2,1)S(1)}, u32[]{:S(2)}, u32[]{:S(2)}) collective-permute-start(bf16[4,4,192,384]{3,2,0,1:T(8,128)(2,1)S(1)} %pad_maximum_fusion.3), channel_id=1, source_target_pairs={{0,4},{4,0},{8,12},{12,8},{16,20},{20,16},{24,28},{28,24},{1,5},{5... | collective-permute-start | bytes 7077896 | tf_op jit(solution)/shard_map/ppermute | solution.py:85
  483.4 86.2 %collective-permute-start.85 = (bf16[1,1,192,1536]{3,2,1,0:T(8,128)(2,1)S(1)}, bf16[1,1,192,1536]{3,2,1,0:T(8,128)(2,1)S(1)}, u32[]{:S(2)}, u32[]{:S(2)}) collective-permute-start(bf16[1,1,192,1536]{3,2,1,0:T(8,128)(2,1)S(1)} %fusion.84), channel_id=1, source_target_pairs={{0,4},{4,0},{8,12},{12,8},{16,20},{20,16},{24,28},{28,24},{1,5},{5... | collective-permute-start | bytes 1769480 | tf_op jit(solution)/shard_map/ppermute | solution.py:85
  483.8 91.6 %collective-permute-start.92 = (bf16[1,192,1536]{2,1,0:T(8,128)(2,1)S(1)}, bf16[1,192,1536]{2,1,0:T(8,128)(2,1)S(1)}, u32[]{:S(2)}, u32[]{:S(2)}) collective-permute-start(bf16[1,192,1536]{2,1,0:T(8,128)(2,1)S(1)} %get-tuple-element.137), channel_id=1, source_target_pairs={{24,16},{28,20},{16,8},{20,12},{8,0},{12,4},{25,17},{29,21},{17,9}... | collective-permute-start | bytes 1769480 | tf_op jit(solution)/shard_map/ppermute | solution.py:105
  485.7 91.6 %collective-permute-start.91 = (bf16[1,192,1536]{2,1,0:T(8,128)(2,1)S(1)}, bf16[1,192,1536]{2,1,0:T(8,128)(2,1)S(1)}, u32[]{:S(2)}, u32[]{:S(2)}) collective-permute-start(bf16[1,192,1536]{2,1,0:T(8,128)(2,1)S(1)} %get-tuple-element.136), channel_id=1, source_target_pairs={{0,8},{4,12},{8,16},{12,20},{16,24},{20,28},{1,9},{5,13},{9,17},{1... | collective-permute-start | bytes 1769480 | tf_op jit(solution)/shard_map/ppermute | solution.py:105
  570.8 14.4 %collective-permute-start.78 = (bf16[1,192,384]{2,1,0:T(8,128)(2,1)S(1)}, bf16[1,192,384]{2,1,0:T(8,128)(2,1)S(1)}, u32[]{:S(2)}, u32[]{:S(2)}) collective-permute-start(bf16[1,192,384]{2,1,0:T(8,128)(2,1)S(1)} %get-tuple-element.117), channel_id=1, source_target_pairs={{24,16},{28,20},{16,8},{20,12},{8,0},{12,4},{25,17},{29,21},{17,9}... | collective-permute-start | bytes 442376 | tf_op jit(solution)/shard_map/ppermute | solution.py:105
  583.7 14.3 %collective-permute-start.47 = (bf16[1,192,1152]{2,1,0:T(8,128)(2,1)S(1)}, bf16[1,192,1152]{2,1,0:T(8,128)(2,1)S(1)}, u32[]{:S(2)}, u32[]{:S(2)}) collective-permute-start(bf16[1,192,1152]{2,1,0:T(8,128)(2,1)S(1)} %get-tuple-element.86), channel_id=1, source_target_pairs={{0,8},{4,12},{1,9},{5,13},{2,10},{6,14},{3,11},{7,15}} | collective-permute-start | bytes 1327112 | tf_op jit(solution)/shard_map/ppermute | solution.py:105
  598.2 14.9 %collective-permute-start.49 = (bf16[1,192,1152]{2,1,0:T(8,128)(2,1)S(1)}, bf16[1,192,1152]{2,1,0:T(8,128)(2,1)S(1)}, u32[]{:S(2)}, u32[]{:S(2)}) collective-permute-start(bf16[1,192,1152]{2,1,0:T(8,128)(2,1)S(1)} %get-tuple-element.90), channel_id=1, source_target_pairs={{0,8},{4,12},{8,16},{12,20},{1,9},{5,13},{9,17},{13,21},{2,10},{6,... | collective-permute-start | bytes 1327112 | tf_op jit(solution)/shard_map/ppermute | solution.py:105
  603.2 19.5 %collective-permute-start.60 = (bf16[4,192,384]{2,1,0:T(8,128)(2,1)S(1)}, bf16[4,192,384]{2,1,0:T(8,128)(2,1)S(1)}, u32[]{:S(2)}, u32[]{:S(2)}) collective-permute-start(bf16[4,192,384]{2,1,0:T(8,128)(2,1)S(1)} %get-tuple-element.97), channel_id=1, source_target_pairs={{0,8},{4,12},{1,9},{5,13},{2,10},{6,14},{3,11},{7,15}} | collective-permute-start | bytes 1769480 | tf_op jit(solution)/shard_map/ppermute | solution.py:105
  604.6 18.0 %collective-permute-start.61 = (bf16[4,192,384]{2,1,0:T(8,128)(2,1)S(1)}, bf16[4,192,384]{2,1,0:T(8,128)(2,1)S(1)}, u32[]{:S(2)}, u32[]{:S(2)}) collective-permute-start(bf16[4,192,384]{2,1,0:T(8,128)(2,1)S(1)} %get-tuple-element.98), channel_id=1, source_target_pairs={{24,16},{28,20},{25,17},{29,21},{26,18},{30,22},{27,19},{31,23}} | collective-permute-start | bytes 1769480 | tf_op jit(solution)/shard_map/ppermute | solution.py:105
  622.8 18.1 %collective-permute-start.62 = (bf16[4,192,384]{2,1,0:T(8,128)(2,1)S(1)}, bf16[4,192,384]{2,1,0:T(8,128)(2,1)S(1)}, u32[]{:S(2)}, u32[]{:S(2)}) collective-permute-start(bf16[4,192,384]{2,1,0:T(8,128)(2,1)S(1)} %get-tuple-element.101), channel_id=1, source_target_pairs={{0,8},{4,12},{8,16},{12,20},{1,9},{5,13},{9,17},{13,21},{2,10},{6,... | collective-permute-start | bytes 1769480 | tf_op jit(solution)/shard_map/ppermute | solution.py:105
  626.2 18.1 %collective-permute-start.63 = (bf16[4,192,384]{2,1,0:T(8,128)(2,1)S(1)}, bf16[4,192,384]{2,1,0:T(8,128)(2,1)S(1)}, u32[]{:S(2)}, u32[]{:S(2)}) collective-permute-start(bf16[4,192,384]{2,1,0:T(8,128)(2,1)S(1)} %get-tuple-element.102), channel_id=1, source_target_pairs={{24,16},{28,20},{16,8},{20,12},{25,17},{29,21},{17,9},{21,13},{26,... | collective-permute-start | bytes 1769480 | tf_op jit(solution)/shard_map/ppermute | solution.py:105
  627.6 26.2 %collective-permute-start.52 = (bf16[1,192,1152]{2,1,0:T(8,128)(2,1)S(1)}, bf16[1,192,1152]{2,1,0:T(8,128)(2,1)S(1)}, u32[]{:S(2)}, u32[]{:S(2)}) collective-permute-start(bf16[1,192,1152]{2,1,0:T(8,128)(2,1)S(1)} %get-tuple-element.95), channel_id=1, source_target_pairs={{24,16},{28,20},{16,8},{20,12},{8,0},{12,4},{25,17},{29,21},{17,9}... | collective-permute-start | bytes 1327112 | tf_op jit(solution)/shard_map/ppermute | solution.py:105
  629.6 24.2 %collective-permute-start.51 = (bf16[1,192,1152]{2,1,0:T(8,128)(2,1)S(1)}, bf16[1,192,1152]{2,1,0:T(8,128)(2,1)S(1)}, u32[]{:S(2)}, u32[]{:S(2)}) collective-permute-start(bf16[1,192,1152]{2,1,0:T(8,128)(2,1)S(1)} %get-tuple-element.94), channel_id=1, source_target_pairs={{0,8},{4,12},{8,16},{12,20},{16,24},{20,28},{1,9},{5,13},{9,17},{1... | collective-permute-start | bytes 1327112 | tf_op jit(solution)/shard_map/ppermute | solution.py:105
  644.5 16.9 %collective-permute-start.65 = (bf16[4,192,384]{2,1,0:T(8,128)(2,1)S(1)}, bf16[4,192,384]{2,1,0:T(8,128)(2,1)S(1)}, u32[]{:S(2)}, u32[]{:S(2)}) collective-permute-start(bf16[4,192,384]{2,1,0:T(8,128)(2,1)S(1)} %get-tuple-element.106), channel_id=1, source_target_pairs={{24,16},{28,20},{16,8},{20,12},{8,0},{12,4},{25,17},{29,21},{17,9}... | collective-permute-start | bytes 1769480 | tf_op jit(solution)/shard_map/ppermute | solution.py:105
  646.4 15.0 %collective-permute-start.64 = (bf16[4,192,384]{2,1,0:T(8,128)(2,1)S(1)}, bf16[4,192,384]{2,1,0:T(8,128)(2,1)S(1)}, u32[]{:S(2)}, u32[]{:S(2)}) collective-permute-start(bf16[4,192,384]{2,1,0:T(8,128)(2,1)S(1)} %get-tuple-element.105), channel_id=1, source_target_pairs={{0,8},{4,12},{8,16},{12,20},{16,24},{20,28},{1,9},{5,13},{9,17},{1... | collective-permute-start | bytes 1769480 | tf_op jit(solution)/shard_map/ppermute | solution.py:105
  (135 other events, 1066.8 us)
